TPU v7x, 512 devices: a whole 4x8x8 slice. The times are simulated.
512 devices in a mesh: wx: 128 (over y, x, z_hi, core), ny: 4 (over z_lo).
Axes of the slice: x: 4, y: 8, z: 8 (z_hi: 2, z_lo: 4; z = z_hi * 4 + z_lo), core: 2. Of those that a mesh axis runs over, the one named last changes fastest.
Arguments:
- displacement: float32 [3, 512, 6, 512], P(None, 'wx', None, 'ny'), may hold values from -0.1 to 0.1
- velocity: float32 [3, 512, 6, 512], P(None, 'wx', None, 'ny'), may hold values from -1 to 1
- labels: int32 [512, 6, 512], P('wx', None, 'ny'), may hold values from 0 to 7
- bond_mask: int32 [61, 512, 6, 512], P(None, 'wx', None, 'ny'), may hold values 0 or 1
- stiffness: float32 [8], replicated, may hold values from 1 to 10
- critical: float32 [8], replicated, may hold values from 0.02 to 0.2
Outputs:
- final_displacement: float32 [3, 512, 6, 512], P(None, 'wx', None, 'ny')
- final_velocity: float32 [3, 512, 6, 512], P(None, 'wx', None, 'ny')
All inputs are finite; a program needn't handle non-finite values. No bound on the sum of `bond_mask` on one device may be relied on, other than what follows from the above.
Results may differ from a plain program's by a relative error of at most 0.00002.
Values sent between devices are 32-bit elements; how exact they have to be, the bound alone decides.
No kernel may reach another device: no remote copies, remote signals or barrier semaphores. Data moves between devices by JAX's collectives and lax.ppermute only.
A program may use at most 64 MiB of HBM per device.

v0:
```python
import math

import jax
import jax.numpy as jnp
from jax import lax
from jax.sharding import PartitionSpec as P

STEPS = 3
MATS = 8


time_step = 0.05


def with_halo(block, sides, width):
    for axis, dim in sides:
        count = lax.axis_size(axis)
        forward = [(i, i + 1) for i in range(count - 1)]
        backward = [(target, source) for source, target in forward]
        low = lax.ppermute(
            lax.slice_in_dim(block, block.shape[dim] - width, None, axis=dim), axis, forward
        )
        high = lax.ppermute(lax.slice_in_dim(block, 0, width, axis=dim), axis, backward)
        block = jnp.concatenate([low, block, high], axis=dim)
    return block


def shifted(value, axis, steps):
    count = lax.axis_size(axis)
    initial, last = (max(0, -steps), min(count, count - steps))
    return lax.ppermute(value, axis, [(source, source + steps) for source in range(initial, last)])


def bond_offsets():
    chosen = []
    for step_x in range(0, 4):
        for step_z in range(-3, 4):
            for step_y in range(-3, 4):
                if step_x * step_x + step_z * step_z + step_y * step_y <= 9:
                    if step_x > 0 or (step_x == 0 and (step_z > 0 or (step_z == 0 and step_y > 0))):
                        chosen.append((step_x, step_z, step_y))
    return chosen


def node_material(labels, stiffness, critical):
    modulus = jnp.zeros(labels.shape, jnp.float32)
    strain_limit = jnp.zeros(labels.shape, jnp.float32)
    for material in range(MATS):
        matches = labels == material
        modulus = jnp.where(matches, stiffness[material], modulus)
        strain_limit = jnp.where(matches, critical[material], strain_limit)
    return (modulus, strain_limit)


def pair_force(
    offset, source, target, modulus_here, modulus_there, limit_here, limit_there, intact
):
    length = math.sqrt(offset[0] * offset[0] + offset[1] * offset[1] + offset[2] * offset[2])
    relative = [
        float(offset[component]) + target[component] - source[component] for component in range(3)
    ]
    distance = jnp.sqrt(
        relative[0] * relative[0] + relative[1] * relative[1] + relative[2] * relative[2]
    )
    stretch = (distance - length) / length
    pair_modulus = 2.0 * modulus_here * modulus_there / (modulus_here + modulus_there)
    pair_limit = 0.5 * (limit_here + limit_there)
    ratio = stretch / pair_limit
    magnitude = intact * pair_modulus * stretch / (1.0 + ratio * ratio) / (length * length)
    return jnp.stack([magnitude * part for part in relative])


def extend(source):
    widened = with_halo(source, (("ny", 3),), 3)
    front_rows = shifted(widened[:, :3], "wx", -1)
    return jnp.concatenate([widened, front_rows], axis=1)


def send_back(spread, rows_x, rows_y):
    returned = shifted(spread[:, rows_x:], "wx", 1)
    central = spread[:, :rows_x].at[:, :3].add(returned)
    lower_rim = shifted(central[:, :, :, :3], "ny", -1)
    upper_rim = shifted(central[:, :, :, rows_y + 3 :], "ny", 1)
    interior = central[:, :, :, 3 : 3 + rows_y]
    interior = interior.at[:, :, :, rows_y - 3 :].add(lower_rim)
    return interior.at[:, :, :, :3].add(upper_rim)


def on_device(displacement, velocity, labels, bond_mask, stiffness, critical):
    rows_x, rows_z, rows_y = labels.shape
    modulus, strain_limit = node_material(labels, stiffness, critical)
    material_ext = extend(jnp.stack([modulus, strain_limit]))
    material_ext = jnp.pad(material_ext, ((0, 0), (0, 0), (3, 3), (0, 0)))
    extent_x = rows_x * lax.axis_size("wx")
    extent_y = rows_y * lax.axis_size("ny")
    global_x = lax.axis_index("wx") * rows_x + jnp.arange(rows_x, dtype=jnp.int32).reshape(
        rows_x, 1, 1
    )
    global_y = lax.axis_index("ny") * rows_y + jnp.arange(rows_y, dtype=jnp.int32).reshape(
        1, 1, rows_y
    )
    depth_index = jnp.arange(rows_z, dtype=jnp.int32).reshape(1, rows_z, 1)
    offsets = bond_offsets()
    intact_list = []
    for number, offset in enumerate(offsets):
        step_x, step_z, step_y = offset
        inside = global_x + step_x < extent_x
        inside = inside & (depth_index + step_z >= 0) & (depth_index + step_z < rows_z)
        inside = inside & (global_y + step_y >= 0) & (global_y + step_y < extent_y)
        intact_list.append(jnp.where(inside, bond_mask[number], 0).astype(jnp.float32))
    for repeat in range(STEPS):
        disp_ext = jnp.pad(extend(displacement), ((0, 0), (0, 0), (3, 3), (0, 0)))
        force_here = jnp.zeros(displacement.shape, jnp.float32)
        spread = jnp.zeros(disp_ext.shape, jnp.float32)
        for number, offset in enumerate(offsets):
            step_x, step_z, step_y = offset
            low_z, low_y = (3 + step_z, 3 + step_y)
            target = disp_ext[
                :, step_x : step_x + rows_x, low_z : low_z + rows_z, low_y : low_y + rows_y
            ]
            there = material_ext[
                :, step_x : step_x + rows_x, low_z : low_z + rows_z, low_y : low_y + rows_y
            ]
            force = pair_force(
                offset,
                displacement,
                target,
                modulus,
                there[0],
                strain_limit,
                there[1],
                intact_list[number],
            )
            force_here = force_here + force
            spread = spread + jnp.pad(
                -force, ((0, 0), (step_x, 3 - step_x), (low_z, 3 - step_z), (low_y, 3 - step_y))
            )
        spread = spread[:, :, 3 : 3 + rows_z, :]
        force = force_here + send_back(spread, rows_x, rows_y)
        velocity = velocity + time_step * force
        displacement = displacement + time_step * velocity
    return (displacement, velocity)


def solution(mesh):
    in_specs = (
        P(None, "wx", None, "ny"),
        P(None, "wx", None, "ny"),
        P("wx", None, "ny"),
        P(None, "wx", None, "ny"),
        P(),
        P(),
    )
    out_specs = (P(None, "wx", None, "ny"), P(None, "wx", None, "ny"))
    return jax.shard_map(
        on_device, mesh=mesh, in_specs=in_specs, out_specs=out_specs, check_vma=False
    )
```

profile of v0, /device:TPU:32, one launch (start us, length us, event | category | flops | bytes accessed | tf_op | source)
XLA Modules:
  0.0 181.6 jit_solution(18270894318590187046)
XLA Ops:
  0.6 1.6 fusion.3135
  2.3 0.7 fusion.3136
  3.0 0.7 copy-done.32
  3.7 5.0 %select_select_fusion = (f32[4,6,128]{2,0,1:T(4,128)S(1)}, pred[4,6,128]{2,0,1:T(4,128)(4,1)S(1)}, pred[4,6,128]{2,0,1:T(4,128)(4,1)S(1)}, pred[4,6,128]{2,0,1:T...) fusion(f32[]{:T(128)} %bitcast.17, f32[]{:T(128)} %bitcast.16, ...), kind=kLoop, calls=%fused_computation.4769 | loop fusion | flops 49152 | bytes 49184 | tf_op jit(solution)/shard_map/jit(_where)/select_n | solution.py:51
  8.7 4.9 %select_select_fusion.1 = f32[4,6,128]{2,0,1:T(4,128)S(1)} fusion(pred[4,6,128]{2,0,1:T(4,128)(4,1)S(1)} %get-tuple-element.563, pred[4,6,128]{2,0,1:T(4,128)(4,1)S(1)} %get-tuple-element.562, pred[4,6,128]{2,0,1:T(4,128)(4,1)S(1)} %get-tuple-element.561, pred[4,6,128]{2,0,1:T(4,128)(4,1)S(1)} %get-tuple-element.560, ...), kind=kLoop, calls=%fused_computation.4770 | loop fusion | flops 24576 | bytes 36896 | tf_op jit(solution)/shard_map/jit(_where)/select_n | solution.py:50
  13.7 4.4 %collective-permute-start.2 = (f32[2,4,6,3]{3,1,2,0:T(4,128)S(1)}, f32[2,4,6,3]{3,1,2,0:T(4,128)S(1)}, u32[]{:S(2)}, u32[]{:S(2)}) collective-permute-start(f32[2,4,6,3]{3,1,2,0:T(4,128)S(1)} %get-tuple-element.1366), channel_id=1, source_target_pairs={{0,1},{1,2},{2,3},{4,5},{5,6},{6,7},{8,9},{9,10},{10,11},{12,13},{... | collective-permute-start | bytes 1736 | tf_op jit(solution)/shard_map/ppermute | solution.py:20
  18.1 1.3 collective-permute-start
  19.5 4.9 %collective-permute-start.4 = (f32[3,4,6,3]{3,1,2,0:T(4,128)S(1)}, f32[3,4,6,3]{3,1,2,0:T(4,128)S(1)}, u32[]{:S(2)}, u32[]{:S(2)}) collective-permute-start(f32[3,4,6,3]{3,1,2,0:T(4,128)S(1)} %get-tuple-element.1364), channel_id=1, source_target_pairs={{0,1},{1,2},{2,3},{4,5},{5,6},{6,7},{8,9},{9,10},{10,11},{12,13},{... | collective-permute-start | bytes 2600 | tf_op jit(solution)/shard_map/ppermute | solution.py:20
  24.4 1.3 collective-permute-start.1
  26.2 10.3 %collective-permute-start.3 = (f32[2,3,6,134]{3,1,2,0:T(4,128)S(1)}, f32[2,3,6,134]{3,1,2,0:T(4,128)S(1)}, u32[]{:S(2)}, u32[]{:S(2)}) collective-permute-start(f32[2,3,6,134]{3,1,2,0:T(4,128)S(1)} %pad_maximum_fusion.10), channel_id=1, source_target_pairs={{4,0},{8,4},{12,8},{16,12},{20,16},{24,20},{28,24},{32,28},{36,32}... | collective-permute-start | bytes 57896 | tf_op jit(solution)/shard_map/ppermute | solution.py:31
  36.7 3.4 %collective-permute-start.5 = (f32[3,3,6,134]{3,1,2,0:T(4,128)S(1)}, f32[3,3,6,134]{3,1,2,0:T(4,128)S(1)}, u32[]{:S(2)}, u32[]{:S(2)}) collective-permute-start(f32[3,3,6,134]{3,1,2,0:T(4,128)S(1)} %pad_maximum_fusion.8), channel_id=1, source_target_pairs={{4,0},{8,4},{12,8},{16,12},{20,16},{24,20},{28,24},{32,28},{36,32}... | collective-permute-start | bytes 86840 | tf_op jit(solution)/shard_map/ppermute | solution.py:31
  40.2 0.7 multiply_bitcast_fusion.103
  40.9 0.7 multiply_bitcast_fusion.106
  41.6 0.7 multiply_bitcast_fusion.109
  42.5 0.4 copy-done.19
  44.3 0.7 multiply_bitcast_fusion.70
  45.0 0.7 multiply_bitcast_fusion.73
  51.7 0.7 fusion.2434
  54.1 2.5 %pad_add_fusion.2 = f32[3,7,12,134]{3,1,2,0:T(8,128)S(1)} fusion(f32[3,4,6,128]{3,1,2,0:T(4,128)S(1)} %fusion.122, f32[3,4,6,128]{3,1,2,0:T(4,128)S(1)} %fusion.123, f32[3,4,6,128]{3,1,2,0:T(4,128)S(1)} %fusion.124, f32[3,4,6,128]{3,1,2,0:T(4,128)S(1)} %fusion.125, f32[3,4,6,128]{3,1,2,0:T(4,128)S(1)} %fusion.126, f32[3,4,6,128]{3,1,2,0:T(4,128)S(1)} %fusion.127, ...), kind=kLoop, calls=%fused_computation.519 | loop fusion | flops 2026080 | bytes 2383776 | tf_op jit(solution)/shard_map/add | solution.py:135
  56.6 1.9 %collective-permute-start.6 = (f32[3,3,6,134]{3,1,2,0:T(4,128)S(1)}, f32[3,3,6,134]{3,1,2,0:T(4,128)S(1)}, u32[]{:S(2)}, u32[]{:S(2)}) collective-permute-start(f32[3,3,6,134]{3,1,2,0:T(4,128)S(1)} %slice.5429), channel_id=1, source_target_pairs={{0,4},{4,8},{8,12},{12,16},{16,20},{20,24},{24,28},{28,32},{32,36}... | collective-permute-start | bytes 86840 | tf_op jit(solution)/shard_map/ppermute | solution.py:31
  58.6 11.8 %collective-permute-done.6 = f32[3,3,6,134]{3,1,2,0:T(4,128)S(1)} collective-permute-done((f32[3,3,6,134]{3,1,2,0:T(4,128)S(1)}, f32[3,3,6,134]{3,1,2,0:T(4,128)S(1)}, u32[]{:S(2)}, u32[]{:S(2)}) %collective-permute-start.6) | collective-permute-done | bytes 28976 | tf_op jit(solution)/shard_map/ppermute | solution.py:31
  70.4 0.3 scatter-add.30
  70.8 1.3 collective-permute-start.7
  72.2 5.4 %collective-permute-start.8 = (f32[3,4,6,3]{3,1,2,0:T(4,128)S(1)}, f32[3,4,6,3]{3,1,2,0:T(4,128)S(1)}, u32[]{:S(2)}, u32[]{:S(2)}) collective-permute-start(f32[3,4,6,3]{3,1,2,0:T(4,128)S(1)} %get-tuple-element.1350), channel_id=1, source_target_pairs={{0,1},{1,2},{2,3},{4,5},{5,6},{6,7},{8,9},{9,10},{10,11},{12,13},{... | collective-permute-start | bytes 2600 | tf_op jit(solution)/shard_map/ppermute | solution.py:31
  77.6 2.8 %scatter-add.31 = f32[3,4,6,128]{3,1,2,0:T(4,128)S(1)} dynamic-update-slice(f32[3,4,6,128]{3,1,2,0:T(4,128)S(1)} %slice.5430, f32[3,4,6,3]{3,1,2,0:T(4,128)S(1)} %slice_add_fusion.8, s32[]{:T(128)} %constant.792.clone.1, s32[]{:T(128)} %constant.792.clone.1, s32[]{:T(128)} %constant.792.clone.1, s32[]{:T(128)} %constant.823.clone.1) | dynamic-update-slice | bytes 1732 | tf_op jit(solution)/shard_map/scatter-add | solution.py:85
  80.5 0.4 scatter-add.34
  80.9 0.2 copy-done.22
  81.2 0.7 multiply_add_fusion.4
  82.0 3.9 %collective-permute-start.10 = (f32[3,4,6,3]{3,1,2,0:T(4,128)S(1)}, f32[3,4,6,3]{3,1,2,0:T(4,128)S(1)}, u32[]{:S(2)}, u32[]{:S(2)}) collective-permute-start(f32[3,4,6,3]{3,1,2,0:T(4,128)S(1)} %get-tuple-element.1362), channel_id=1, source_target_pairs={{0,1},{1,2},{2,3},{4,5},{5,6},{6,7},{8,9},{9,10},{10,11},{12,13},{... | collective-permute-start | bytes 2600 | tf_op jit(solution)/shard_map/ppermute | solution.py:20
  86.0 1.3 collective-permute-start.9
  87.3 0.3 collective-permute-done.10
  87.6 4.2 %collective-permute-done.9 = f32[3,4,6,3]{3,1,2,0:T(4,128)S(1)} collective-permute-done((f32[3,4,6,3]{3,1,2,0:T(4,128)S(1)}, f32[3,4,6,3]{3,1,2,0:T(4,128)S(1)}, u32[]{:S(2)}, u32[]{:S(2)}) %collective-permute-start.9) | collective-permute-done | bytes 896 | tf_op jit(solution)/shard_map/ppermute | solution.py:23
  92.0 1.9 %collective-permute-start.11 = (f32[3,3,6,134]{3,1,2,0:T(4,128)S(1)}, f32[3,3,6,134]{3,1,2,0:T(4,128)S(1)}, u32[]{:S(2)}, u32[]{:S(2)}) collective-permute-start(f32[3,3,6,134]{3,1,2,0:T(4,128)S(1)} %pad_maximum_fusion.6), channel_id=1, source_target_pairs={{4,0},{8,4},{12,8},{16,12},{20,16},{24,20},{28,24},{32,28},{36,32}... | collective-permute-start | bytes 86840 | tf_op jit(solution)/shard_map/ppermute | solution.py:31
  94.0 0.6 copy-done.28
  94.8 1.0 collective-permute-done.11
  96.1 0.6 copy-done.2
  97.5 0.6 copy-done.27
  98.5 0.6 copy-done.26
  102.7 0.7 copy-done.25
  105.9 2.5 %pad_add_fusion.1 = f32[3,7,12,134]{3,1,2,0:T(8,128)S(1)} fusion(f32[3,4,6,128]{3,1,2,0:T(4,128)S(1)} %fusion.61, f32[3,4,6,128]{3,1,2,0:T(4,128)S(1)} %fusion.62, f32[3,4,6,128]{3,1,2,0:T(4,128)S(1)} %fusion.63, f32[3,4,6,128]{3,1,2,0:T(4,128)S(1)} %fusion.64, f32[3,4,6,128]{3,1,2,0:T(4,128)S(1)} %fusion.65, f32[3,4,6,128]{3,1,2,0:T(4,128)S(1)} %fusion.66, ...), kind=kLoop, calls=%fused_computation.518 | loop fusion | flops 2026080 | bytes 2383776 | tf_op jit(solution)/shard_map/add | solution.py:135
  108.4 1.9 %collective-permute-start.12 = (f32[3,3,6,134]{3,1,2,0:T(4,128)S(1)}, f32[3,3,6,134]{3,1,2,0:T(4,128)S(1)}, u32[]{:S(2)}, u32[]{:S(2)}) collective-permute-start(f32[3,3,6,134]{3,1,2,0:T(4,128)S(1)} %slice.5491), channel_id=1, source_target_pairs={{0,4},{4,8},{8,12},{12,16},{16,20},{20,24},{24,28},{28,32},{32,36}... | collective-permute-start | bytes 86840 | tf_op jit(solution)/shard_map/ppermute | solution.py:31
  110.3 12.4 %collective-permute-done.12 = f32[3,3,6,134]{3,1,2,0:T(4,128)S(1)} collective-permute-done((f32[3,3,6,134]{3,1,2,0:T(4,128)S(1)}, f32[3,3,6,134]{3,1,2,0:T(4,128)S(1)}, u32[]{:S(2)}, u32[]{:S(2)}) %collective-permute-start.12) | collective-permute-done | bytes 28976 | tf_op jit(solution)/shard_map/ppermute | solution.py:31
  122.8 0.3 scatter-add.35
  123.2 1.3 collective-permute-start.13
  124.5 4.8 %collective-permute-start.14 = (f32[3,4,6,3]{3,1,2,0:T(4,128)S(1)}, f32[3,4,6,3]{3,1,2,0:T(4,128)S(1)}, u32[]{:S(2)}, u32[]{:S(2)}) collective-permute-start(f32[3,4,6,3]{3,1,2,0:T(4,128)S(1)} %get-tuple-element.1345), channel_id=1, source_target_pairs={{0,1},{1,2},{2,3},{4,5},{5,6},{6,7},{8,9},{9,10},{10,11},{12,13},{... | collective-permute-start | bytes 2600 | tf_op jit(solution)/shard_map/ppermute | solution.py:31
  129.3 2.8 %scatter-add.36 = f32[3,4,6,128]{3,1,2,0:T(4,128)S(1)} dynamic-update-slice(f32[3,4,6,128]{3,1,2,0:T(4,128)S(1)} %slice.5492, f32[3,4,6,3]{3,1,2,0:T(4,128)S(1)} %slice_add_fusion.6, s32[]{:T(128)} %constant.792.clone.1, s32[]{:T(128)} %constant.792.clone.1, s32[]{:T(128)} %constant.792.clone.1, s32[]{:T(128)} %constant.823.clone.1) | dynamic-update-slice | bytes 1732 | tf_op jit(solution)/shard_map/scatter-add | solution.py:85
  132.2 0.4 scatter-add.39
  132.5 0.8 multiply_add_fusion.2
  133.4 3.2 %collective-permute-start.16 = (f32[3,4,6,3]{3,1,2,0:T(4,128)S(1)}, f32[3,4,6,3]{3,1,2,0:T(4,128)S(1)}, u32[]{:S(2)}, u32[]{:S(2)}) collective-permute-start(f32[3,4,6,3]{3,1,2,0:T(4,128)S(1)} %get-tuple-element.1360), channel_id=1, source_target_pairs={{0,1},{1,2},{2,3},{4,5},{5,6},{6,7},{8,9},{9,10},{10,11},{12,13},{... | collective-permute-start | bytes 2600 | tf_op jit(solution)/shard_map/ppermute | solution.py:20
  136.6 1.3 collective-permute-start.15
  137.9 0.3 collective-permute-done.16
  138.2 4.2 %collective-permute-done.15 = f32[3,4,6,3]{3,1,2,0:T(4,128)S(1)} collective-permute-done((f32[3,4,6,3]{3,1,2,0:T(4,128)S(1)}, f32[3,4,6,3]{3,1,2,0:T(4,128)S(1)}, u32[]{:S(2)}, u32[]{:S(2)}) %collective-permute-start.15) | collective-permute-done | bytes 896 | tf_op jit(solution)/shard_map/ppermute | solution.py:23
  142.6 1.9 %collective-permute-start.17 = (f32[3,3,6,134]{3,1,2,0:T(4,128)S(1)}, f32[3,3,6,134]{3,1,2,0:T(4,128)S(1)}, u32[]{:S(2)}, u32[]{:S(2)}) collective-permute-start(f32[3,3,6,134]{3,1,2,0:T(4,128)S(1)} %pad_maximum_fusion.4), channel_id=1, source_target_pairs={{4,0},{8,4},{12,8},{16,12},{20,16},{24,20},{28,24},{32,28},{36,32}... | collective-permute-start | bytes 86840 | tf_op jit(solution)/shard_map/ppermute | solution.py:31
  144.6 0.2 fusion.1738
  144.9 1.6 collective-permute-done.17
  154.1 2.5 %pad_add_fusion = f32[3,7,12,134]{3,1,2,0:T(8,128)S(1)} fusion(f32[3,4,6,128]{3,1,2,0:T(4,128)S(1)} %fusion, f32[3,4,6,128]{3,1,2,0:T(4,128)S(1)} %fusion.1, f32[3,4,6,128]{3,1,2,0:T(4,128)S(1)} %fusion.2, f32[3,4,6,128]{3,1,2,0:T(4,128)S(1)} %fusion.3, f32[3,4,6,128]{3,1,2,0:T(4,128)S(1)} %fusion.4, f32[3,4,6,128]{3,1,2,0:T(4,128)S(1)} %fusion.5, ...), kind=kLoop, calls=%fused_computation.517 | loop fusion | flops 2026080 | bytes 2383776 | tf_op jit(solution)/shard_map/add | solution.py:135
  156.6 1.9 %collective-permute-start.18 = (f32[3,3,6,134]{3,1,2,0:T(4,128)S(1)}, f32[3,3,6,134]{3,1,2,0:T(4,128)S(1)}, u32[]{:S(2)}, u32[]{:S(2)}) collective-permute-start(f32[3,3,6,134]{3,1,2,0:T(4,128)S(1)} %slice.5553), channel_id=1, source_target_pairs={{0,4},{4,8},{8,12},{12,16},{16,20},{20,24},{24,28},{28,32},{32,36}... | collective-permute-start | bytes 86840 | tf_op jit(solution)/shard_map/ppermute | solution.py:31
  158.6 11.9 %collective-permute-done.18 = f32[3,3,6,134]{3,1,2,0:T(4,128)S(1)} collective-permute-done((f32[3,3,6,134]{3,1,2,0:T(4,128)S(1)}, f32[3,3,6,134]{3,1,2,0:T(4,128)S(1)}, u32[]{:S(2)}, u32[]{:S(2)}) %collective-permute-start.18) | collective-permute-done | bytes 28976 | tf_op jit(solution)/shard_map/ppermute | solution.py:31
  170.5 0.3 scatter-add.40
  170.9 1.3 collective-permute-start.19
  172.2 4.5 %collective-permute-start.20 = (f32[3,4,6,3]{3,1,2,0:T(4,128)S(1)}, f32[3,4,6,3]{3,1,2,0:T(4,128)S(1)}, u32[]{:S(2)}, u32[]{:S(2)}) collective-permute-start(f32[3,4,6,3]{3,1,2,0:T(4,128)S(1)} %get-tuple-element.1340), channel_id=1, source_target_pairs={{0,1},{1,2},{2,3},{4,5},{5,6},{6,7},{8,9},{9,10},{10,11},{12,13},{... | collective-permute-start | bytes 2600 | tf_op jit(solution)/shard_map/ppermute | solution.py:31
  176.8 2.8 %scatter-add.41 = f32[3,4,6,128]{3,1,2,0:T(4,128)S(1)} dynamic-update-slice(f32[3,4,6,128]{3,1,2,0:T(4,128)S(1)} %slice.5554, f32[3,4,6,3]{3,1,2,0:T(4,128)S(1)} %slice_add_fusion.4, s32[]{:T(128)} %constant.792.clone.1, s32[]{:T(128)} %constant.792.clone.1, s32[]{:T(128)} %constant.792.clone.1, s32[]{:T(128)} %constant.823.clone.1) | dynamic-update-slice | bytes 1732 | tf_op jit(solution)/shard_map/scatter-add | solution.py:85
  179.6 0.4 scatter-add.44
  180.0 1.6 multiply_add_fusion
  (470 shorter events, 24.4 us)
Async XLA Ops:
  0.6 1.6 copy-start.31
  3.0 0.7 copy-start.32
  13.6 5.8 %copy-start = (f32[3,4,6,128]{3,1,2,0:T(4,128)S(1)}, f32[3,4,6,128]{3,1,2,0:T(4,128)}, u32[]{:S(2)}) copy-start(f32[3,4,6,128]{3,1,2,0:T(4,128)} %param.24) | copy-start | bytes 110596
  13.6 26.5 %copy-start.1 = (s32[61,4,6,128]{3,1,2,0:T(4,128)S(1)}, s32[61,4,6,128]{3,1,2,0:T(4,128)}, u32[]{:S(2)}) copy-start(s32[61,4,6,128]{3,1,2,0:T(4,128)} %param.27) | copy-start | bytes 2248708
  13.7 12.4 %collective-permute-start.2 = (f32[2,4,6,3]{3,1,2,0:T(4,128)S(1)}, f32[2,4,6,3]{3,1,2,0:T(4,128)S(1)}, u32[]{:S(2)}, u32[]{:S(2)}) collective-permute-start(f32[2,4,6,3]{3,1,2,0:T(4,128)S(1)} %get-tuple-element.1366), channel_id=1, source_target_pairs={{0,1},{1,2},{2,3},{4,5},{5,6},{6,7},{8,9},{9,10},{10,11},{12,13},{... | collective-permute-start | bytes 1736 | tf_op jit(solution)/shard_map/ppermute | solution.py:20
  18.1 8.0 %collective-permute-start = (f32[2,4,6,3]{3,1,2,0:T(4,128)S(1)}, f32[2,4,6,3]{3,1,2,0:T(4,128)S(1)}, u32[]{:S(2)}, u32[]{:S(2)}) collective-permute-start(f32[2,4,6,3]{3,1,2,0:T(4,128)S(1)} %get-tuple-element.1367), channel_id=1, source_target_pairs={{1,0},{2,1},{3,2},{5,4},{6,5},{7,6},{9,8},{10,9},{11,10},{13,12},{... | collective-permute-start | bytes 1736 | tf_op jit(solution)/shard_map/ppermute | solution.py:23
  19.5 17.0 %collective-permute-start.4 = (f32[3,4,6,3]{3,1,2,0:T(4,128)S(1)}, f32[3,4,6,3]{3,1,2,0:T(4,128)S(1)}, u32[]{:S(2)}, u32[]{:S(2)}) collective-permute-start(f32[3,4,6,3]{3,1,2,0:T(4,128)S(1)} %get-tuple-element.1364), channel_id=1, source_target_pairs={{0,1},{1,2},{2,3},{4,5},{5,6},{6,7},{8,9},{9,10},{10,11},{12,13},{... | collective-permute-start | bytes 2600 | tf_op jit(solution)/shard_map/ppermute | solution.py:20
  24.4 12.1 %collective-permute-start.1 = (f32[3,4,6,3]{3,1,2,0:T(4,128)S(1)}, f32[3,4,6,3]{3,1,2,0:T(4,128)S(1)}, u32[]{:S(2)}, u32[]{:S(2)}) collective-permute-start(f32[3,4,6,3]{3,1,2,0:T(4,128)S(1)} %get-tuple-element.1365), channel_id=1, source_target_pairs={{1,0},{2,1},{3,2},{5,4},{6,5},{7,6},{9,8},{10,9},{11,10},{13,12},{... | collective-permute-start | bytes 2600 | tf_op jit(solution)/shard_map/ppermute | solution.py:23
  26.2 16.9 %collective-permute-start.3 = (f32[2,3,6,134]{3,1,2,0:T(4,128)S(1)}, f32[2,3,6,134]{3,1,2,0:T(4,128)S(1)}, u32[]{:S(2)}, u32[]{:S(2)}) collective-permute-start(f32[2,3,6,134]{3,1,2,0:T(4,128)S(1)} %pad_maximum_fusion.10), channel_id=1, source_target_pairs={{4,0},{8,4},{12,8},{16,12},{20,16},{24,20},{28,24},{32,28},{36,32}... | collective-permute-start | bytes 57896 | tf_op jit(solution)/shard_map/ppermute | solution.py:31
  36.7 6.6 %collective-permute-start.5 = (f32[3,3,6,134]{3,1,2,0:T(4,128)S(1)}, f32[3,3,6,134]{3,1,2,0:T(4,128)S(1)}, u32[]{:S(2)}, u32[]{:S(2)}) collective-permute-start(f32[3,3,6,134]{3,1,2,0:T(4,128)S(1)} %pad_maximum_fusion.8), channel_id=1, source_target_pairs={{4,0},{8,4},{12,8},{16,12},{20,16},{24,20},{28,24},{32,28},{36,32}... | collective-permute-start | bytes 86840 | tf_op jit(solution)/shard_map/ppermute | solution.py:31
  40.9 2.1 %copy-start.15 = (f32[1,4,6,128]{3,1,2,0:T(4,128)}, f32[1,4,6,128]{3,1,2,0:T(4,128)S(1)}, u32[]{:S(2)}) copy-start(f32[1,4,6,128]{3,1,2,0:T(4,128)S(1)} %get-tuple-element.378) | copy-start | bytes 36868
  41.6 1.5 copy-start.17
  42.3 0.6 copy-start.19
  42.4 0.6 copy-start.3
  42.4 0.6 copy-start.5
  42.5 0.6 copy-start.7
  42.5 0.6 copy-start.9
  42.5 0.6 copy-start.11
  42.5 0.6 copy-start.13
  45.0 8.8 %copy-start.21 = (f32[1,4,6,128]{3,1,2,0:T(4,128)}, f32[1,4,6,128]{3,1,2,0:T(4,128)S(1)}, u32[]{:S(2)}) copy-start(f32[1,4,6,128]{3,1,2,0:T(4,128)S(1)} %get-tuple-element.552) | copy-start | bytes 36868
  45.7 7.0 %copy-start.23 = (f32[1,4,6,128]{3,1,2,0:T(4,128)}, f32[1,4,6,128]{3,1,2,0:T(4,128)S(1)}, u32[]{:S(2)}) copy-start(f32[1,4,6,128]{3,1,2,0:T(4,128)S(1)} %get-tuple-element.525) | copy-start | bytes 36868
  56.6 13.8 %collective-permute-start.6 = (f32[3,3,6,134]{3,1,2,0:T(4,128)S(1)}, f32[3,3,6,134]{3,1,2,0:T(4,128)S(1)}, u32[]{:S(2)}, u32[]{:S(2)}) collective-permute-start(f32[3,3,6,134]{3,1,2,0:T(4,128)S(1)} %slice.5429), channel_id=1, source_target_pairs={{0,4},{4,8},{8,12},{12,16},{16,20},{20,24},{24,28},{28,32},{32,36}... | collective-permute-start | bytes 86840 | tf_op jit(solution)/shard_map/ppermute | solution.py:31
  70.8 6.8 %collective-permute-start.7 = (f32[3,4,6,3]{3,1,2,0:T(4,128)S(1)}, f32[3,4,6,3]{3,1,2,0:T(4,128)S(1)}, u32[]{:S(2)}, u32[]{:S(2)}) collective-permute-start(f32[3,4,6,3]{3,1,2,0:T(4,128)S(1)} %get-tuple-element.1351), channel_id=1, source_target_pairs={{1,0},{2,1},{3,2},{5,4},{6,5},{7,6},{9,8},{10,9},{11,10},{13,12},{... | collective-permute-start | bytes 2600 | tf_op jit(solution)/shard_map/ppermute | solution.py:31
  72.1 8.8 %copy-start.16 = (f32[1,4,6,128]{3,1,2,0:T(4,128)S(1)}, f32[1,4,6,128]{3,1,2,0:T(4,128)}, u32[]{:S(2)}) copy-start(f32[1,4,6,128]{3,1,2,0:T(4,128)} %copy-done.15) | copy-start | bytes 36868
  72.1 8.8 %copy-start.18 = (f32[1,4,6,128]{3,1,2,0:T(4,128)S(1)}, f32[1,4,6,128]{3,1,2,0:T(4,128)}, u32[]{:S(2)}) copy-start(f32[1,4,6,128]{3,1,2,0:T(4,128)} %copy-done.17) | copy-start | bytes 36868
  72.1 8.8 %copy-start.20 = (f32[1,4,6,128]{3,1,2,0:T(4,128)S(1)}, f32[1,4,6,128]{3,1,2,0:T(4,128)}, u32[]{:S(2)}) copy-start(f32[1,4,6,128]{3,1,2,0:T(4,128)} %copy-done.19) | copy-start | bytes 36868
  72.1 8.8 %copy-start.30 = (f32[3,4,6,128]{3,1,2,0:T(4,128)S(1)}, f32[3,4,6,128]{3,1,2,0:T(4,128)}, u32[]{:S(2)}) copy-start(f32[3,4,6,128]{3,1,2,0:T(4,128)} %param.25) | copy-start | bytes 110596
  72.2 8.2 %collective-permute-start.8 = (f32[3,4,6,3]{3,1,2,0:T(4,128)S(1)}, f32[3,4,6,3]{3,1,2,0:T(4,128)S(1)}, u32[]{:S(2)}, u32[]{:S(2)}) collective-permute-start(f32[3,4,6,3]{3,1,2,0:T(4,128)S(1)} %get-tuple-element.1350), channel_id=1, source_target_pairs={{0,1},{1,2},{2,3},{4,5},{5,6},{6,7},{8,9},{9,10},{10,11},{12,13},{... | collective-permute-start | bytes 2600 | tf_op jit(solution)/shard_map/ppermute | solution.py:31
  80.4 0.7 copy-start.22
  80.4 0.7 copy-start.24
  80.4 0.7 copy-start.4
  80.4 0.7 copy-start.6
  80.5 0.7 copy-start.8
  80.5 0.7 copy-start.10
  80.5 0.7 copy-start.12
  80.5 0.7 copy-start.14
  82.0 5.5 %collective-permute-start.10 = (f32[3,4,6,3]{3,1,2,0:T(4,128)S(1)}, f32[3,4,6,3]{3,1,2,0:T(4,128)S(1)}, u32[]{:S(2)}, u32[]{:S(2)}) collective-permute-start(f32[3,4,6,3]{3,1,2,0:T(4,128)S(1)} %get-tuple-element.1362), channel_id=1, source_target_pairs={{0,1},{1,2},{2,3},{4,5},{5,6},{6,7},{8,9},{9,10},{10,11},{12,13},{... | collective-permute-start | bytes 2600 | tf_op jit(solution)/shard_map/ppermute | solution.py:20
  86.0 5.9 %collective-permute-start.9 = (f32[3,4,6,3]{3,1,2,0:T(4,128)S(1)}, f32[3,4,6,3]{3,1,2,0:T(4,128)S(1)}, u32[]{:S(2)}, u32[]{:S(2)}) collective-permute-start(f32[3,4,6,3]{3,1,2,0:T(4,128)S(1)} %get-tuple-element.1363), channel_id=1, source_target_pairs={{1,0},{2,1},{3,2},{5,4},{6,5},{7,6},{9,8},{10,9},{11,10},{13,12},{... | collective-permute-start | bytes 2600 | tf_op jit(solution)/shard_map/ppermute | solution.py:23
  92.0 3.9 %collective-permute-start.11 = (f32[3,3,6,134]{3,1,2,0:T(4,128)S(1)}, f32[3,3,6,134]{3,1,2,0:T(4,128)S(1)}, u32[]{:S(2)}, u32[]{:S(2)}) collective-permute-start(f32[3,3,6,134]{3,1,2,0:T(4,128)S(1)} %pad_maximum_fusion.6), channel_id=1, source_target_pairs={{4,0},{8,4},{12,8},{16,12},{20,16},{24,20},{28,24},{32,28},{36,32}... | collective-permute-start | bytes 86840 | tf_op jit(solution)/shard_map/ppermute | solution.py:31
  93.9 0.7 copy-start.28
  93.9 0.7 copy-start.29
  96.0 0.7 copy-start.2
  97.4 0.7 copy-start.27
  98.4 0.7 copy-start.26
  102.6 0.7 copy-start.25
  108.4 14.4 %collective-permute-start.12 = (f32[3,3,6,134]{3,1,2,0:T(4,128)S(1)}, f32[3,3,6,134]{3,1,2,0:T(4,128)S(1)}, u32[]{:S(2)}, u32[]{:S(2)}) collective-permute-start(f32[3,3,6,134]{3,1,2,0:T(4,128)S(1)} %slice.5491), channel_id=1, source_target_pairs={{0,4},{4,8},{8,12},{12,16},{16,20},{20,24},{24,28},{28,32},{32,36}... | collective-permute-start | bytes 86840 | tf_op jit(solution)/shard_map/ppermute | solution.py:31
  123.2 6.2 %collective-permute-start.13 = (f32[3,4,6,3]{3,1,2,0:T(4,128)S(1)}, f32[3,4,6,3]{3,1,2,0:T(4,128)S(1)}, u32[]{:S(2)}, u32[]{:S(2)}) collective-permute-start(f32[3,4,6,3]{3,1,2,0:T(4,128)S(1)} %get-tuple-element.1346), channel_id=1, source_target_pairs={{1,0},{2,1},{3,2},{5,4},{6,5},{7,6},{9,8},{10,9},{11,10},{13,12},{... | collective-permute-start | bytes 2600 | tf_op jit(solution)/shard_map/ppermute | solution.py:31
  124.5 7.6 %collective-permute-start.14 = (f32[3,4,6,3]{3,1,2,0:T(4,128)S(1)}, f32[3,4,6,3]{3,1,2,0:T(4,128)S(1)}, u32[]{:S(2)}, u32[]{:S(2)}) collective-permute-start(f32[3,4,6,3]{3,1,2,0:T(4,128)S(1)} %get-tuple-element.1345), channel_id=1, source_target_pairs={{0,1},{1,2},{2,3},{4,5},{5,6},{6,7},{8,9},{9,10},{10,11},{12,13},{... | collective-permute-start | bytes 2600 | tf_op jit(solution)/shard_map/ppermute | solution.py:31
  133.4 4.8 %collective-permute-start.16 = (f32[3,4,6,3]{3,1,2,0:T(4,128)S(1)}, f32[3,4,6,3]{3,1,2,0:T(4,128)S(1)}, u32[]{:S(2)}, u32[]{:S(2)}) collective-permute-start(f32[3,4,6,3]{3,1,2,0:T(4,128)S(1)} %get-tuple-element.1360), channel_id=1, source_target_pairs={{0,1},{1,2},{2,3},{4,5},{5,6},{6,7},{8,9},{9,10},{10,11},{12,13},{... | collective-permute-start | bytes 2600 | tf_op jit(solution)/shard_map/ppermute | solution.py:20
  136.6 5.9 %collective-permute-start.15 = (f32[3,4,6,3]{3,1,2,0:T(4,128)S(1)}, f32[3,4,6,3]{3,1,2,0:T(4,128)S(1)}, u32[]{:S(2)}, u32[]{:S(2)}) collective-permute-start(f32[3,4,6,3]{3,1,2,0:T(4,128)S(1)} %get-tuple-element.1361), channel_id=1, source_target_pairs={{1,0},{2,1},{3,2},{5,4},{6,5},{7,6},{9,8},{10,9},{11,10},{13,12},{... | collective-permute-start | bytes 2600 | tf_op jit(solution)/shard_map/ppermute | solution.py:23
  142.6 3.9 %collective-permute-start.17 = (f32[3,3,6,134]{3,1,2,0:T(4,128)S(1)}, f32[3,3,6,134]{3,1,2,0:T(4,128)S(1)}, u32[]{:S(2)}, u32[]{:S(2)}) collective-permute-start(f32[3,3,6,134]{3,1,2,0:T(4,128)S(1)} %pad_maximum_fusion.4), channel_id=1, source_target_pairs={{4,0},{8,4},{12,8},{16,12},{20,16},{24,20},{28,24},{32,28},{36,32}... | collective-permute-start | bytes 86840 | tf_op jit(solution)/shard_map/ppermute | solution.py:31
  156.6 13.9 %collective-permute-start.18 = (f32[3,3,6,134]{3,1,2,0:T(4,128)S(1)}, f32[3,3,6,134]{3,1,2,0:T(4,128)S(1)}, u32[]{:S(2)}, u32[]{:S(2)}) collective-permute-start(f32[3,3,6,134]{3,1,2,0:T(4,128)S(1)} %slice.5553), channel_id=1, source_target_pairs={{0,4},{4,8},{8,12},{12,16},{16,20},{20,24},{24,28},{28,32},{32,36}... | collective-permute-start | bytes 86840 | tf_op jit(solution)/shard_map/ppermute | solution.py:31
  170.9 5.9 %collective-permute-start.19 = (f32[3,4,6,3]{3,1,2,0:T(4,128)S(1)}, f32[3,4,6,3]{3,1,2,0:T(4,128)S(1)}, u32[]{:S(2)}, u32[]{:S(2)}) collective-permute-start(f32[3,4,6,3]{3,1,2,0:T(4,128)S(1)} %get-tuple-element.1341), channel_id=1, source_target_pairs={{1,0},{2,1},{3,2},{5,4},{6,5},{7,6},{9,8},{10,9},{11,10},{13,12},{... | collective-permute-start | bytes 2600 | tf_op jit(solution)/shard_map/ppermute | solution.py:31
  172.2 7.4 %collective-permute-start.20 = (f32[3,4,6,3]{3,1,2,0:T(4,128)S(1)}, f32[3,4,6,3]{3,1,2,0:T(4,128)S(1)}, u32[]{:S(2)}, u32[]{:S(2)}) collective-permute-start(f32[3,4,6,3]{3,1,2,0:T(4,128)S(1)} %get-tuple-element.1340), channel_id=1, source_target_pairs={{0,1},{1,2},{2,3},{4,5},{5,6},{6,7},{8,9},{9,10},{10,11},{12,13},{... | collective-permute-start | bytes 2600 | tf_op jit(solution)/shard_map/ppermute | solution.py:31
where the time goes:
time: 183 us; the launch traced here: 182 us
  starting transfers between devices  63.5 us (35%)
  other arithmetic  47.9 us (26%)
  waiting for transfers between devices  47.9 us (26%)
  local copies, waits for them, and re-layouts  18.1 us (10%)
  between operations  4.14 us (2%)
    ppermute x13, starting transfers between devices, shifted(): lax.ppermute(value, axis, [(source, source + steps) for source in range(i...  41.9 us
    ppermute x13, waiting for transfers between devices, shifted(): lax.ppermute(value, axis, [(source, source + steps) for source in range(i...  38.8 us
    another operation x171, other arithmetic, pair_force(): return jnp.stack([magnitude * part for part in relative])  23.5 us
    ppermute x4, starting transfers between devices, with_halo(): lax.ppermute(lax.slice_in_dim(block, block.shape[dim] - width, None, axis...  16.4 us
    ppermute x4, waiting for transfers between devices, with_halo(): lax.ppermute(lax.slice_in_dim(block, 0, width, axis=dim), axis, backward)  8.48 us
    scatter-add x3, local copies, waits for them, and re-layouts, send_back(): interior = interior.at[:, :, :, rows_y - 3:].add(lower_rim)  8.35 us
    add x3, other arithmetic, on_device(): spread + jnp.pad(-force, ((0, 0), (step_x, 3 - step_x), (low_z, 3 - step_...  7.41 us
    ppermute x4, starting transfers between devices, with_halo(): lax.ppermute(lax.slice_in_dim(block, 0, width, axis=dim), axis, backward)  5.17 us
  transfers between devices with their start and end apart: 21, of which 9 were waited for; matrix products, arithmetic and copies ran while one was open for 7% of the time, Pallas kernels for 0%

commit v1 on v0

v1 whole, which is shorter than its diff:
```python
import math

import jax
import jax.numpy as jnp
from jax import lax
from jax.experimental import pallas as pl
from jax.experimental.pallas import tpu as pltpu
from jax.sharding import PartitionSpec as P

STEPS = 3
MATS = 8
DT = 0.05
X, Z, Y = 4, 6, 128
R = X * Z
W = 9
G = 42
SLOTS = 4
F32 = jnp.float32


def bond_offsets():
    out = []
    for a in range(0, 4):
        for b in range(-3, 4):
            for c in range(-3, 4):
                if a * a + b * b + c * c <= 9:
                    if a > 0 or (a == 0 and (b > 0 or (b == 0 and c > 0))):
                        out.append((a, b, c))
    return out


OFFS = bond_offsets()
NB = len(OFFS)
CROSS = [k for k in range(NB) if OFFS[k][0] > 0]


def rows_of(k):
    return OFFS[k][0] * Z + OFFS[k][1]


PREV_AT = {}
_at = 0
for _k in CROSS:
    PREV_AT[_k] = _at
    _at += rows_of(_k)
PREV_ROWS = -(-_at // 8) * 8
STATE0 = 5 * R
UNITS = 18 + NB + len(CROSS)
YROWS = -(-UNITS // SLOTS) * 8
EDGE = 8
BLOCK = R + EDGE


def lanes(rows):
    return lax.broadcasted_iota(jnp.int32, (rows, Y), 1)


def roll(x, shift):
    shift %= Y
    return x if shift == 0 else pltpu.roll(x, shift, axis=1)


def params(n):
    return pltpu.CompilerParams(vmem_limit_bytes=n << 20)


def vmem(n):
    return [pl.BlockSpec(memory_space=pltpu.VMEM)] * n


def smem(n):
    return [pl.BlockSpec(memory_space=pltpu.SMEM)] * n


def shape(rows):
    return jax.ShapeDtypeStruct((rows, Y), F32)


def first_kernel(nwx, nny, stiff, crit, u, v, lab, mask, st, xf, v0, m_out, tmp):
    wx, ny = lax.axis_index("wx"), lax.axis_index("ny")
    for q in range(3):
        for x in range(X):
            st[q * R + x * Z : q * R + (x + 1) * Z, :] = u[pl.ds(q * R + x, Z, stride=X), :]
            v0[q * R + x * Z : q * R + (x + 1) * Z, :] = v[pl.ds(q * R + x, Z, stride=X), :]
    for x in range(X):
        tmp[x * Z : (x + 1) * Z, :] = lab[pl.ds(x, Z, stride=X), :]
    label = tmp[...]
    mod = jnp.zeros((R, Y), F32)
    lim = jnp.zeros((R, Y), F32)
    for t in range(MATS):
        hit = label == t
        mod = jnp.where(hit, stiff[t], mod)
        lim = jnp.where(hit, crit[t], lim)
    st[3 * R : 4 * R, :] = mod
    st[4 * R : 5 * R, :] = lim
    xf[0:STATE0, :] = st[...]
    row = lax.broadcasted_iota(jnp.int32, (R, Y), 0)
    zi = row % Z
    gx = wx * X + row // Z
    gy = ny * Y + lanes(R)
    for k, (a, b, c) in enumerate(OFFS):
        for x in range(X):
            m_out[k * R + x * Z : k * R + (x + 1) * Z, :] = mask[
                pl.ds(k * R + x, Z, stride=X), :
            ].astype(F32)
        ok = (zi + b >= 0) & (zi + b < Z) & (gx + a < nwx * X)
        if c:
            ok = ok & (gy + c >= 0) & (gy + c < nny * Y)
        m_out[k * R : (k + 1) * R, :] = jnp.where(ok, m_out[k * R : (k + 1) * R, :], 0.0)
        if a:
            o = rows_of(k)
            at = STATE0 + PREV_AT[k]
            xf[at : at + o, :] = m_out[(k + 1) * R - o : (k + 1) * R, :]
    if _at < PREV_ROWS:
        xf[STATE0 + _at : STATE0 + PREV_ROWS, :] = jnp.zeros((PREV_ROWS - _at, Y), F32)


def pack_kernel(st, rf, rb, v0, m, to_upper, to_lower, buf):
    def unit(n):
        if n < 15:
            s, q = (n // 3, n % 3) if n < 9 else (n % 3, 3 + (n - 9) // 3)
            return (rf, st, rb)[s][q * R : (q + 1) * R, :]
        if n < 18:
            return v0[(n - 15) * R : (n - 14) * R, :]
        if n < 18 + NB:
            return m[(n - 18) * R : (n - 17) * R, :]
        k = CROSS[n - 18 - NB]
        o = rows_of(k)
        at = (n - 18 - NB) * R
        buf[at : at + R - o, :] = jnp.zeros((R - o, Y), F32)
        buf[at + R - o : at + R, :] = rf[STATE0 + PREV_AT[k] : STATE0 + PREV_AT[k] + o, :]
        return buf[at : at + R, :]

    lane = lanes(8)
    for t in range(YROWS // 8):
        up = jnp.zeros((8, Y), F32)
        low = jnp.zeros((8, Y), F32)
        for p in range(SLOTS):
            if t * SLOTS + p >= UNITS:
                continue
            value = unit(t * SLOTS + p)
            for g in range(3):
                part = value[8 * g : 8 * g + 8, :]
                at = G * g + W * p
                here = (lane >= at) & (lane < at + W)
                up = jnp.where(here, roll(part, at + W), up)
                low = jnp.where(here, roll(part, at), low)
        to_upper[8 * t : 8 * t + 8, :] = up
        to_lower[8 * t : 8 * t + 8, :] = low


def expand(edge):
    lane = lanes(8)
    keep = (lane < W) | (lane >= Y - W)
    return [jnp.where(keep, roll(edge, Y - W - G * g), 0.0) for g in range(3)]


def spread_shifts(main, side, number, sh, qh, with_edge):
    rows = 3 * R
    lane = lanes(rows)
    for c in range(-3, 4):
        at = (number * 7 + c + 3) * rows
        if c == 0:
            moved, outer = main, side
        else:
            a, b = roll(main, -c), roll(side, -c)
            inner = (lane + c >= 0) & (lane + c < Y)
            moved, outer = jnp.where(inner, a, b), jnp.where(inner, b, a)
        sh[at : at + rows, :] = moved
        if with_edge:
            q = rows - 16
            ln = lanes(q)
            packed = jnp.where(
                ln < G,
                roll(outer[0:q, :], W),
                jnp.where(ln < 2 * G, roll(outer[8 : q + 8, :], G + W), roll(outer[16:, :], 2 * G + W)),
            )
            at = (number * 7 + c + 3) * q
            qh[at : at + q, :] = packed


def neighbours(sh, qh, number, o, c):
    rows, q = 3 * R, 3 * R - 16
    at = (number * 7 + c + 3) * rows + R + o
    main = sh[at : at + R, :]
    if qh is None:
        return main, None
    at = (number * 7 + c + 3) * q + R + o
    return main, qh[at : at + EDGE, :]


def pair_terms(d, here, there, kk, hh, length, acc):
    e = [there[q] + float(d[q]) - here[q] if d[q] else there[q] - here[q] for q in range(3)]
    t = jnp.sqrt(e[0] * e[0] + e[1] * e[1] + e[2] * e[2]) - length
    mag = kk * t / (hh + t * t)
    return [acc[q] + mag * e[q] for q in range(3)]


def forces(u_main, u_edge, sh, qh, kc, hc):
    acc = [jnp.zeros((R, Y), F32) for _ in range(3)]
    acc_e = [jnp.zeros((EDGE, Y), F32) for _ in range(3)]
    for k, off in enumerate(OFFS):
        length = math.sqrt(off[0] ** 2 + off[1] ** 2 + off[2] ** 2)
        for way in (0, 1):
            sign = 1 - 2 * way
            d = [sign * x for x in off]
            n = 2 * k + way
            both = [neighbours(sh, qh, q, sign * rows_of(k), d[2]) for q in range(3)]
            at = n * BLOCK
            acc = pair_terms(
                d, u_main, [x[0] for x in both], kc[at : at + R, :], hc[at : at + R, :], length, acc
            )
            if qh is not None:
                acc_e = pair_terms(
                    d, u_edge, [x[1] for x in both],
                    kc[at + R : at + BLOCK, :], hc[at + R : at + BLOCK, :], length, acc_e,
                )
    return acc, acc_e


def slab_sides(edges):
    return jnp.concatenate(sum([expand(e) for e in edges], []), axis=0)


def start_kernel(st, rf, rb, v0, m, rl, ru, kc, hc, s1, v1, sh, qh, tm0, tm1):
    lane = lanes(8)
    place = lane % G
    below = (place < W) & (lane < 3 * G)
    above = (place >= W) & (place < 2 * W) & (lane < 3 * G)

    def edge(n):
        t, p = n // SLOTS, n % SLOTS
        lo = roll(rl[8 * t : 8 * t + 8, :], -W * p)
        hi = roll(ru[8 * t : 8 * t + 8, :], W - W * p)
        return jnp.where(below, lo, jnp.where(above, hi, 0.0))

    def filled(x):
        return jnp.where(x > 0.0, x, 1.0)

    own_edge = []
    for q in range(5):
        at = q * R
        main = jnp.concatenate([rf[at : at + R, :], st[at : at + R, :], rb[at : at + R, :]], axis=0)
        edges = [edge(s * 3 + q) if q < 3 else edge(9 + 3 * (q - 3) + s) for s in range(3)]
        side = slab_sides(edges)
        if q >= 3:
            main, side = filled(main), filled(side)
        own_edge.append(edges[1] if q < 3 else filled(edges[1]))
        spread_shifts(main, side, q, sh, qh, True)

    mod, lim = st[3 * R : 4 * R, :], st[4 * R : 5 * R, :]
    mod_e, lim_e = own_edge[3], own_edge[4]

    def coefficients(mask, m_i, m_j, l_i, l_j, length):
        half = 0.5 * (l_i + l_j)
        sq = half * half
        kk = mask * (2.0 * m_i * m_j / (m_i + m_j)) * sq * (1.0 / length)
        return kk, sq * (length * length)

    cross = {k: i for i, k in enumerate(CROSS)}
    zero = jnp.zeros((R, Y), F32)
    for k, off in enumerate(OFFS):
        length = math.sqrt(off[0] ** 2 + off[1] ** 2 + off[2] ** 2)
        o, c = rows_of(k), off[2]
        mask = m[k * R : (k + 1) * R, :]
        mask_e = edge(18 + k)
        base = k * 2 * R
        tm0[base + R : base + 2 * R, :] = mask
        tm1[base + R : base + 2 * R, :] = slab_sides([mask_e])
        if o:
            tm0[base : base + R, :] = zero
            tm1[base : base + R, :] = zero
            if k in cross:
                tm0[base + R - o : base + R, :] = rf[
                    STATE0 + PREV_AT[k] : STATE0 + PREV_AT[k] + o, :
                ]
                tm1[base : base + R, :] = slab_sides([edge(18 + NB + cross[k])])
        a, b = tm0[base + R - o : base + 2 * R - o, :], tm1[base + R - o : base + 2 * R - o, :]
        if c:
            a, b = roll(a, c), roll(b, c)
            ln = lanes(R)
            inner = (ln - c >= 0) & (ln - c < Y)
            a, b = jnp.where(inner, a, b), jnp.where(inner, b, a)
        b_e = jnp.where(
            lane < G,
            roll(b[0:8, :], W),
            jnp.where(lane < 2 * G, roll(b[8:16, :], G + W), roll(b[16:24, :], 2 * G + W)),
        )
        for way, (mm, me) in enumerate(((mask, mask_e), (a, b_e))):
            sign = 1 - 2 * way
            mj, mj_e = neighbours(sh, qh, 3, sign * o, sign * c)
            lj, lj_e = neighbours(sh, qh, 4, sign * o, sign * c)
            at = (2 * k + way) * BLOCK
            kk, hh = coefficients(mm, mod, mj, lim, lj, length)
            kc[at : at + R, :] = kk
            hc[at : at + R, :] = hh
            kk, hh = coefficients(me, mod_e, mj_e, lim_e, lj_e, length)
            kc[at + R : at + BLOCK, :] = kk
            hc[at + R : at + BLOCK, :] = hh

    u_main = [st[q * R : (q + 1) * R, :] for q in range(3)]
    acc, acc_e = forces(u_main, own_edge[:3], sh, qh, kc, hc)
    for q in range(3):
        vel = v0[q * R : (q + 1) * R, :] + DT * acc[q]
        vel_e = edge(15 + q) + DT * acc_e[q]
        at = q * BLOCK
        v1[at : at + R, :] = vel
        v1[at + R : at + BLOCK, :] = vel_e
        s1[at : at + R, :] = u_main[q] + DT * vel
        s1[at + R : at + BLOCK, :] = own_edge[q] + DT * vel_e


def step_kernel(last, s, ra, rb, v, kc, hc, s_out, v_out, sh, qh, ext, side):
    even = lax.rem(lax.axis_index("wx"), 2) == 0
    for q in range(3):
        at = q * BLOCK
        top = jnp.where(even, rb[at : at + BLOCK, :], ra[at : at + BLOCK, :])
        end = jnp.where(even, ra[at : at + BLOCK, :], rb[at : at + BLOCK, :])
        mid = s[at : at + BLOCK, :]
        main = jnp.concatenate([top[:R], mid[:R], end[:R]], axis=0)
        sides = slab_sides([top[R:], mid[R:], end[R:]])
        spread_shifts(main, sides, q, sh, qh, not last)
    u_main = [s[q * BLOCK : q * BLOCK + R, :] for q in range(3)]
    u_edge = [s[q * BLOCK + R : (q + 1) * BLOCK, :] for q in range(3)]
    acc, acc_e = forces(u_main, u_edge, sh, None if last else qh, kc, hc)
    for q in range(3):
        at = q * BLOCK
        vel = v[at : at + R, :] + DT * acc[q]
        dis = u_main[q] + DT * vel
        if last:
            ext[q * R : (q + 1) * R, :] = dis
            side[q * R : (q + 1) * R, :] = vel
            for x in range(X):
                rows = slice(q * R + x * Z, q * R + (x + 1) * Z)
                s_out[pl.ds(q * R + x, Z, stride=X), :] = ext[rows, :]
                v_out[pl.ds(q * R + x, Z, stride=X), :] = side[rows, :]
        else:
            v_out[at : at + R, :] = vel
            s_out[at : at + R, :] = dis
            vel_e = v[at + R : at + BLOCK, :] + DT * acc_e[q]
            v_out[at + R : at + BLOCK, :] = vel_e
            s_out[at + R : at + BLOCK, :] = u_edge[q] + DT * vel_e


def on_device(nwx, nny, displacement, velocity, labels, bond_mask, stiffness, critical):
    import functools

    flat = lambda x: x.transpose(0, 2, 1, 3).reshape(-1, Y)
    u, v, mask = flat(displacement), flat(velocity), flat(bond_mask)
    lab = labels.transpose(1, 0, 2).reshape(R, Y)
    st, xf, v0, m = pl.pallas_call(
        functools.partial(first_kernel, nwx, nny),
        out_shape=(shape(STATE0), shape(STATE0 + PREV_ROWS), shape(3 * R), shape(NB * R)),
        in_specs=smem(2) + vmem(4),
        out_specs=tuple(vmem(4)),
        scratch_shapes=[pltpu.VMEM((R, Y), jnp.int32)],
        compiler_params=params(16),
        name="first",
    )(stiffness, critical, u, v, lab, mask)
    rf = lax.ppermute(xf, "wx", [(i, i + 1) for i in range(nwx - 1)])
    rb = lax.ppermute(st, "wx", [(i + 1, i) for i in range(nwx - 1)])
    to_upper, to_lower = pl.pallas_call(
        pack_kernel,
        out_shape=(shape(YROWS), shape(YROWS)),
        in_specs=vmem(5),
        out_specs=tuple(vmem(2)),
        scratch_shapes=[pltpu.VMEM((len(CROSS) * R, Y), F32)],
        compiler_params=params(16),
        name="pack",
    )(st, rf, rb, v0, m)
    rl = lax.ppermute(to_upper, "ny", [(i, i + 1) for i in range(nny - 1)])
    ru = lax.ppermute(to_lower, "ny", [(i + 1, i) for i in range(nny - 1)])
    kc, hc, s, vel = pl.pallas_call(
        start_kernel,
        out_shape=(shape(2 * NB * BLOCK), shape(2 * NB * BLOCK), shape(3 * BLOCK), shape(3 * BLOCK)),
        in_specs=vmem(7),
        out_specs=tuple(vmem(4)),
        scratch_shapes=[
            pltpu.VMEM((5 * 7 * 3 * R, Y), F32),
            pltpu.VMEM((5 * 7 * (3 * R - 16), Y), F32),
            pltpu.VMEM((NB * 2 * R, Y), F32),
            pltpu.VMEM((NB * 2 * R, Y), F32),
        ],
        compiler_params=params(24),
        name="start",
    )(st, rf, rb, v0, m, rl, ru)
    near = [(i, i ^ 1) for i in range(nwx)]
    far = [(i, i + 1) for i in range(1, nwx - 1, 2)] + [(i + 1, i) for i in range(1, nwx - 1, 2)]
    for n in range(1, STEPS):
        last = n == STEPS - 1
        rb = lax.ppermute(s, "wx", far)
        ra = lax.ppermute(s, "wx", near)
        size = 3 * R if last else 3 * BLOCK
        s, vel = pl.pallas_call(
            functools.partial(step_kernel, last),
            out_shape=(shape(size), shape(size)),
            in_specs=vmem(6),
            out_specs=tuple(vmem(2)),
            scratch_shapes=[
                pltpu.VMEM((3 * 7 * 3 * R, Y), F32),
                pltpu.VMEM((3 * 7 * (3 * R - 16), Y), F32),
                pltpu.VMEM((3 * R, Y), F32),
                pltpu.VMEM((3 * R, Y), F32),
            ],
            compiler_params=params(16),
            name="last" if last else "middle",
        )(s, ra, rb, vel, kc, hc)
    back = lambda x: x.reshape(3, Z, X, Y).transpose(0, 2, 1, 3)
    return back(s), back(vel)


def solution(mesh):
    import functools

    wide = P(None, "wx", None, "ny")
    return jax.shard_map(
        functools.partial(on_device, mesh.shape["wx"], mesh.shape["ny"]),
        mesh=mesh,
        in_specs=(wide, wide, P("wx", None, "ny"), wide, P(), P()),
        out_specs=(wide, wide),
        check_vma=False,
    )
```

time: 183 us -> 86.9 us (0.47)
  the two profiles are of different devices: /device:TPU:32 before, /device:TPU:96 now
where the time goes in v1:
time: 86.9 us; the launch traced here: 86.4 us
  starting transfers between devices  44.9 us (52%)
  Pallas kernels  23.7 us (27%)
  waiting for transfers between devices  12.4 us (14%)
  local copies, waits for them, and re-layouts  4.66 us (5%)
    ppermute x2, starting transfers between devices, on_device(): rb = lax.ppermute(s, 'wx', far)  19.4 us
    pallas_call x1, Pallas kernels, on_device(): pl.pallas_call(start_kernel, out_shape=(shape(2 * NB * BLOCK), shape(2 *...  16.3 us
    ppermute x1, starting transfers between devices, on_device(): rb = lax.ppermute(st, 'wx', [(i + 1, i) for i in range(nwx - 1)])  11.8 us
    ppermute x1, starting transfers between devices, on_device(): rl = lax.ppermute(to_upper, 'ny', [(i, i + 1) for i in range(nny - 1)])  6.07 us
    pallas_call x2, Pallas kernels, on_device(): pl.pallas_call(functools.partial(step_kernel, last), out_shape=(shape(siz...  5.8 us
    ppermute x2, waiting for transfers between devices, on_device(): rb = lax.ppermute(s, 'wx', far)  4.68 us
    unnamed x12, local copies, waits for them, and re-layouts  4.66 us
    ppermute x2, starting transfers between devices, on_device(): ra = lax.ppermute(s, 'wx', near)  3.84 us
  transfers between devices with their start and end apart: 8, of which 6 were waited for; matrix products, arithmetic and copies ran while one was open for 0% of the time, Pallas kernels for 0%

profile of v1, /device:TPU:96, one launch (start us, length us, event | category | flops | bytes accessed | tf_op | source)
XLA Modules:
  0.0 86.4 jit_solution(4905747157532603275)
XLA Ops:
  0.6 0.0 copy-start
  0.6 1.1 %copy-done = s32[61,4,6,128]{3,1,2,0:T(4,128)S(1)} copy-done((s32[61,4,6,128]{3,1,2,0:T(4,128)S(1)}, s32[61,4,6,128]{3,1,2,0:T(4,128)}, u32[]{:S(2)}) %copy-start) | copy-done | bytes 749592
  1.8 0.0 copy-start.1
  1.8 0.8 copy-done.1
  2.5 0.0 copy-start.2
  2.5 0.8 copy-done.2
  3.3 0.0 copy-start.3
  3.3 0.7 copy-done.3
  4.0 0.0 copy-start.4
  4.0 0.7 copy-done.4
  4.7 0.0 copy-start.5
  4.7 0.7 copy-done.5
  5.3 0.9 %first.1 = (f32[120,128]{1,0:T(8,128)S(1)}, f32[544,128]{1,0:T(8,128)S(1)}, f32[72,128]{1,0:T(8,128)S(1)}, f32[1464,128]{1,0:T(8,128)S(1)}) custom-call(f32[8]{0:T(128)S(1)} %copy-done.4, f32[8]{0:T(128)S(1)} %copy-done.5, f32[72,128]{1,0:T(8,128)S(1)} %bitcast.19, f32[72,128]{1,0:T(8,128)S(1)} %bitcast.20, s32[24,128]{1,0:T(8,128)S(1)} %bitcast.21, ...), custom_call_target="tpu_custom_call" | custom-call | tf_op jit(solution)/shard_map/first/pallas_call | solution.py:351
  6.2 1.9 %collective-permute-start = (f32[544,128]{1,0:T(8,128)S(1)}, f32[544,128]{1,0:T(8,128)S(1)}, u32[]{:S(2)}, u32[]{:S(2)}) collective-permute-start(f32[544,128]{1,0:T(8,128)S(1)} %get-tuple-element.17), channel_id=1, source_target_pairs={{0,4},{4,8},{8,12},{12,16},{16,20},{20,24},{24,28},{28,32},{32,36}... | collective-permute-start | bytes 835592 | tf_op jit(solution)/shard_map/ppermute | solution.py:360
  8.1 11.8 %collective-permute-start.1 = (f32[120,128]{1,0:T(8,128)S(1)}, f32[120,128]{1,0:T(8,128)S(1)}, u32[]{:S(2)}, u32[]{:S(2)}) collective-permute-start(f32[120,128]{1,0:T(8,128)S(1)} %get-tuple-element.16.st), channel_id=1, source_target_pairs={{4,0},{8,4},{12,8},{16,12},{20,16},{24,20},{28,24},{32,28},{36,32}... | collective-permute-start | bytes 184328 | tf_op jit(solution)/shard_map/ppermute | solution.py:361
  19.9 1.8 %collective-permute-done.1.rb = f32[120,128]{1,0:T(8,128)S(1)} collective-permute-done((f32[120,128]{1,0:T(8,128)S(1)}, f32[120,128]{1,0:T(8,128)S(1)}, u32[]{:S(2)}, u32[]{:S(2)}) %collective-permute-start.1) | collective-permute-done | bytes 61472 | tf_op jit(solution)/shard_map/ppermute | solution.py:361
  21.7 0.5 collective-permute-done.rf
  22.2 0.8 pack.1
  23.0 6.1 %collective-permute-start.2 = (f32[256,128]{1,0:T(8,128)S(1)}, f32[256,128]{1,0:T(8,128)S(1)}, u32[]{:S(2)}, u32[]{:S(2)}) collective-permute-start(f32[256,128]{1,0:T(8,128)S(1)} %get-tuple-element.20), channel_id=1, source_target_pairs={{0,1},{1,2},{2,3},{4,5},{5,6},{6,7},{8,9},{9,10},{10,11},{12,13},{... | collective-permute-start | bytes 393224 | tf_op jit(solution)/shard_map/ppermute | solution.py:371
  29.1 1.9 %collective-permute-start.3 = (f32[256,128]{1,0:T(8,128)S(1)}, f32[256,128]{1,0:T(8,128)S(1)}, u32[]{:S(2)}, u32[]{:S(2)}) collective-permute-start(f32[256,128]{1,0:T(8,128)S(1)} %get-tuple-element.21), channel_id=1, source_target_pairs={{1,0},{2,1},{3,2},{5,4},{6,5},{7,6},{9,8},{10,9},{11,10},{13,12},{... | collective-permute-start | bytes 393224 | tf_op jit(solution)/shard_map/ppermute | solution.py:372
  31.0 1.9 %collective-permute-done.2.rl = f32[256,128]{1,0:T(8,128)S(1)} collective-permute-done((f32[256,128]{1,0:T(8,128)S(1)}, f32[256,128]{1,0:T(8,128)S(1)}, u32[]{:S(2)}, u32[]{:S(2)}) %collective-permute-start.2) | collective-permute-done | bytes 131104 | tf_op jit(solution)/shard_map/ppermute | solution.py:371
  32.9 3.4 %collective-permute-done.3.ru = f32[256,128]{1,0:T(8,128)S(1)} collective-permute-done((f32[256,128]{1,0:T(8,128)S(1)}, f32[256,128]{1,0:T(8,128)S(1)}, u32[]{:S(2)}, u32[]{:S(2)}) %collective-permute-start.3) | collective-permute-done | bytes 131104 | tf_op jit(solution)/shard_map/ppermute | solution.py:372
  36.3 16.3 %start.1 = (f32[3904,128]{1,0:T(8,128)S(1)}, f32[3904,128]{1,0:T(8,128)S(1)}, f32[96,128]{1,0:T(8,128)S(1)}, f32[96,128]{1,0:T(8,128)S(1)}) custom-call(f32[120,128]{1,0:T(8,128)S(1)} %get-tuple-element.16.st, f32[544,128]{1,0:T(8,128)S(1)} %collective-permute-done.rf, f32[120,128]{1,0:T(8,128)S(1)} %collective-permute-done.1.rb, ...), custom_call_target="tpu_custom_call" | custom-call | tf_op jit(solution)/shard_map/start/pallas_call | solution.py:373
  52.6 9.9 %collective-permute-start.5 = (f32[96,128]{1,0:T(8,128)S(1)}, f32[96,128]{1,0:T(8,128)S(1)}, u32[]{:S(2)}, u32[]{:S(2)}) collective-permute-start(f32[96,128]{1,0:T(8,128)S(1)} %get-tuple-element.22.s), channel_id=1, source_target_pairs={{4,8},{12,16},{20,24},{28,32},{36,40},{44,48},{52,56},{60,64},{68,... | collective-permute-start | bytes 147464 | tf_op jit(solution)/shard_map/ppermute | solution.py:391
  62.5 1.9 %collective-permute-start.4 = (f32[96,128]{1,0:T(8,128)S(1)}, f32[96,128]{1,0:T(8,128)S(1)}, u32[]{:S(2)}, u32[]{:S(2)}) collective-permute-start(f32[96,128]{1,0:T(8,128)S(1)} %get-tuple-element.22.s), channel_id=1, source_target_pairs={{0,4},{4,0},{8,12},{12,8},{16,20},{20,16},{24,28},{28,24},{32,36},... | collective-permute-start | bytes 147464 | tf_op jit(solution)/shard_map/ppermute | solution.py:392
  64.4 2.1 %collective-permute-done.5.rb = f32[96,128]{1,0:T(8,128)S(1)} collective-permute-done((f32[96,128]{1,0:T(8,128)S(1)}, f32[96,128]{1,0:T(8,128)S(1)}, u32[]{:S(2)}, u32[]{:S(2)}) %collective-permute-start.5) | collective-permute-done | bytes 49184 | tf_op jit(solution)/shard_map/ppermute | solution.py:391
  66.6 0.0 collective-permute-done.4.ra
  66.6 3.3 %middle.1 = (f32[96,128]{1,0:T(8,128)S(1)}, f32[96,128]{1,0:T(8,128)S(1)}) custom-call(f32[96,128]{1,0:T(8,128)S(1)} %get-tuple-element.22.s, f32[96,128]{1,0:T(8,128)S(1)} %collective-permute-done.4.ra, f32[96,128]{1,0:T(8,128)S(1)} %collective-permute-done.5.rb, f32[96,128]{1,0:T(8,128)S(1)} %get-tuple-element.23.v, f32[3904,128]{1,0:T(8,128)S(1)} %get-tuple-element.24.kc, ...), custom_call_target="tpu_custom_call" | custom-call | tf_op jit(solution)/shard_map/middle/pallas_call | solution.py:394
  69.9 9.5 %collective-permute-start.7 = (f32[96,128]{1,0:T(8,128)S(1)}, f32[96,128]{1,0:T(8,128)S(1)}, u32[]{:S(2)}, u32[]{:S(2)}) collective-permute-start(f32[96,128]{1,0:T(8,128)S(1)} %get-tuple-element.26.s), channel_id=1, source_target_pairs={{4,8},{12,16},{20,24},{28,32},{36,40},{44,48},{52,56},{60,64},{68,... | collective-permute-start | bytes 147464 | tf_op jit(solution)/shard_map/ppermute | solution.py:391
  79.4 1.9 %collective-permute-start.6 = (f32[96,128]{1,0:T(8,128)S(1)}, f32[96,128]{1,0:T(8,128)S(1)}, u32[]{:S(2)}, u32[]{:S(2)}) collective-permute-start(f32[96,128]{1,0:T(8,128)S(1)} %get-tuple-element.26.s), channel_id=1, source_target_pairs={{0,4},{4,0},{8,12},{12,8},{16,20},{20,16},{24,28},{28,24},{32,36},... | collective-permute-start | bytes 147464 | tf_op jit(solution)/shard_map/ppermute | solution.py:392
  81.3 2.6 %collective-permute-done.7.rb = f32[96,128]{1,0:T(8,128)S(1)} collective-permute-done((f32[96,128]{1,0:T(8,128)S(1)}, f32[96,128]{1,0:T(8,128)S(1)}, u32[]{:S(2)}, u32[]{:S(2)}) %collective-permute-start.7) | collective-permute-done | bytes 49184 | tf_op jit(solution)/shard_map/ppermute | solution.py:391
  83.9 0.0 collective-permute-done.6.ra
  83.9 2.5 %last.1 = (f32[72,128]{1,0:T(8,128)}, f32[72,128]{1,0:T(8,128)}) custom-call(f32[96,128]{1,0:T(8,128)S(1)} %get-tuple-element.26.s, f32[96,128]{1,0:T(8,128)S(1)} %collective-permute-done.6.ra, f32[96,128]{1,0:T(8,128)S(1)} %collective-permute-done.7.rb, f32[96,128]{1,0:T(8,128)S(1)} %get-tuple-element.27.v, f32[3904,128]{1,0:T(8,128)S(1)} %get-tuple-element.24.kc, ...), custom_call_target="tpu_custom_call" | custom-call | tf_op jit(solution)/shard_map/last/pallas_call | solution.py:394
Async XLA Ops:
  0.6 1.1 %copy-start = (s32[61,4,6,128]{3,1,2,0:T(4,128)S(1)}, s32[61,4,6,128]{3,1,2,0:T(4,128)}, u32[]{:S(2)}) copy-start(s32[61,4,6,128]{3,1,2,0:T(4,128)} %param.9) | copy-start | bytes 2248708
  1.8 0.8 copy-start.1
  2.5 0.8 copy-start.2
  3.3 0.7 copy-start.3
  4.0 0.7 copy-start.4
  4.7 0.7 copy-start.5
  6.2 16.0 %collective-permute-start = (f32[544,128]{1,0:T(8,128)S(1)}, f32[544,128]{1,0:T(8,128)S(1)}, u32[]{:S(2)}, u32[]{:S(2)}) collective-permute-start(f32[544,128]{1,0:T(8,128)S(1)} %get-tuple-element.17), channel_id=1, source_target_pairs={{0,4},{4,8},{8,12},{12,16},{16,20},{20,24},{24,28},{28,32},{32,36}... | collective-permute-start | bytes 835592 | tf_op jit(solution)/shard_map/ppermute | solution.py:360
  8.1 13.6 %collective-permute-start.1 = (f32[120,128]{1,0:T(8,128)S(1)}, f32[120,128]{1,0:T(8,128)S(1)}, u32[]{:S(2)}, u32[]{:S(2)}) collective-permute-start(f32[120,128]{1,0:T(8,128)S(1)} %get-tuple-element.16.st), channel_id=1, source_target_pairs={{4,0},{8,4},{12,8},{16,12},{20,16},{24,20},{28,24},{32,28},{36,32}... | collective-permute-start | bytes 184328 | tf_op jit(solution)/shard_map/ppermute | solution.py:361
  23.0 9.9 %collective-permute-start.2 = (f32[256,128]{1,0:T(8,128)S(1)}, f32[256,128]{1,0:T(8,128)S(1)}, u32[]{:S(2)}, u32[]{:S(2)}) collective-permute-start(f32[256,128]{1,0:T(8,128)S(1)} %get-tuple-element.20), channel_id=1, source_target_pairs={{0,1},{1,2},{2,3},{4,5},{5,6},{6,7},{8,9},{9,10},{10,11},{12,13},{... | collective-permute-start | bytes 393224 | tf_op jit(solution)/shard_map/ppermute | solution.py:371
  29.1 7.3 %collective-permute-start.3 = (f32[256,128]{1,0:T(8,128)S(1)}, f32[256,128]{1,0:T(8,128)S(1)}, u32[]{:S(2)}, u32[]{:S(2)}) collective-permute-start(f32[256,128]{1,0:T(8,128)S(1)} %get-tuple-element.21), channel_id=1, source_target_pairs={{1,0},{2,1},{3,2},{5,4},{6,5},{7,6},{9,8},{10,9},{11,10},{13,12},{... | collective-permute-start | bytes 393224 | tf_op jit(solution)/shard_map/ppermute | solution.py:372
  52.6 14.0 %collective-permute-start.5 = (f32[96,128]{1,0:T(8,128)S(1)}, f32[96,128]{1,0:T(8,128)S(1)}, u32[]{:S(2)}, u32[]{:S(2)}) collective-permute-start(f32[96,128]{1,0:T(8,128)S(1)} %get-tuple-element.22.s), channel_id=1, source_target_pairs={{4,8},{12,16},{20,24},{28,32},{36,40},{44,48},{52,56},{60,64},{68,... | collective-permute-start | bytes 147464 | tf_op jit(solution)/shard_map/ppermute | solution.py:391
  62.5 4.1 %collective-permute-start.4 = (f32[96,128]{1,0:T(8,128)S(1)}, f32[96,128]{1,0:T(8,128)S(1)}, u32[]{:S(2)}, u32[]{:S(2)}) collective-permute-start(f32[96,128]{1,0:T(8,128)S(1)} %get-tuple-element.22.s), channel_id=1, source_target_pairs={{0,4},{4,0},{8,12},{12,8},{16,20},{20,16},{24,28},{28,24},{32,36},... | collective-permute-start | bytes 147464 | tf_op jit(solution)/shard_map/ppermute | solution.py:392
  69.9 14.0 %collective-permute-start.7 = (f32[96,128]{1,0:T(8,128)S(1)}, f32[96,128]{1,0:T(8,128)S(1)}, u32[]{:S(2)}, u32[]{:S(2)}) collective-permute-start(f32[96,128]{1,0:T(8,128)S(1)} %get-tuple-element.26.s), channel_id=1, source_target_pairs={{4,8},{12,16},{20,24},{28,32},{36,40},{44,48},{52,56},{60,64},{68,... | collective-permute-start | bytes 147464 | tf_op jit(solution)/shard_map/ppermute | solution.py:391
  79.4 4.5 %collective-permute-start.6 = (f32[96,128]{1,0:T(8,128)S(1)}, f32[96,128]{1,0:T(8,128)S(1)}, u32[]{:S(2)}, u32[]{:S(2)}) collective-permute-start(f32[96,128]{1,0:T(8,128)S(1)} %get-tuple-element.26.s), channel_id=1, source_target_pairs={{0,4},{4,0},{8,12},{12,8},{16,20},{20,16},{24,28},{28,24},{32,36},... | collective-permute-start | bytes 147464 | tf_op jit(solution)/shard_map/ppermute | solution.py:392

commit v2 on v1

v2 whole, which is shorter than its diff:
```python
import functools
import math

import jax
import jax.numpy as jnp
from jax import lax
from jax.experimental import pallas as pl
from jax.experimental.pallas import tpu as pltpu
from jax.sharding import PartitionSpec as P


STEPS = 3
MATS = 8
DT = 0.05
X, Z, Y = 4, 6, 128
R = X * Z
W = 9
G = 42
SLOTS = 4
F32 = jnp.float32


def bond_offsets():
    out = []
    for a in range(0, 4):
        for b in range(-3, 4):
            for c in range(-3, 4):
                if a * a + b * b + c * c <= 9:
                    if a > 0 or (a == 0 and (b > 0 or (b == 0 and c > 0))):
                        out.append((a, b, c))
    return out


OFFS = bond_offsets()
NB = len(OFFS)
CROSS = [k for k in range(NB) if OFFS[k][0] > 0]


def rows_of(k):
    return OFFS[k][0] * Z + OFFS[k][1]


PREV_AT = {}
_at = 0
for _k in CROSS:
    PREV_AT[_k] = _at
    _at += rows_of(_k)
PREV_ROWS = -(-_at // 8) * 8
STATE0 = 5 * R
UNITS = 18 + 2 * NB
YROWS = -(-UNITS // SLOTS) * 8
EDGE = 8
BLOCK = R + EDGE


def lanes(rows):
    return lax.broadcasted_iota(jnp.int32, (rows, Y), 1)


def roll(x, shift):
    shift %= Y
    return x if shift == 0 else pltpu.roll(x, shift, axis=1)


def params(n):
    return pltpu.CompilerParams(vmem_limit_bytes=n << 20)


def vmem(n):
    return [pl.BlockSpec(memory_space=pltpu.VMEM)] * n


def shape(rows):
    return jax.ShapeDtypeStruct((rows, Y), F32)


def first_kernel(nwx, nny, *refs):
    given, (st, xf, v0, m_out), local, sems = refs[:6], refs[6:10], refs[10:16], refs[16]
    tmp = refs[17]
    copies = [pltpu.make_async_copy(g, l, sems.at[i]) for i, (g, l) in enumerate(zip(given, local))]
    for copy in copies:
        copy.start()
    stiff, crit, u, v, lab, mask = local
    wx, ny = lax.axis_index("wx"), lax.axis_index("ny")
    for copy in copies[:5]:
        copy.wait()
    for q in range(3):
        for x in range(X):
            st[q * R + x * Z : q * R + (x + 1) * Z, :] = u[pl.ds(q * R + x, Z, stride=X), :]
            v0[q * R + x * Z : q * R + (x + 1) * Z, :] = v[pl.ds(q * R + x, Z, stride=X), :]
    for x in range(X):
        tmp[x * Z : (x + 1) * Z, :] = lab[pl.ds(x, Z, stride=X), :]
    label = tmp[...]
    mod = jnp.zeros((R, Y), F32)
    lim = jnp.zeros((R, Y), F32)
    for t in range(MATS):
        hit = label == t
        mod = jnp.where(hit, stiff[t], mod)
        lim = jnp.where(hit, crit[t], lim)
    st[3 * R : 4 * R, :] = mod
    st[4 * R : 5 * R, :] = lim
    xf[0:STATE0, :] = st[...]
    row = lax.broadcasted_iota(jnp.int32, (R, Y), 0)
    zi = row % Z
    gx = wx * X + row // Z
    gy = ny * Y + lanes(R)
    copies[5].wait()
    for k, (a, b, c) in enumerate(OFFS):
        for x in range(X):
            m_out[k * R + x * Z : k * R + (x + 1) * Z, :] = mask[
                pl.ds(k * R + x, Z, stride=X), :
            ].astype(F32)
        ok = (zi + b >= 0) & (zi + b < Z) & (gx + a < nwx * X)
        if c:
            ok = ok & (gy + c >= 0) & (gy + c < nny * Y)
        m_out[k * R : (k + 1) * R, :] = jnp.where(ok, m_out[k * R : (k + 1) * R, :], 0.0)
        if a:
            o = rows_of(k)
            at = STATE0 + PREV_AT[k]
            xf[at : at + o, :] = m_out[(k + 1) * R - o : (k + 1) * R, :]
    if _at < PREV_ROWS:
        xf[STATE0 + _at : STATE0 + PREV_ROWS, :] = jnp.zeros((PREV_ROWS - _at, Y), F32)


def pack_kernel(st, rf, rb, v0, m, to_upper, to_lower, im):
    def unit(n):
        if n < 15:
            s, q = (n // 3, n % 3) if n < 9 else (n % 3, 3 + (n - 9) // 3)
            return (rf, st, rb)[s][q * R : (q + 1) * R, :]
        if n < 18:
            return v0[(n - 15) * R : (n - 14) * R, :]
        k = (n - 18) % NB
        if n < 18 + NB:
            return m[k * R : (k + 1) * R, :]
        o, at = rows_of(k), k * R
        if o == 0:
            im[at : at + R, :] = m[at : at + R, :]
        else:
            if OFFS[k][0]:
                im[at : at + o, :] = rf[STATE0 + PREV_AT[k] : STATE0 + PREV_AT[k] + o, :]
            else:
                im[at : at + o, :] = jnp.zeros((o, Y), F32)
            im[at + o : at + R, :] = m[at : at + R - o, :]
        return im[at : at + R, :]

    lane = lanes(8)
    for t in range(YROWS // 8):
        up = jnp.zeros((8, Y), F32)
        low = jnp.zeros((8, Y), F32)
        for p in range(SLOTS):
            if t * SLOTS + p >= UNITS:
                continue
            value = unit(t * SLOTS + p)
            for g in range(3):
                part = value[8 * g : 8 * g + 8, :]
                at = G * g + W * p
                here = (lane >= at) & (lane < at + W)
                up = jnp.where(here, roll(part, at + W), up)
                low = jnp.where(here, roll(part, at), low)
        to_upper[8 * t : 8 * t + 8, :] = up
        to_lower[8 * t : 8 * t + 8, :] = low


OWN = 6


def places():
    lane = lanes(8)
    return lane % G, lane < 3 * G


def tied(main, edge, with_edge=True):
    lane = lanes(8)
    rows = []
    for g in range(3):
        part = main[8 * g : 8 * g + 8, :]
        low = roll(edge, -(G * g + W))
        high = roll(edge, -(G * g + W + 2 * OWN))
        rows.append(jnp.where(lane < 3, low, jnp.where(lane >= Y - 3, high, part)))
    if with_edge:
        place, inside = places()
        for g in range(3):
            part = main[8 * g : 8 * g + 8, :]
            here = inside & (lane >= G * g) & (lane < G * (g + 1))
            low = here & (place >= W + 3) & (place < W + OWN)
            high = here & (place >= W + OWN) & (place < W + OWN + 3)
            edge = jnp.where(low, roll(part, G * g + W), edge)
            edge = jnp.where(high, roll(part, G * g + W + 2 * OWN), edge)
    return jnp.concatenate(rows, axis=0), edge


def shift_slabs(main, number, sh):
    rows = 3 * R
    for c in range(-3, 4):
        at = (number * 7 + c + 3) * rows
        sh[at : at + rows, :] = roll(main, -c)


def shift_edges(edges, number, qh):
    q = 3 * R - 16
    lane = lanes(8)
    tiles = []
    for n in range(q // 8):
        part = [roll(edges[(n + g) // 3], G * (g - (n + g) % 3)) for g in range(3)]
        tiles.append(jnp.where(lane < G, part[0], jnp.where(lane < 2 * G, part[1], part[2])))
    for c in range(-3, 4):
        at = (number * 7 + c + 3) * q
        for n, tile in enumerate(tiles):
            qh[at + 8 * n : at + 8 * n + 8, :] = roll(tile, -c)


def slab_at(number, o, c):
    return (number * 7 + c + 3) * 3 * R + R + o


def edge_at(number, o, c):
    return (number * 7 + c + 3) * (3 * R - 16) + R + o


DIRECTED = [(n // 2, 1 - 2 * (n % 2)) for n in range(2 * NB)]


def in_parts(live, size, fn):
    for start in range(0, 2 * NB, size):
        pl.when(live)(functools.partial(fn, range(start, min(start + size, 2 * NB))))


def add_forces(numbers, here, shifted, at_of, rows, kc, hc, acc):
    total = [acc[q * rows : (q + 1) * rows, :] for q in range(3)]
    mine = [here[q] for q in range(3)]
    for n in numbers:
        k, sign = DIRECTED[n]
        a, b, c = OFFS[k]
        length = math.sqrt(a * a + b * b + c * c)
        d = (sign * a, sign * b, sign * c)
        e = []
        for q in range(3):
            at = at_of(q, sign * rows_of(k), d[2])
            there = shifted[at : at + rows, :]
            e.append(there + float(d[q]) - mine[q] if d[q] else there - mine[q])
        sq = e[0] * e[0] + e[1] * e[1] + e[2] * e[2]
        t = sq * lax.rsqrt(jnp.maximum(sq, 1e-36)) - length
        mag = kc[n * rows : (n + 1) * rows, :] * t / (hc[n * rows : (n + 1) * rows, :] + t * t)
        total = [total[q] + mag * e[q] for q in range(3)]
    for q in range(3):
        acc[q * rows : (q + 1) * rows, :] = total[q]


def coefficients(mask, m_i, m_j, l_i, l_j, length):
    half = 0.5 * (l_i + l_j)
    sq = half * half
    return mask * (2.0 * m_i * m_j / (m_i + m_j)) * sq * (1.0 / length), sq * (length * length)


def length_of(k):
    a, b, c = OFFS[k]
    return math.sqrt(a * a + b * b + c * c)


def filled(x):
    return jnp.where(x > 0.0, x, 1.0)


PART = 16
PART_EDGE = 64


def slab_kernel(nwx, st, rf, rb, v0, m, im, kc, hc, u1, v1, sh, acc):
    live = lax.axis_index("wx") < nwx
    for q in range(5):
        at = q * R
        main = jnp.concatenate([rf[at : at + R, :], st[at : at + R, :], rb[at : at + R, :]], axis=0)
        shift_slabs(filled(main) if q >= 3 else main, q, sh)
    acc[...] = jnp.zeros_like(acc)

    def part(numbers):
        mod, lim = st[3 * R : 4 * R, :], st[4 * R : 5 * R, :]
        for n in numbers:
            k, sign = DIRECTED[n]
            o, c = sign * rows_of(k), sign * OFFS[k][2]
            mask = m[k * R : (k + 1) * R, :] if sign > 0 else roll(im[k * R : (k + 1) * R, :], -c)
            mj, lj = (sh[slab_at(q, o, c) : slab_at(q, o, c) + R, :] for q in (3, 4))
            kk, hh = coefficients(mask, mod, mj, lim, lj, length_of(k))
            kc[n * R : (n + 1) * R, :] = kk
            hc[n * R : (n + 1) * R, :] = hh
        here = [st[q * R : (q + 1) * R, :] for q in range(3)]
        add_forces(numbers, here, sh, slab_at, R, kc, hc, acc)

    in_parts(live, PART, part)
    vel = v0[...] + DT * acc[...]
    v1[...] = vel
    u1[...] = st[0 : 3 * R, :] + DT * vel


def edge_kernel(nwx, rl, ru, mine_up, mine_low, u1, v1, kc, hc, s_out, v_out, qh, acc, ue):
    live = lax.axis_index("wx") < nwx
    place, inside = places()

    def edge(n):
        t, p = n // SLOTS, n % SLOTS
        at = slice(8 * t, 8 * t + 8)
        out = jnp.where(inside & (place < W), roll(rl[at, :], -W * p), 0.0)
        own = roll(mine_low[at, :], W - W * p)
        out = jnp.where(inside & (place >= W) & (place < W + OWN), own, out)
        own = roll(mine_up[at, :], 2 * OWN - W * p)
        out = jnp.where(inside & (place >= W + OWN) & (place < W + 2 * OWN), own, out)
        above = roll(ru[at, :], W + 2 * OWN - W * p)
        return jnp.where(
            inside & (place >= W + 2 * OWN) & (place < 2 * W + 2 * OWN), above, out
        )

    for q in range(5):
        tiles = [edge(s * 3 + q) if q < 3 else edge(9 + 3 * (q - 3) + s) for s in range(3)]
        if q >= 3:
            tiles = [filled(x) for x in tiles]
        ue[8 * q : 8 * q + 8, :] = tiles[1]
        shift_edges(tiles, q, qh)
    acc[...] = jnp.zeros_like(acc)

    def part(numbers):
        mod, lim = ue[24:32, :], ue[32:40, :]
        for n in numbers:
            k, sign = DIRECTED[n]
            o, c = sign * rows_of(k), sign * OFFS[k][2]
            mask = edge(18 + k) if sign > 0 else roll(edge(18 + NB + k), -c)
            mj, lj = (qh[edge_at(q, o, c) : edge_at(q, o, c) + EDGE, :] for q in (3, 4))
            kk, hh = coefficients(mask, mod, mj, lim, lj, length_of(k))
            kc[n * EDGE : (n + 1) * EDGE, :] = kk
            hc[n * EDGE : (n + 1) * EDGE, :] = hh
        here = [ue[q * EDGE : (q + 1) * EDGE, :] for q in range(3)]
        add_forces(numbers, here, qh, edge_at, EDGE, kc, hc, acc)

    in_parts(live, PART_EDGE // 2, part)
    for q in range(3):
        vel = edge(15 + q) + DT * acc[q * EDGE : (q + 1) * EDGE, :]
        dis = ue[q * EDGE : (q + 1) * EDGE, :] + DT * vel
        finish(q, u1[q * R : (q + 1) * R, :], dis, v1[q * R : (q + 1) * R, :], vel, s_out, v_out)


def finish(q, dis, dis_e, vel, vel_e, s_out, v_out):
    dis, dis_e = tied(dis, dis_e)
    at = q * BLOCK
    s_out[at : at + R, :] = dis
    s_out[at + R : at + BLOCK, :] = dis_e
    v_out[at : at + R, :] = vel
    v_out[at + R : at + BLOCK, :] = vel_e


def step_kernel(nwx, last, s, ra, rb, v, kc, hc, ke, he, s_out, v_out, sh, qh, acc, acc_e):
    wx = lax.axis_index("wx")
    live = wx < nwx
    even = lax.rem(wx, 2) == 0
    for q in range(3):
        at = q * BLOCK
        top = jnp.where(even, rb[at : at + BLOCK, :], ra[at : at + BLOCK, :])
        end = jnp.where(even, ra[at : at + BLOCK, :], rb[at : at + BLOCK, :])
        mid = s[at : at + BLOCK, :]
        shift_slabs(jnp.concatenate([top[:R], mid[:R], end[:R]], axis=0), q, sh)
        shift_edges([top[R:], mid[R:], end[R:]], q, qh)
    acc[...] = jnp.zeros_like(acc)
    acc_e[...] = jnp.zeros_like(acc_e)
    u_main = [s[q * BLOCK : q * BLOCK + R, :] for q in range(3)]
    u_edge = [s[q * BLOCK + R : (q + 1) * BLOCK, :] for q in range(3)]

    def slab_part(numbers):
        here = [s[q * BLOCK : q * BLOCK + R, :] for q in range(3)]
        add_forces(numbers, here, sh, slab_at, R, kc, hc, acc)

    def edge_part(numbers):
        here = [s[q * BLOCK + R : (q + 1) * BLOCK, :] for q in range(3)]
        add_forces(numbers, here, qh, edge_at, EDGE, ke, he, acc_e)

    in_parts(live, PART, slab_part)
    in_parts(live, PART_EDGE, edge_part)
    for q in range(3):
        at = q * BLOCK
        vel = v[at : at + R, :] + DT * acc[q * R : (q + 1) * R, :]
        dis = u_main[q] + DT * vel
        vel_e = v[at + R : at + BLOCK, :] + DT * acc_e[q * EDGE : (q + 1) * EDGE, :]
        dis_e = u_edge[q] + DT * vel_e
        if not last:
            finish(q, dis, dis_e, vel, vel_e, s_out, v_out)
            continue
        acc[q * R : (q + 1) * R, :] = tied(dis, dis_e, False)[0]
        for x in range(X):
            s_out[pl.ds(q * R + x, Z, stride=X), :] = acc[q * R + x * Z : q * R + (x + 1) * Z, :]
        sh[q * R : (q + 1) * R, :] = tied(vel, vel_e, False)[0]
        for x in range(X):
            v_out[pl.ds(q * R + x, Z, stride=X), :] = sh[q * R + x * Z : q * R + (x + 1) * Z, :]


def call(kernel, outs, specs, scratch, mib, args, flops=0):
    return pl.pallas_call(
        kernel,
        out_shape=tuple(shape(n) for n in outs),
        in_specs=specs,
        out_specs=tuple(vmem(len(outs))),
        scratch_shapes=scratch,
        compiler_params=params(mib),
        cost_estimate=pl.CostEstimate(flops=flops, bytes_accessed=0, transcendentals=0),
    )(*args)


def tall(rows, dtype=F32):
    return pltpu.VMEM((rows, Y), dtype)


def on_device(nwx, nny, displacement, velocity, labels, bond_mask, stiffness, critical):
    flat = lambda x: x.transpose(0, 2, 1, 3).reshape(-1, Y)
    u, v, mask = flat(displacement), flat(velocity), flat(bond_mask)
    lab = labels.transpose(1, 0, 2).reshape(R, Y)
    sh3, qh3 = 7 * 3 * R, 7 * (3 * R - 16)
    i32 = jnp.int32
    st, xf, v0, m = call(
        functools.partial(first_kernel, nwx, nny),
        (STATE0, STATE0 + PREV_ROWS, 3 * R, NB * R),
        [pl.BlockSpec(memory_space=pltpu.HBM)] * 6,
        [pltpu.SMEM((MATS,), F32), pltpu.SMEM((MATS,), F32), tall(3 * R), tall(3 * R),
         tall(R, i32), tall(NB * R, i32), pltpu.SemaphoreType.DMA((6,)), tall(R, i32)],
        16, tuple(pltpu.with_memory_space_constraint(x, pltpu.HBM) for x in (stiffness, critical, u, v, lab, mask)),
    )
    rf = lax.ppermute(xf, "wx", [(i, i + 1) for i in range(nwx - 1)])
    rb = lax.ppermute(st, "wx", [(i + 1, i) for i in range(nwx - 1)])
    to_upper, to_lower, im = call(
        pack_kernel, (YROWS, YROWS, NB * R), vmem(5), [], 16, (st, rf, rb, v0, m)
    )
    rl = lax.ppermute(to_upper, "ny", [(i, i + 1) for i in range(nny - 1)])
    ru = lax.ppermute(to_lower, "ny", [(i + 1, i) for i in range(nny - 1)])
    kc, hc, u1, v1 = call(
        functools.partial(slab_kernel, nwx),
        (2 * NB * R, 2 * NB * R, 3 * R, 3 * R), vmem(6), [tall(5 * sh3), tall(3 * R)],
        24, (st, rf, rb, v0, m, im), 50_000_000,
    )
    ke, he, s, vel = call(
        functools.partial(edge_kernel, nwx),
        (2 * NB * EDGE, 2 * NB * EDGE, 3 * BLOCK, 3 * BLOCK), vmem(6),
        [tall(5 * qh3), tall(3 * EDGE), tall(5 * EDGE)],
        16, (rl, ru, to_upper, to_lower, u1, v1),
    )
    near = [(i, i ^ 1) for i in range(nwx)]
    far = [(i, i + 1) for i in range(1, nwx - 1, 2)] + [(i + 1, i) for i in range(1, nwx - 1, 2)]
    for n in range(1, STEPS):
        last = n == STEPS - 1
        rb = lax.ppermute(s, "wx", far)
        ra = lax.ppermute(s, "wx", near)
        size = 3 * R if last else 3 * BLOCK
        s, vel = call(
            functools.partial(step_kernel, nwx, last),
            (size, size), vmem(8),
            [tall(3 * sh3), tall(3 * qh3), tall(3 * R), tall(3 * EDGE)],
            16, (s, ra, rb, vel, kc, hc, ke, he),
        )
    back = lambda x: x.reshape(3, Z, X, Y).transpose(0, 2, 1, 3)
    return back(s), back(vel)


def solution(mesh):
    wide = P(None, "wx", None, "ny")
    return jax.shard_map(
        functools.partial(on_device, mesh.shape["wx"], mesh.shape["ny"]),
        mesh=mesh,
        in_specs=(wide, wide, P("wx", None, "ny"), wide, P(), P()),
        out_specs=(wide, wide),
        check_vma=False,
    )
```

time: 86.9 us -> 74.6 us (0.86)
  the two profiles are of different devices: /device:TPU:96 before, /device:TPU:32 now
where the time goes in v2:
time: 74.6 us; the launch traced here: 74.3 us
  starting transfers between devices  40.6 us (54%)
  waiting for transfers between devices  19.1 us (26%)
  Pallas kernels  13.7 us (18%)
  between operations  0.75 us (1%)
    ppermute x2, starting transfers between devices, on_device(): rb = lax.ppermute(s, 'wx', far)  18.5 us
    pallas_call x6, Pallas kernels, call(): pl.pallas_call(kernel, out_shape=tuple((shape(n) for n in outs)), in_spec...  13.7 us
    ppermute x1, starting transfers between devices, on_device(): rb = lax.ppermute(st, 'wx', [(i + 1, i) for i in range(nwx - 1)])  12.4 us
    ppermute x2, waiting for transfers between devices, on_device(): rb = lax.ppermute(s, 'wx', far)  8.92 us
    ppermute x1, waiting for transfers between devices, on_device(): ru = lax.ppermute(to_lower, 'ny', [(i + 1, i) for i in range(nny - 1)])  5.67 us
    ppermute x2, starting transfers between devices, on_device(): ra = lax.ppermute(s, 'wx', near)  5.05 us
    ppermute x1, waiting for transfers between devices, on_device(): rf = lax.ppermute(xf, 'wx', [(i, i + 1) for i in range(nwx - 1)])  2.68 us
    ppermute x1, starting transfers between devices, on_device(): rf = lax.ppermute(xf, 'wx', [(i, i + 1) for i in range(nwx - 1)])  1.92 us
  transfers between devices with their start and end apart: 8, of which 5 were waited for; matrix products, arithmetic and copies ran while one was open for 0% of the time, Pallas kernels for 3%

profile of v2, /device:TPU:32, one launch (start us, length us, event | category | flops | bytes accessed | tf_op | source)
XLA Modules:
  0.0 74.3 jit_solution(2720099956298427068)
XLA Ops:
  0.6 1.5 %shard_map.77 = (f32[120,128]{1,0:T(8,128)S(1)}, f32[544,128]{1,0:T(8,128)S(1)}, f32[72,128]{1,0:T(8,128)S(1)}, f32[1464,128]{1,0:T(8,128)S(1)}) custom-call(f32[8]{0:T(128)} %refs_0_.1, f32[8]{0:T(128)} %refs_1_.1, f32[72,128]{1,0:T(8,128)} %bitcast.19, f32[72,128]{1,0:T(8,128)} %bitcast.20, s32[24,128]{1,0:T(8,128)} %bitcast.21, s32[1464,128]{1,0:T(8,128)} %bitcast.18), custom_call_target="tpu_custom_call" | custom-call | tf_op jit(solution)/shard_map/pallas_call | solution.py:393
  2.2 1.9 %collective-permute-start = (f32[544,128]{1,0:T(8,128)S(1)}, f32[544,128]{1,0:T(8,128)S(1)}, u32[]{:S(2)}, u32[]{:S(2)}) collective-permute-start(f32[544,128]{1,0:T(8,128)S(1)} %get-tuple-element.22), channel_id=1, source_target_pairs={{0,4},{4,8},{8,12},{12,16},{16,20},{20,24},{24,28},{28,32},{32,36}... | collective-permute-start | bytes 835592 | tf_op jit(solution)/shard_map/ppermute | solution.py:422
  4.1 12.4 %collective-permute-start.1 = (f32[120,128]{1,0:T(8,128)S(1)}, f32[120,128]{1,0:T(8,128)S(1)}, u32[]{:S(2)}, u32[]{:S(2)}) collective-permute-start(f32[120,128]{1,0:T(8,128)S(1)} %get-tuple-element.21.st), channel_id=1, source_target_pairs={{4,0},{8,4},{12,8},{16,12},{20,16},{24,20},{28,24},{32,28},{36,32}... | collective-permute-start | bytes 184328 | tf_op jit(solution)/shard_map/ppermute | solution.py:423
  16.5 1.8 %collective-permute-done.1.rb = f32[120,128]{1,0:T(8,128)S(1)} collective-permute-done((f32[120,128]{1,0:T(8,128)S(1)}, f32[120,128]{1,0:T(8,128)S(1)}, u32[]{:S(2)}, u32[]{:S(2)}) %collective-permute-start.1) | collective-permute-done | bytes 61472 | tf_op jit(solution)/shard_map/ppermute | solution.py:423
  18.4 2.7 %collective-permute-done.rf = f32[544,128]{1,0:T(8,128)S(1)} collective-permute-done((f32[544,128]{1,0:T(8,128)S(1)}, f32[544,128]{1,0:T(8,128)S(1)}, u32[]{:S(2)}, u32[]{:S(2)}) %collective-permute-start) | collective-permute-done | bytes 278560 | tf_op jit(solution)/shard_map/ppermute | solution.py:422
  21.1 0.9 %shard_map.78 = (f32[280,128]{1,0:T(8,128)S(1)}, f32[280,128]{1,0:T(8,128)S(1)}, f32[1464,128]{1,0:T(8,128)S(1)}) custom-call(f32[120,128]{1,0:T(8,128)S(1)} %get-tuple-element.21.st, f32[544,128]{1,0:T(8,128)S(1)} %collective-permute-done.rf, f32[120,128]{1,0:T(8,128)S(1)} %collective-permute-done.1.rb, f32[72,128]{1,0:T(8,128)S(1)} %get-tuple-element.23.v0, ...), custom_call_target="tpu_custom_call" | custom-call | tf_op jit(solution)/shard_map/pallas_call | solution.py:393
  22.0 1.4 %collective-permute-start.2 = (f32[280,128]{1,0:T(8,128)S(1)}, f32[280,128]{1,0:T(8,128)S(1)}, u32[]{:S(2)}, u32[]{:S(2)}) collective-permute-start(f32[280,128]{1,0:T(8,128)S(1)} %get-tuple-element.25.mine_up), channel_id=1, source_target_pairs={{0,1},{1,2},{2,3},{4,5},{5,6},{6,7},{8,9},{9,10},{10,11},{12,13},{... | collective-permute-start | bytes 430088 | tf_op jit(solution)/shard_map/ppermute | solution.py:427
  23.4 1.3 %collective-permute-start.3 = (f32[280,128]{1,0:T(8,128)S(1)}, f32[280,128]{1,0:T(8,128)S(1)}, u32[]{:S(2)}, u32[]{:S(2)}) collective-permute-start(f32[280,128]{1,0:T(8,128)S(1)} %get-tuple-element.26.mine_low), channel_id=1, source_target_pairs={{1,0},{2,1},{3,2},{5,4},{6,5},{7,6},{9,8},{10,9},{11,10},{13,12},{... | collective-permute-start | bytes 430088 | tf_op jit(solution)/shard_map/ppermute | solution.py:428
  24.7 2.3 %shard_map.79 = (f32[2928,128]{1,0:T(8,128)S(1)}, f32[2928,128]{1,0:T(8,128)S(1)}, f32[72,128]{1,0:T(8,128)S(1)}, f32[72,128]{1,0:T(8,128)S(1)}) custom-call(f32[120,128]{1,0:T(8,128)S(1)} %get-tuple-element.21.st, f32[544,128]{1,0:T(8,128)S(1)} %collective-permute-done.rf, f32[120,128]{1,0:T(8,128)S(1)} %collective-permute-done.1.rb, ...), custom_call_target="tpu_custom_call" | custom-call | flops 50000000 | tf_op jit(solution)/shard_map/pallas_call | solution.py:393
  27.0 0.0 collective-permute-done.2.rl
  27.0 5.7 %collective-permute-done.3.ru = f32[280,128]{1,0:T(8,128)S(1)} collective-permute-done((f32[280,128]{1,0:T(8,128)S(1)}, f32[280,128]{1,0:T(8,128)S(1)}, u32[]{:S(2)}, u32[]{:S(2)}) %collective-permute-start.3) | collective-permute-done | bytes 143392 | tf_op jit(solution)/shard_map/ppermute | solution.py:428
  32.7 3.5 %shard_map.80 = (f32[976,128]{1,0:T(8,128)S(1)}, f32[976,128]{1,0:T(8,128)S(1)}, f32[96,128]{1,0:T(8,128)S(1)}, f32[96,128]{1,0:T(8,128)S(1)}) custom-call(f32[280,128]{1,0:T(8,128)S(1)} %collective-permute-done.2.rl, f32[280,128]{1,0:T(8,128)S(1)} %collective-permute-done.3.ru, f32[280,128]{1,0:T(8,128)S(1)} %get-tuple-element.25.mine_up, ...), custom_call_target="tpu_custom_call" | custom-call | tf_op jit(solution)/shard_map/pallas_call | solution.py:393
  36.2 3.1 %collective-permute-start.4 = (f32[96,128]{1,0:T(8,128)S(1)}, f32[96,128]{1,0:T(8,128)S(1)}, u32[]{:S(2)}, u32[]{:S(2)}) collective-permute-start(f32[96,128]{1,0:T(8,128)S(1)} %get-tuple-element.30.s), channel_id=1, source_target_pairs={{0,4},{4,0},{8,12},{12,8},{16,20},{20,16},{24,28},{28,24},{32,36},... | collective-permute-start | bytes 147464 | tf_op jit(solution)/shard_map/ppermute | solution.py:445
  39.4 9.3 %collective-permute-start.5 = (f32[96,128]{1,0:T(8,128)S(1)}, f32[96,128]{1,0:T(8,128)S(1)}, u32[]{:S(2)}, u32[]{:S(2)}) collective-permute-start(f32[96,128]{1,0:T(8,128)S(1)} %get-tuple-element.30.s), channel_id=1, source_target_pairs={{4,8},{12,16},{20,24},{28,32},{36,40},{44,48},{52,56},{60,64},{68,... | collective-permute-start | bytes 147464 | tf_op jit(solution)/shard_map/ppermute | solution.py:444
  48.6 0.0 collective-permute-done.4.ra
  48.6 4.3 %collective-permute-done.5.rb = f32[96,128]{1,0:T(8,128)S(1)} collective-permute-done((f32[96,128]{1,0:T(8,128)S(1)}, f32[96,128]{1,0:T(8,128)S(1)}, u32[]{:S(2)}, u32[]{:S(2)}) %collective-permute-start.5) | collective-permute-done | bytes 49184 | tf_op jit(solution)/shard_map/ppermute | solution.py:444
  52.9 2.4 %shard_map.81 = (f32[96,128]{1,0:T(8,128)S(1)}, f32[96,128]{1,0:T(8,128)S(1)}) custom-call(f32[96,128]{1,0:T(8,128)S(1)} %get-tuple-element.30.s, f32[96,128]{1,0:T(8,128)S(1)} %collective-permute-done.4.ra, f32[96,128]{1,0:T(8,128)S(1)} %collective-permute-done.5.rb, f32[96,128]{1,0:T(8,128)S(1)} %get-tuple-element.31.v, ...), custom_call_target="tpu_custom_call" | custom-call | tf_op jit(solution)/shard_map/pallas_call | solution.py:393
  55.3 1.9 %collective-permute-start.6 = (f32[96,128]{1,0:T(8,128)S(1)}, f32[96,128]{1,0:T(8,128)S(1)}, u32[]{:S(2)}, u32[]{:S(2)}) collective-permute-start(f32[96,128]{1,0:T(8,128)S(1)} %get-tuple-element.36.s), channel_id=1, source_target_pairs={{0,4},{4,0},{8,12},{12,8},{16,20},{20,16},{24,28},{28,24},{32,36},... | collective-permute-start | bytes 147464 | tf_op jit(solution)/shard_map/ppermute | solution.py:445
  57.3 9.3 %collective-permute-start.7 = (f32[96,128]{1,0:T(8,128)S(1)}, f32[96,128]{1,0:T(8,128)S(1)}, u32[]{:S(2)}, u32[]{:S(2)}) collective-permute-start(f32[96,128]{1,0:T(8,128)S(1)} %get-tuple-element.36.s), channel_id=1, source_target_pairs={{4,8},{12,16},{20,24},{28,32},{36,40},{44,48},{52,56},{60,64},{68,... | collective-permute-start | bytes 147464 | tf_op jit(solution)/shard_map/ppermute | solution.py:444
  66.5 0.0 collective-permute-done.6.ra
  66.5 4.7 %collective-permute-done.7.rb = f32[96,128]{1,0:T(8,128)S(1)} collective-permute-done((f32[96,128]{1,0:T(8,128)S(1)}, f32[96,128]{1,0:T(8,128)S(1)}, u32[]{:S(2)}, u32[]{:S(2)}) %collective-permute-start.7) | collective-permute-done | bytes 49184 | tf_op jit(solution)/shard_map/ppermute | solution.py:444
  71.2 3.0 %shard_map.82 = (f32[72,128]{1,0:T(8,128)}, f32[72,128]{1,0:T(8,128)}) custom-call(f32[96,128]{1,0:T(8,128)S(1)} %get-tuple-element.36.s, f32[96,128]{1,0:T(8,128)S(1)} %collective-permute-done.6.ra, f32[96,128]{1,0:T(8,128)S(1)} %collective-permute-done.7.rb, f32[96,128]{1,0:T(8,128)S(1)} %get-tuple-element.37.v, f32[2928,128]{1,0:T(8,128)S(1)} %get-tuple-element.32.kc, ...), custom_call_target="tpu_custom_call" | custom-call | tf_op jit(solution)/shard_map/pallas_call | solution.py:393
Async XLA Ops:
  2.2 18.9 %collective-permute-start = (f32[544,128]{1,0:T(8,128)S(1)}, f32[544,128]{1,0:T(8,128)S(1)}, u32[]{:S(2)}, u32[]{:S(2)}) collective-permute-start(f32[544,128]{1,0:T(8,128)S(1)} %get-tuple-element.22), channel_id=1, source_target_pairs={{0,4},{4,8},{8,12},{12,16},{16,20},{20,24},{24,28},{28,32},{32,36}... | collective-permute-start | bytes 835592 | tf_op jit(solution)/shard_map/ppermute | solution.py:422
  4.1 14.3 %collective-permute-start.1 = (f32[120,128]{1,0:T(8,128)S(1)}, f32[120,128]{1,0:T(8,128)S(1)}, u32[]{:S(2)}, u32[]{:S(2)}) collective-permute-start(f32[120,128]{1,0:T(8,128)S(1)} %get-tuple-element.21.st), channel_id=1, source_target_pairs={{4,0},{8,4},{12,8},{16,12},{20,16},{24,20},{28,24},{32,28},{36,32}... | collective-permute-start | bytes 184328 | tf_op jit(solution)/shard_map/ppermute | solution.py:423
  22.0 5.0 %collective-permute-start.2 = (f32[280,128]{1,0:T(8,128)S(1)}, f32[280,128]{1,0:T(8,128)S(1)}, u32[]{:S(2)}, u32[]{:S(2)}) collective-permute-start(f32[280,128]{1,0:T(8,128)S(1)} %get-tuple-element.25.mine_up), channel_id=1, source_target_pairs={{0,1},{1,2},{2,3},{4,5},{5,6},{6,7},{8,9},{9,10},{10,11},{12,13},{... | collective-permute-start | bytes 430088 | tf_op jit(solution)/shard_map/ppermute | solution.py:427
  23.4 9.3 %collective-permute-start.3 = (f32[280,128]{1,0:T(8,128)S(1)}, f32[280,128]{1,0:T(8,128)S(1)}, u32[]{:S(2)}, u32[]{:S(2)}) collective-permute-start(f32[280,128]{1,0:T(8,128)S(1)} %get-tuple-element.26.mine_low), channel_id=1, source_target_pairs={{1,0},{2,1},{3,2},{5,4},{6,5},{7,6},{9,8},{10,9},{11,10},{13,12},{... | collective-permute-start | bytes 430088 | tf_op jit(solution)/shard_map/ppermute | solution.py:428
  36.2 12.4 %collective-permute-start.4 = (f32[96,128]{1,0:T(8,128)S(1)}, f32[96,128]{1,0:T(8,128)S(1)}, u32[]{:S(2)}, u32[]{:S(2)}) collective-permute-start(f32[96,128]{1,0:T(8,128)S(1)} %get-tuple-element.30.s), channel_id=1, source_target_pairs={{0,4},{4,0},{8,12},{12,8},{16,20},{20,16},{24,28},{28,24},{32,36},... | collective-permute-start | bytes 147464 | tf_op jit(solution)/shard_map/ppermute | solution.py:445
  39.4 13.5 %collective-permute-start.5 = (f32[96,128]{1,0:T(8,128)S(1)}, f32[96,128]{1,0:T(8,128)S(1)}, u32[]{:S(2)}, u32[]{:S(2)}) collective-permute-start(f32[96,128]{1,0:T(8,128)S(1)} %get-tuple-element.30.s), channel_id=1, source_target_pairs={{4,8},{12,16},{20,24},{28,32},{36,40},{44,48},{52,56},{60,64},{68,... | collective-permute-start | bytes 147464 | tf_op jit(solution)/shard_map/ppermute | solution.py:444
  55.3 11.2 %collective-permute-start.6 = (f32[96,128]{1,0:T(8,128)S(1)}, f32[96,128]{1,0:T(8,128)S(1)}, u32[]{:S(2)}, u32[]{:S(2)}) collective-permute-start(f32[96,128]{1,0:T(8,128)S(1)} %get-tuple-element.36.s), channel_id=1, source_target_pairs={{0,4},{4,0},{8,12},{12,8},{16,20},{20,16},{24,28},{28,24},{32,36},... | collective-permute-start | bytes 147464 | tf_op jit(solution)/shard_map/ppermute | solution.py:445
  57.3 13.9 %collective-permute-start.7 = (f32[96,128]{1,0:T(8,128)S(1)}, f32[96,128]{1,0:T(8,128)S(1)}, u32[]{:S(2)}, u32[]{:S(2)}) collective-permute-start(f32[96,128]{1,0:T(8,128)S(1)} %get-tuple-element.36.s), channel_id=1, source_target_pairs={{4,8},{12,16},{20,24},{28,32},{36,40},{44,48},{52,56},{60,64},{68,... | collective-permute-start | bytes 147464 | tf_op jit(solution)/shard_map/ppermute | solution.py:444

commit v3 on v2

--- a/solution.py
+++ b/solution.py
@@ -47,8 +47,9 @@
     _at += rows_of(_k)
 PREV_ROWS = -(-_at // 8) * 8
 STATE0 = 5 * R
-UNITS = 18 + 2 * NB
-YROWS = -(-UNITS // SLOTS) * 8
+UNITS_OWN = 8 + NB
+UNITS_NEXT = 10 + NB
+YROWS = -(-UNITS_NEXT // SLOTS) * 8
 EDGE = 8
 BLOCK = R + EDGE
 
@@ -122,16 +123,42 @@
         xf[STATE0 + _at : STATE0 + PREV_ROWS, :] = jnp.zeros((PREV_ROWS - _at, Y), F32)
 
 
-def pack_kernel(st, rf, rb, v0, m, to_upper, to_lower, im):
+def pack_units(unit, units, to_upper, to_lower):
+    lane = lanes(8)
+    for t in range(YROWS // 8):
+        up = jnp.zeros((8, Y), F32)
+        low = jnp.zeros((8, Y), F32)
+        for p in range(SLOTS):
+            if t * SLOTS + p >= units:
+                continue
+            value = unit(t * SLOTS + p)
+            for g in range(3):
+                part = value[8 * g : 8 * g + 8, :]
+                at = G * g + W * p
+                here = (lane >= at) & (lane < at + W)
+                up = jnp.where(here, roll(part, at + W), up)
+                low = jnp.where(here, roll(part, at), low)
+        to_upper[8 * t : 8 * t + 8, :] = up
+        to_lower[8 * t : 8 * t + 8, :] = low
+
+
+def pack_own_kernel(st, v0, m, to_upper, to_lower):
     def unit(n):
-        if n < 15:
-            s, q = (n // 3, n % 3) if n < 9 else (n % 3, 3 + (n - 9) // 3)
-            return (rf, st, rb)[s][q * R : (q + 1) * R, :]
-        if n < 18:
-            return v0[(n - 15) * R : (n - 14) * R, :]
-        k = (n - 18) % NB
-        if n < 18 + NB:
-            return m[k * R : (k + 1) * R, :]
+        if n < 5:
+            return st[n * R : (n + 1) * R, :]
+        if n < 8:
+            return v0[(n - 5) * R : (n - 4) * R, :]
+        return m[(n - 8) * R : (n - 7) * R, :]
+
+    pack_units(unit, UNITS_OWN, to_upper, to_lower)
+
+
+def pack_kernel(rf, rb, m, to_upper, to_lower, im):
+    def unit(n):
+        if n < 10:
+            ref, q = (rf, rb)[n // 5], n % 5
+            return ref[q * R : (q + 1) * R, :]
+        k = n - 10
         o, at = rows_of(k), k * R
         if o == 0:
             im[at : at + R, :] = m[at : at + R, :]
@@ -143,22 +170,36 @@
             im[at + o : at + R, :] = m[at : at + R - o, :]
         return im[at : at + R, :]
 
-    lane = lanes(8)
-    for t in range(YROWS // 8):
-        up = jnp.zeros((8, Y), F32)
-        low = jnp.zeros((8, Y), F32)
-        for p in range(SLOTS):
-            if t * SLOTS + p >= UNITS:
-                continue
-            value = unit(t * SLOTS + p)
-            for g in range(3):
-                part = value[8 * g : 8 * g + 8, :]
-                at = G * g + W * p
-                here = (lane >= at) & (lane < at + W)
-                up = jnp.where(here, roll(part, at + W), up)
-                low = jnp.where(here, roll(part, at), low)
-        to_upper[8 * t : 8 * t + 8, :] = up
-        to_lower[8 * t : 8 * t + 8, :] = low
+    pack_units(unit, UNITS_NEXT, to_upper, to_lower)
+
+
+def group_place(lo, hi):
+    place, inside = places()
+    return inside & (place >= lo) & (place < hi)
+
+
+def own_columns(n, mine_up, mine_low, out):
+    t, p = n // SLOTS, n % SLOTS
+    at = slice(8 * t, 8 * t + 8)
+    out = jnp.where(group_place(W, W + OWN), roll(mine_low[at, :], W - W * p), out)
+    return jnp.where(group_place(W + OWN, W + 2 * OWN), roll(mine_up[at, :], 2 * OWN - W * p), out)
+
+
+def outer_columns(n, rl, ru, out):
+    t, p = n // SLOTS, n % SLOTS
+    at = slice(8 * t, 8 * t + 8)
+    out = jnp.where(group_place(0, W), roll(rl[at, :], -W * p), out)
+    return jnp.where(
+        group_place(W + 2 * OWN, 2 * W + 2 * OWN), roll(ru[at, :], W + 2 * OWN - W * p), out
+    )
+
+
+def unpack_kernel(rl, ru, up1, low1, up2, low2, own, beside):
+    zero = jnp.zeros((8, Y), F32)
+    for n in range(UNITS_OWN):
+        own[8 * n : 8 * n + 8, :] = outer_columns(n, rl, ru, own_columns(n, up1, low1, zero))
+    for n in range(UNITS_NEXT):
+        beside[8 * n : 8 * n + 8, :] = own_columns(n, up2, low2, zero)
 
 
 OWN = 6
@@ -189,11 +230,11 @@
     return jnp.concatenate(rows, axis=0), edge
 
 
-def shift_slabs(main, number, sh):
+def shift_slabs(main, number, sh, first=0):
     rows = 3 * R
     for c in range(-3, 4):
-        at = (number * 7 + c + 3) * rows
-        sh[at : at + rows, :] = roll(main, -c)
+        at = (number * 7 + c + 3) * rows + first
+        sh[at : at + main.shape[0], :] = roll(main, -c)
 
 
 def shift_edges(edges, number, qh):
@@ -218,16 +259,18 @@
 
 
 DIRECTED = [(n // 2, 1 - 2 * (n % 2)) for n in range(2 * NB)]
-
-
-def in_parts(live, size, fn):
-    for start in range(0, 2 * NB, size):
-        pl.when(live)(functools.partial(fn, range(start, min(start + size, 2 * NB))))
-
-
-def add_forces(numbers, here, shifted, at_of, rows, kc, hc, acc):
-    total = [acc[q * rows : (q + 1) * rows, :] for q in range(3)]
-    mine = [here[q] for q in range(3)]
+ALL = list(range(2 * NB))
+
+
+def in_parts(live, numbers, size, fn):
+    for start in range(0, len(numbers), size):
+        pl.when(live)(functools.partial(fn, numbers[start : start + size]))
+
+
+def add_forces(numbers, here, shifted, at_of, rows, kc, hc, acc, lo=0, hi=None):
+    hi = rows if hi is None else hi
+    total = [acc[q * rows + lo : q * rows + hi, :] for q in range(3)]
+    mine = [here(q)[lo:hi, :] if (lo, hi) == (0, rows) else here(q, lo, hi) for q in range(3)]
     for n in numbers:
         k, sign = DIRECTED[n]
         a, b, c = OFFS[k]
@@ -236,14 +279,27 @@
         e = []
         for q in range(3):
             at = at_of(q, sign * rows_of(k), d[2])
-            there = shifted[at : at + rows, :]
+            there = shifted[at + lo : at + hi, :]
             e.append(there + float(d[q]) - mine[q] if d[q] else there - mine[q])
         sq = e[0] * e[0] + e[1] * e[1] + e[2] * e[2]
         t = sq * lax.rsqrt(jnp.maximum(sq, 1e-36)) - length
-        mag = kc[n * rows : (n + 1) * rows, :] * t / (hc[n * rows : (n + 1) * rows, :] + t * t)
+        at = n * rows
+        mag = kc[at + lo : at + hi, :] * t / (hc[at + lo : at + hi, :] + t * t)
         total = [total[q] + mag * e[q] for q in range(3)]
     for q in range(3):
-        acc[q * rows : (q + 1) * rows, :] = total[q]
+        acc[q * rows + lo : q * rows + hi, :] = total[q]
+
+
+def rows_from(ref, stride, start=0):
+    def here(q, lo=0, hi=None):
+        hi = R if hi is None else hi
+        return ref[q * stride + start + lo : q * stride + start + hi, :]
+
+    return here
+
+
+def edges_from(ref, stride, start=0):
+    return lambda q: ref[q * stride + start : q * stride + start + EDGE, :]
 
 
 def coefficients(mask, m_i, m_j, l_i, l_j, length):
@@ -283,34 +339,25 @@
             kk, hh = coefficients(mask, mod, mj, lim, lj, length_of(k))
             kc[n * R : (n + 1) * R, :] = kk
             hc[n * R : (n + 1) * R, :] = hh
-        here = [st[q * R : (q + 1) * R, :] for q in range(3)]
-        add_forces(numbers, here, sh, slab_at, R, kc, hc, acc)
-
-    in_parts(live, PART, part)
+        add_forces(numbers, rows_from(st, R), sh, slab_at, R, kc, hc, acc)
+
+    in_parts(live, ALL, PART, part)
     vel = v0[...] + DT * acc[...]
     v1[...] = vel
     u1[...] = st[0 : 3 * R, :] + DT * vel
 
 
-def edge_kernel(nwx, rl, ru, mine_up, mine_low, u1, v1, kc, hc, s_out, v_out, qh, acc, ue):
+def edge_kernel(nwx, rl, ru, own, beside, u1, v1, kc, hc, s_out, v_out, qh, acc, ue):
     live = lax.axis_index("wx") < nwx
-    place, inside = places()
-
-    def edge(n):
-        t, p = n // SLOTS, n % SLOTS
-        at = slice(8 * t, 8 * t + 8)
-        out = jnp.where(inside & (place < W), roll(rl[at, :], -W * p), 0.0)
-        own = roll(mine_low[at, :], W - W * p)
-        out = jnp.where(inside & (place >= W) & (place < W + OWN), own, out)
-        own = roll(mine_up[at, :], 2 * OWN - W * p)
-        out = jnp.where(inside & (place >= W + OWN) & (place < W + 2 * OWN), own, out)
-        above = roll(ru[at, :], W + 2 * OWN - W * p)
-        return jnp.where(
-            inside & (place >= W + 2 * OWN) & (place < 2 * W + 2 * OWN), above, out
-        )
+
+    def own_tile(n):
+        return own[8 * n : 8 * n + 8, :]
+
+    def tile(n):
+        return outer_columns(n, rl, ru, beside[8 * n : 8 * n + 8, :])
 
     for q in range(5):
-        tiles = [edge(s * 3 + q) if q < 3 else edge(9 + 3 * (q - 3) + s) for s in range(3)]
+        tiles = [tile(q), own_tile(q), tile(5 + q)]
         if q >= 3:
             tiles = [filled(x) for x in tiles]
         ue[8 * q : 8 * q + 8, :] = tiles[1]
@@ -322,17 +369,16 @@
         for n in numbers:
             k, sign = DIRECTED[n]
             o, c = sign * rows_of(k), sign * OFFS[k][2]
-            mask = edge(18 + k) if sign > 0 else roll(edge(18 + NB + k), -c)
+            mask = own_tile(8 + k) if sign > 0 else roll(tile(10 + k), -c)
             mj, lj = (qh[edge_at(q, o, c) : edge_at(q, o, c) + EDGE, :] for q in (3, 4))
             kk, hh = coefficients(mask, mod, mj, lim, lj, length_of(k))
             kc[n * EDGE : (n + 1) * EDGE, :] = kk
             hc[n * EDGE : (n + 1) * EDGE, :] = hh
-        here = [ue[q * EDGE : (q + 1) * EDGE, :] for q in range(3)]
-        add_forces(numbers, here, qh, edge_at, EDGE, kc, hc, acc)
-
-    in_parts(live, PART_EDGE // 2, part)
+        add_forces(numbers, edges_from(ue, EDGE), qh, edge_at, EDGE, kc, hc, acc)
+
+    in_parts(live, ALL, PART_EDGE, part)
     for q in range(3):
-        vel = edge(15 + q) + DT * acc[q * EDGE : (q + 1) * EDGE, :]
+        vel = own_tile(5 + q) + DT * acc[q * EDGE : (q + 1) * EDGE, :]
         dis = ue[q * EDGE : (q + 1) * EDGE, :] + DT * vel
         finish(q, u1[q * R : (q + 1) * R, :], dis, v1[q * R : (q + 1) * R, :], vel, s_out, v_out)
 
@@ -346,38 +392,79 @@
     v_out[at + R : at + BLOCK, :] = vel_e
 
 
-def step_kernel(nwx, last, s, ra, rb, v, kc, hc, ke, he, s_out, v_out, sh, qh, acc, acc_e):
-    wx = lax.axis_index("wx")
-    live = wx < nwx
-    even = lax.rem(wx, 2) == 0
-    for q in range(3):
-        at = q * BLOCK
-        top = jnp.where(even, rb[at : at + BLOCK, :], ra[at : at + BLOCK, :])
-        end = jnp.where(even, ra[at : at + BLOCK, :], rb[at : at + BLOCK, :])
-        mid = s[at : at + BLOCK, :]
-        shift_slabs(jnp.concatenate([top[:R], mid[:R], end[:R]], axis=0), q, sh)
-        shift_edges([top[R:], mid[R:], end[R:]], q, qh)
+def toward(sign):
+    return {a: [n for n in ALL if DIRECTED[n][1] == sign and OFFS[n // 2][0] == a] for a in (1, 2, 3)}
+
+
+def mid_kernel(s, near, kc, hc, ke, he, acc, acc_e, sh, qh):
+    even = lax.rem(lax.axis_index("wx"), 2) == 0
     acc[...] = jnp.zeros_like(acc)
     acc_e[...] = jnp.zeros_like(acc_e)
-    u_main = [s[q * BLOCK : q * BLOCK + R, :] for q in range(3)]
-    u_edge = [s[q * BLOCK + R : (q + 1) * BLOCK, :] for q in range(3)]
-
-    def slab_part(numbers):
-        here = [s[q * BLOCK : q * BLOCK + R, :] for q in range(3)]
-        add_forces(numbers, here, sh, slab_at, R, kc, hc, acc)
-
-    def edge_part(numbers):
-        here = [s[q * BLOCK + R : (q + 1) * BLOCK, :] for q in range(3)]
-        add_forces(numbers, here, qh, edge_at, EDGE, ke, he, acc_e)
-
-    in_parts(live, PART, slab_part)
-    in_parts(live, PART_EDGE, edge_part)
+    zero = jnp.zeros((EDGE, Y), F32)
+
+    def build(far_sign):
+        for q in range(3):
+            at = q * BLOCK
+            mid, other = s[at : at + BLOCK, :], near[at : at + BLOCK, :]
+            if far_sign < 0:
+                shift_slabs(jnp.concatenate([zero, mid[:R], other[:R]], axis=0), q, sh, R - 8)
+                shift_edges([zero, mid[R:], other[R:]], q, qh)
+            else:
+                shift_slabs(jnp.concatenate([other[:R], mid[:R], zero], axis=0), q, sh)
+                shift_edges([other[R:], mid[R:], zero], q, qh)
+
+    for far_sign, side in ((-1, even), (1, jnp.logical_not(even))):
+        pl.when(side)(functools.partial(build, far_sign))
+        leaving = toward(far_sign)
+        whole = [n for n in ALL if not any(n in x for x in leaving.values())]
+
+        def slab_part(numbers):
+            add_forces(numbers, rows_from(s, BLOCK), sh, slab_at, R, kc, hc, acc)
+
+        def edge_part(numbers):
+            add_forces(numbers, edges_from(s, BLOCK, R), qh, edge_at, EDGE, ke, he, acc_e)
+
+        in_parts(side, whole, PART, slab_part)
+        in_parts(side, whole, PART_EDGE, edge_part)
+        for a in (1, 2, 3):
+            lo, hi = (Z * a, R) if far_sign < 0 else (0, R - Z * a)
+
+            def inner_part(numbers, lo=lo, hi=hi):
+                add_forces(numbers, rows_from(s, BLOCK), sh, slab_at, R, kc, hc, acc, lo, hi)
+
+            in_parts(side, leaving[a], PART, inner_part)
+
+
+def far_kernel(last, s, near, far, v, part, part_e, kc, hc, ke, he, s_out, v_out, sh, qh, acc, acc_e):
+    even = lax.rem(lax.axis_index("wx"), 2) == 0
+    acc[...] = part[...]
+    acc_e[...] = part_e[...]
+
+    def side_part(far_sign):
+        for q in range(3):
+            at = q * BLOCK
+            mid, close, other = (x[at : at + BLOCK, :] for x in (s, near, far))
+            if far_sign < 0:
+                shift_slabs(jnp.concatenate([other[:R], mid[:8]], axis=0), q, sh)
+                shift_edges([other[R:], mid[R:], close[R:]], q, qh)
+            else:
+                shift_slabs(jnp.concatenate([mid[R - 8 : R], other[:R]], axis=0), q, sh, 2 * R - 8)
+                shift_edges([close[R:], mid[R:], other[R:]], q, qh)
+        leaving = toward(far_sign)
+        for a in (1, 2, 3):
+            lo, hi = (0, Z * a) if far_sign < 0 else (R - Z * a, R)
+            add_forces(leaving[a], rows_from(s, BLOCK), sh, slab_at, R, kc, hc, acc, lo, hi)
+        numbers = leaving[1] + leaving[2] + leaving[3]
+        add_forces(numbers, edges_from(s, BLOCK, R), qh, edge_at, EDGE, ke, he, acc_e)
+
+    for far_sign, side in ((-1, even), (1, jnp.logical_not(even))):
+        pl.when(side)(functools.partial(side_part, far_sign))
     for q in range(3):
         at = q * BLOCK
         vel = v[at : at + R, :] + DT * acc[q * R : (q + 1) * R, :]
-        dis = u_main[q] + DT * vel
+        dis = s[at : at + R, :] + DT * vel
         vel_e = v[at + R : at + BLOCK, :] + DT * acc_e[q * EDGE : (q + 1) * EDGE, :]
-        dis_e = u_edge[q] + DT * vel_e
+        dis_e = s[at + R : at + BLOCK, :] + DT * vel_e
         if not last:
             finish(q, dis, dis_e, vel, vel_e, s_out, v_out)
             continue
@@ -419,23 +506,32 @@
          tall(R, i32), tall(NB * R, i32), pltpu.SemaphoreType.DMA((6,)), tall(R, i32)],
         16, tuple(pltpu.with_memory_space_constraint(x, pltpu.HBM) for x in (stiffness, critical, u, v, lab, mask)),
     )
+    up = [(i, i + 1) for i in range(nny - 1)]
+    down = [(i + 1, i) for i in range(nny - 1)]
     rf = lax.ppermute(xf, "wx", [(i, i + 1) for i in range(nwx - 1)])
     rb = lax.ppermute(st, "wx", [(i + 1, i) for i in range(nwx - 1)])
-    to_upper, to_lower, im = call(
-        pack_kernel, (YROWS, YROWS, NB * R), vmem(5), [], 16, (st, rf, rb, v0, m)
-    )
-    rl = lax.ppermute(to_upper, "ny", [(i, i + 1) for i in range(nny - 1)])
-    ru = lax.ppermute(to_lower, "ny", [(i + 1, i) for i in range(nny - 1)])
+    up1, low1 = call(pack_own_kernel, (YROWS, YROWS), vmem(3), [], 16, (st, v0, m), 5_000_000)
+    rl1 = lax.ppermute(up1, "ny", up)
+    ru1 = lax.ppermute(low1, "ny", down)
+    up2, low2, im = call(
+        pack_kernel, (YROWS, YROWS, NB * R), vmem(3), [], 16, (rf, rb, m), 5_000_000
+    )
+    rl2 = lax.ppermute(up2, "ny", up)
+    ru2 = lax.ppermute(low2, "ny", down)
     kc, hc, u1, v1 = call(
         functools.partial(slab_kernel, nwx),
         (2 * NB * R, 2 * NB * R, 3 * R, 3 * R), vmem(6), [tall(5 * sh3), tall(3 * R)],
         24, (st, rf, rb, v0, m, im), 50_000_000,
     )
+    own, beside = call(
+        unpack_kernel, (UNITS_OWN * 8, UNITS_NEXT * 8), vmem(6), [], 16,
+        (rl1, ru1, up1, low1, up2, low2), 5_000_000,
+    )
     ke, he, s, vel = call(
         functools.partial(edge_kernel, nwx),
         (2 * NB * EDGE, 2 * NB * EDGE, 3 * BLOCK, 3 * BLOCK), vmem(6),
         [tall(5 * qh3), tall(3 * EDGE), tall(5 * EDGE)],
-        16, (rl, ru, to_upper, to_lower, u1, v1),
+        16, (rl2, ru2, own, beside, u1, v1),
     )
     near = [(i, i ^ 1) for i in range(nwx)]
     far = [(i, i + 1) for i in range(1, nwx - 1, 2)] + [(i + 1, i) for i in range(1, nwx - 1, 2)]
@@ -443,12 +539,16 @@
         last = n == STEPS - 1
         rb = lax.ppermute(s, "wx", far)
         ra = lax.ppermute(s, "wx", near)
+        acc, acc_e = call(
+            mid_kernel, (3 * R, 3 * EDGE), vmem(6), [tall(3 * sh3), tall(3 * qh3)],
+            16, (s, ra, kc, hc, ke, he), 50_000_000,
+        )
         size = 3 * R if last else 3 * BLOCK
         s, vel = call(
-            functools.partial(step_kernel, nwx, last),
-            (size, size), vmem(8),
+            functools.partial(far_kernel, last),
+            (size, size), vmem(10),
             [tall(3 * sh3), tall(3 * qh3), tall(3 * R), tall(3 * EDGE)],
-            16, (s, ra, rb, vel, kc, hc, ke, he),
+            16, (s, ra, rb, vel, acc, acc_e, kc, hc, ke, he),
         )
     back = lambda x: x.reshape(3, Z, X, Y).transpose(0, 2, 1, 3)
     return back(s), back(vel)

time: 74.6 us -> 69.4 us (0.930)
  waiting for transfers between devices: 19.1 us -> 10.7 us
  starting transfers between devices: 40.6 us -> 45 us
  Pallas kernels: 13.7 us -> 12.4 us
    ppermute x2 -> x4, starting transfers between devices: 2.72 us -> 11.1 us  [the longest x1 4.91 us: on_device(): rl2 = lax.ppermute(up2, 'ny', up)]
    ppermute x2 -> x4, waiting for transfers between devices: 5.67 us -> 2.53 us  [the longest x1 2.52 us: on_device(): ru2 = lax.ppermute(low2, 'ny', down)]
    ppermute x2, starting transfers between devices: 18.5 us -> 15.7 us  [on_device(): rb = lax.ppermute(s, 'wx', far)]
    ppermute x1, waiting for transfers between devices: 2.68 us -> 0.01 us  [on_device(): rf = lax.ppermute(xf, 'wx', [(i, i + 1) for i in range(nwx - 1)])]
    ppermute x1, waiting for transfers between devices: 1.85 us -> 0.01 us  [on_device(): rb = lax.ppermute(st, 'wx', [(i + 1, i) for i in range(nwx - 1)])]
    pallas_call x6 -> x10, Pallas kernels: 13.7 us -> 12.4 us  [call(): pl.pallas_call(kernel, out_shape=tuple((shape(n) for n in outs)), in_spec...]
    ppermute x2, starting transfers between devices: 5.05 us -> 3.84 us  [on_device(): ra = lax.ppermute(s, 'wx', near)]
    ppermute x2, waiting for transfers between devices: 8.92 us -> 8.17 us  [on_device(): rb = lax.ppermute(s, 'wx', far)]
  transfers between devices with their start and end apart: 8 -> 10, of which waited for: 5 -> 3; matrix products, arithmetic and copies ran while one was open for 0% -> 0% of each run, Pallas kernels for 3% -> 11%
where the time goes in v3:
time: 69.4 us; the launch traced here: 69 us
  starting transfers between devices  45 us (65%)
  Pallas kernels  12.4 us (18%)
  waiting for transfers between devices  10.7 us (15%)
  between operations  0.83 us (1%)
    ppermute x2, starting transfers between devices, on_device(): rb = lax.ppermute(s, 'wx', far)  15.7 us
    ppermute x1, starting transfers between devices, on_device(): rb = lax.ppermute(st, 'wx', [(i + 1, i) for i in range(nwx - 1)])  12.4 us
    pallas_call x10, Pallas kernels, call(): pl.pallas_call(kernel, out_shape=tuple((shape(n) for n in outs)), in_spec...  12.4 us
    ppermute x2, waiting for transfers between devices, on_device(): rb = lax.ppermute(s, 'wx', far)  8.17 us
    ppermute x1, starting transfers between devices, on_device(): rl2 = lax.ppermute(up2, 'ny', up)  4.91 us
    ppermute x2, starting transfers between devices, on_device(): ra = lax.ppermute(s, 'wx', near)  3.84 us
    ppermute x1, starting transfers between devices, on_device(): rl1 = lax.ppermute(up1, 'ny', up)  3.61 us
    ppermute x1, waiting for transfers between devices, on_device(): ru2 = lax.ppermute(low2, 'ny', down)  2.52 us
  transfers between devices with their start and end apart: 10, of which 3 were waited for; matrix products, arithmetic and copies ran while one was open for 0% of the time, Pallas kernels for 11%

profile of v3, /device:TPU:32, one launch (start us, length us, event | category | flops | bytes accessed | tf_op | source)
XLA Modules:
  0.0 69.0 jit_solution(2887239120253331095)
XLA Ops:
  0.6 1.5 %shard_map.77 = (f32[120,128]{1,0:T(8,128)S(1)}, f32[544,128]{1,0:T(8,128)S(1)}, f32[72,128]{1,0:T(8,128)S(1)}, f32[1464,128]{1,0:T(8,128)S(1)}) custom-call(f32[8]{0:T(128)} %refs_0_.1, f32[8]{0:T(128)} %refs_1_.1, f32[72,128]{1,0:T(8,128)} %bitcast.19, f32[72,128]{1,0:T(8,128)} %bitcast.20, s32[24,128]{1,0:T(8,128)} %bitcast.21, s32[1464,128]{1,0:T(8,128)} %bitcast.18), custom_call_target="tpu_custom_call" | custom-call | tf_op jit(solution)/shard_map/pallas_call | solution.py:480
  2.2 1.9 %collective-permute-start = (f32[544,128]{1,0:T(8,128)S(1)}, f32[544,128]{1,0:T(8,128)S(1)}, u32[]{:S(2)}, u32[]{:S(2)}) collective-permute-start(f32[544,128]{1,0:T(8,128)S(1)} %get-tuple-element.29), channel_id=1, source_target_pairs={{0,4},{4,8},{8,12},{12,16},{16,20},{20,24},{24,28},{28,32},{32,36}... | collective-permute-start | bytes 835592 | tf_op jit(solution)/shard_map/ppermute | solution.py:511
  4.1 12.4 %collective-permute-start.1 = (f32[120,128]{1,0:T(8,128)S(1)}, f32[120,128]{1,0:T(8,128)S(1)}, u32[]{:S(2)}, u32[]{:S(2)}) collective-permute-start(f32[120,128]{1,0:T(8,128)S(1)} %get-tuple-element.30.st), channel_id=1, source_target_pairs={{4,0},{8,4},{12,8},{16,12},{20,16},{24,20},{28,24},{32,28},{36,32}... | collective-permute-start | bytes 184328 | tf_op jit(solution)/shard_map/ppermute | solution.py:512
  16.5 0.5 shard_map.79
  17.0 3.6 %collective-permute-start.4 = (f32[144,128]{1,0:T(8,128)S(1)}, f32[144,128]{1,0:T(8,128)S(1)}, u32[]{:S(2)}, u32[]{:S(2)}) collective-permute-start(f32[144,128]{1,0:T(8,128)S(1)} %get-tuple-element.35.up1), channel_id=1, source_target_pairs={{0,1},{1,2},{2,3},{4,5},{5,6},{6,7},{8,9},{9,10},{10,11},{12,13},{... | collective-permute-start | bytes 221192 | tf_op jit(solution)/shard_map/ppermute | solution.py:514
  20.6 1.3 %collective-permute-start.5 = (f32[144,128]{1,0:T(8,128)S(1)}, f32[144,128]{1,0:T(8,128)S(1)}, u32[]{:S(2)}, u32[]{:S(2)}) collective-permute-start(f32[144,128]{1,0:T(8,128)S(1)} %get-tuple-element.36.low1), channel_id=1, source_target_pairs={{1,0},{2,1},{3,2},{5,4},{6,5},{7,6},{9,8},{10,9},{11,10},{13,12},{... | collective-permute-start | bytes 221192 | tf_op jit(solution)/shard_map/ppermute | solution.py:515
  21.9 0.0 collective-permute-done.1.rb
  22.0 0.0 collective-permute-done.rf
  22.0 0.5 shard_map.78
  22.5 4.9 %collective-permute-start.2 = (f32[144,128]{1,0:T(8,128)S(1)}, f32[144,128]{1,0:T(8,128)S(1)}, u32[]{:S(2)}, u32[]{:S(2)}) collective-permute-start(f32[144,128]{1,0:T(8,128)S(1)} %get-tuple-element.32.up2), channel_id=1, source_target_pairs={{0,1},{1,2},{2,3},{4,5},{5,6},{6,7},{8,9},{9,10},{10,11},{12,13},{... | collective-permute-start | bytes 221192 | tf_op jit(solution)/shard_map/ppermute | solution.py:519
  27.4 1.3 %collective-permute-start.3 = (f32[144,128]{1,0:T(8,128)S(1)}, f32[144,128]{1,0:T(8,128)S(1)}, u32[]{:S(2)}, u32[]{:S(2)}) collective-permute-start(f32[144,128]{1,0:T(8,128)S(1)} %get-tuple-element.33.low2), channel_id=1, source_target_pairs={{1,0},{2,1},{3,2},{5,4},{6,5},{7,6},{9,8},{10,9},{11,10},{13,12},{... | collective-permute-start | bytes 221192 | tf_op jit(solution)/shard_map/ppermute | solution.py:520
  28.7 0.0 collective-permute-done.4.rl
  28.7 0.0 collective-permute-done.5.ru
  28.7 0.5 shard_map.80
  29.2 2.3 %shard_map.81 = (f32[2928,128]{1,0:T(8,128)S(1)}, f32[2928,128]{1,0:T(8,128)S(1)}, f32[72,128]{1,0:T(8,128)S(1)}, f32[72,128]{1,0:T(8,128)S(1)}) custom-call(f32[120,128]{1,0:T(8,128)S(1)} %get-tuple-element.30.st, f32[544,128]{1,0:T(8,128)S(1)} %collective-permute-done.rf, f32[120,128]{1,0:T(8,128)S(1)} %collective-permute-done.1.rb, ...), custom_call_target="tpu_custom_call" | custom-call | flops 50000000 | tf_op jit(solution)/shard_map/pallas_call | solution.py:480
  31.5 0.0 collective-permute-done.2.rl
  31.5 2.5 %collective-permute-done.3.ru = f32[144,128]{1,0:T(8,128)S(1)} collective-permute-done((f32[144,128]{1,0:T(8,128)S(1)}, f32[144,128]{1,0:T(8,128)S(1)}, u32[]{:S(2)}, u32[]{:S(2)}) %collective-permute-start.3) | collective-permute-done | bytes 73760 | tf_op jit(solution)/shard_map/ppermute | solution.py:520
  34.0 1.3 %shard_map.82 = (f32[976,128]{1,0:T(8,128)S(1)}, f32[976,128]{1,0:T(8,128)S(1)}, f32[96,128]{1,0:T(8,128)S(1)}, f32[96,128]{1,0:T(8,128)S(1)}) custom-call(f32[144,128]{1,0:T(8,128)S(1)} %collective-permute-done.2.rl, f32[144,128]{1,0:T(8,128)S(1)} %collective-permute-done.3.ru, f32[552,128]{1,0:T(8,128)S(1)} %get-tuple-element.37.own, ...), custom_call_target="tpu_custom_call" | custom-call | tf_op jit(solution)/shard_map/pallas_call | solution.py:480
  35.3 1.9 %collective-permute-start.6 = (f32[96,128]{1,0:T(8,128)S(1)}, f32[96,128]{1,0:T(8,128)S(1)}, u32[]{:S(2)}, u32[]{:S(2)}) collective-permute-start(f32[96,128]{1,0:T(8,128)S(1)} %get-tuple-element.42.s), channel_id=1, source_target_pairs={{0,4},{4,0},{8,12},{12,8},{16,20},{20,16},{24,28},{28,24},{32,36},... | collective-permute-start | bytes 147464 | tf_op jit(solution)/shard_map/ppermute | solution.py:541
  37.3 7.6 %collective-permute-start.7 = (f32[96,128]{1,0:T(8,128)S(1)}, f32[96,128]{1,0:T(8,128)S(1)}, u32[]{:S(2)}, u32[]{:S(2)}) collective-permute-start(f32[96,128]{1,0:T(8,128)S(1)} %get-tuple-element.42.s), channel_id=1, source_target_pairs={{4,8},{12,16},{20,24},{28,32},{36,40},{44,48},{52,56},{60,64},{68,... | collective-permute-start | bytes 147464 | tf_op jit(solution)/shard_map/ppermute | solution.py:540
  44.9 0.0 collective-permute-done.6.near
  44.9 1.7 %shard_map.83 = (f32[72,128]{1,0:T(8,128)S(1)}, f32[24,128]{1,0:T(8,128)S(1)}) custom-call(f32[96,128]{1,0:T(8,128)S(1)} %get-tuple-element.42.s, f32[96,128]{1,0:T(8,128)S(1)} %collective-permute-done.6.near, f32[2928,128]{1,0:T(8,128)S(1)} %get-tuple-element.44.kc, f32[2928,128]{1,0:T(8,128)S(1)} %get-tuple-element.45.hc, ...), custom_call_target="tpu_custom_call" | custom-call | flops 50000000 | tf_op jit(solution)/shard_map/pallas_call | solution.py:480
  46.6 4.2 %collective-permute-done.7.far = f32[96,128]{1,0:T(8,128)S(1)} collective-permute-done((f32[96,128]{1,0:T(8,128)S(1)}, f32[96,128]{1,0:T(8,128)S(1)}, u32[]{:S(2)}, u32[]{:S(2)}) %collective-permute-start.7) | collective-permute-done | bytes 49184 | tf_op jit(solution)/shard_map/ppermute | solution.py:540
  50.8 0.8 %shard_map.84 = (f32[96,128]{1,0:T(8,128)S(1)}, f32[96,128]{1,0:T(8,128)S(1)}) custom-call(f32[96,128]{1,0:T(8,128)S(1)} %get-tuple-element.42.s, f32[96,128]{1,0:T(8,128)S(1)} %collective-permute-done.6.near, f32[96,128]{1,0:T(8,128)S(1)} %collective-permute-done.7.far, f32[96,128]{1,0:T(8,128)S(1)} %get-tuple-element.43.v, ...), custom_call_target="tpu_custom_call" | custom-call | tf_op jit(solution)/shard_map/pallas_call | solution.py:480
  51.6 1.9 %collective-permute-start.8 = (f32[96,128]{1,0:T(8,128)S(1)}, f32[96,128]{1,0:T(8,128)S(1)}, u32[]{:S(2)}, u32[]{:S(2)}) collective-permute-start(f32[96,128]{1,0:T(8,128)S(1)} %get-tuple-element.50.s), channel_id=1, source_target_pairs={{0,4},{4,0},{8,12},{12,8},{16,20},{20,16},{24,28},{28,24},{32,36},... | collective-permute-start | bytes 147464 | tf_op jit(solution)/shard_map/ppermute | solution.py:541
  53.5 8.1 %collective-permute-start.9 = (f32[96,128]{1,0:T(8,128)S(1)}, f32[96,128]{1,0:T(8,128)S(1)}, u32[]{:S(2)}, u32[]{:S(2)}) collective-permute-start(f32[96,128]{1,0:T(8,128)S(1)} %get-tuple-element.50.s), channel_id=1, source_target_pairs={{4,8},{12,16},{20,24},{28,32},{36,40},{44,48},{52,56},{60,64},{68,... | collective-permute-start | bytes 147464 | tf_op jit(solution)/shard_map/ppermute | solution.py:540
  61.6 0.0 collective-permute-done.8.near
  61.6 1.9 %shard_map.85 = (f32[72,128]{1,0:T(8,128)S(1)}, f32[24,128]{1,0:T(8,128)S(1)}) custom-call(f32[96,128]{1,0:T(8,128)S(1)} %get-tuple-element.50.s, f32[96,128]{1,0:T(8,128)S(1)} %collective-permute-done.8.near, f32[2928,128]{1,0:T(8,128)S(1)} %get-tuple-element.44.kc, f32[2928,128]{1,0:T(8,128)S(1)} %get-tuple-element.45.hc, ...), custom_call_target="tpu_custom_call" | custom-call | flops 50000000 | tf_op jit(solution)/shard_map/pallas_call | solution.py:480
  63.5 4.0 %collective-permute-done.9.far = f32[96,128]{1,0:T(8,128)S(1)} collective-permute-done((f32[96,128]{1,0:T(8,128)S(1)}, f32[96,128]{1,0:T(8,128)S(1)}, u32[]{:S(2)}, u32[]{:S(2)}) %collective-permute-start.9) | collective-permute-done | bytes 49184 | tf_op jit(solution)/shard_map/ppermute | solution.py:540
  67.5 1.4 %shard_map.86 = (f32[72,128]{1,0:T(8,128)}, f32[72,128]{1,0:T(8,128)}) custom-call(f32[96,128]{1,0:T(8,128)S(1)} %get-tuple-element.50.s, f32[96,128]{1,0:T(8,128)S(1)} %collective-permute-done.8.near, f32[96,128]{1,0:T(8,128)S(1)} %collective-permute-done.9.far, f32[96,128]{1,0:T(8,128)S(1)} %get-tuple-element.51.v, f32[72,128]{1,0:T(8,128)S(1)} %get-tuple-element.52.part, ...), custom_call_target="tpu_custom_call" | custom-call | tf_op jit(solution)/shard_map/pallas_call | solution.py:480
Async XLA Ops:
  2.2 19.8 %collective-permute-start = (f32[544,128]{1,0:T(8,128)S(1)}, f32[544,128]{1,0:T(8,128)S(1)}, u32[]{:S(2)}, u32[]{:S(2)}) collective-permute-start(f32[544,128]{1,0:T(8,128)S(1)} %get-tuple-element.29), channel_id=1, source_target_pairs={{0,4},{4,8},{8,12},{12,16},{16,20},{20,24},{24,28},{28,32},{32,36}... | collective-permute-start | bytes 835592 | tf_op jit(solution)/shard_map/ppermute | solution.py:511
  4.1 17.9 %collective-permute-start.1 = (f32[120,128]{1,0:T(8,128)S(1)}, f32[120,128]{1,0:T(8,128)S(1)}, u32[]{:S(2)}, u32[]{:S(2)}) collective-permute-start(f32[120,128]{1,0:T(8,128)S(1)} %get-tuple-element.30.st), channel_id=1, source_target_pairs={{4,0},{8,4},{12,8},{16,12},{20,16},{24,20},{28,24},{32,28},{36,32}... | collective-permute-start | bytes 184328 | tf_op jit(solution)/shard_map/ppermute | solution.py:512
  17.0 11.7 %collective-permute-start.4 = (f32[144,128]{1,0:T(8,128)S(1)}, f32[144,128]{1,0:T(8,128)S(1)}, u32[]{:S(2)}, u32[]{:S(2)}) collective-permute-start(f32[144,128]{1,0:T(8,128)S(1)} %get-tuple-element.35.up1), channel_id=1, source_target_pairs={{0,1},{1,2},{2,3},{4,5},{5,6},{6,7},{8,9},{9,10},{10,11},{12,13},{... | collective-permute-start | bytes 221192 | tf_op jit(solution)/shard_map/ppermute | solution.py:514
  20.6 8.0 %collective-permute-start.5 = (f32[144,128]{1,0:T(8,128)S(1)}, f32[144,128]{1,0:T(8,128)S(1)}, u32[]{:S(2)}, u32[]{:S(2)}) collective-permute-start(f32[144,128]{1,0:T(8,128)S(1)} %get-tuple-element.36.low1), channel_id=1, source_target_pairs={{1,0},{2,1},{3,2},{5,4},{6,5},{7,6},{9,8},{10,9},{11,10},{13,12},{... | collective-permute-start | bytes 221192 | tf_op jit(solution)/shard_map/ppermute | solution.py:515
  22.5 9.0 %collective-permute-start.2 = (f32[144,128]{1,0:T(8,128)S(1)}, f32[144,128]{1,0:T(8,128)S(1)}, u32[]{:S(2)}, u32[]{:S(2)}) collective-permute-start(f32[144,128]{1,0:T(8,128)S(1)} %get-tuple-element.32.up2), channel_id=1, source_target_pairs={{0,1},{1,2},{2,3},{4,5},{5,6},{6,7},{8,9},{9,10},{10,11},{12,13},{... | collective-permute-start | bytes 221192 | tf_op jit(solution)/shard_map/ppermute | solution.py:519
  27.4 6.6 %collective-permute-start.3 = (f32[144,128]{1,0:T(8,128)S(1)}, f32[144,128]{1,0:T(8,128)S(1)}, u32[]{:S(2)}, u32[]{:S(2)}) collective-permute-start(f32[144,128]{1,0:T(8,128)S(1)} %get-tuple-element.33.low2), channel_id=1, source_target_pairs={{1,0},{2,1},{3,2},{5,4},{6,5},{7,6},{9,8},{10,9},{11,10},{13,12},{... | collective-permute-start | bytes 221192 | tf_op jit(solution)/shard_map/ppermute | solution.py:520
  35.3 9.5 %collective-permute-start.6 = (f32[96,128]{1,0:T(8,128)S(1)}, f32[96,128]{1,0:T(8,128)S(1)}, u32[]{:S(2)}, u32[]{:S(2)}) collective-permute-start(f32[96,128]{1,0:T(8,128)S(1)} %get-tuple-element.42.s), channel_id=1, source_target_pairs={{0,4},{4,0},{8,12},{12,8},{16,20},{20,16},{24,28},{28,24},{32,36},... | collective-permute-start | bytes 147464 | tf_op jit(solution)/shard_map/ppermute | solution.py:541
  37.3 13.5 %collective-permute-start.7 = (f32[96,128]{1,0:T(8,128)S(1)}, f32[96,128]{1,0:T(8,128)S(1)}, u32[]{:S(2)}, u32[]{:S(2)}) collective-permute-start(f32[96,128]{1,0:T(8,128)S(1)} %get-tuple-element.42.s), channel_id=1, source_target_pairs={{4,8},{12,16},{20,24},{28,32},{36,40},{44,48},{52,56},{60,64},{68,... | collective-permute-start | bytes 147464 | tf_op jit(solution)/shard_map/ppermute | solution.py:540
  51.6 10.0 %collective-permute-start.8 = (f32[96,128]{1,0:T(8,128)S(1)}, f32[96,128]{1,0:T(8,128)S(1)}, u32[]{:S(2)}, u32[]{:S(2)}) collective-permute-start(f32[96,128]{1,0:T(8,128)S(1)} %get-tuple-element.50.s), channel_id=1, source_target_pairs={{0,4},{4,0},{8,12},{12,8},{16,20},{20,16},{24,28},{28,24},{32,36},... | collective-permute-start | bytes 147464 | tf_op jit(solution)/shard_map/ppermute | solution.py:541
  53.5 14.0 %collective-permute-start.9 = (f32[96,128]{1,0:T(8,128)S(1)}, f32[96,128]{1,0:T(8,128)S(1)}, u32[]{:S(2)}, u32[]{:S(2)}) collective-permute-start(f32[96,128]{1,0:T(8,128)S(1)} %get-tuple-element.50.s), channel_id=1, source_target_pairs={{4,8},{12,16},{20,24},{28,32},{36,40},{44,48},{52,56},{60,64},{68,... | collective-permute-start | bytes 147464 | tf_op jit(solution)/shard_map/ppermute | solution.py:540

commit v4 on v3

--- a/solution.py
+++ b/solution.py
@@ -75,20 +75,28 @@
     return jax.ShapeDtypeStruct((rows, Y), F32)
 
 
+CHUNKS = ((14, 30), (30, 46), (46, NB), (0, 14))
+
+
 def first_kernel(nwx, nny, *refs):
     given, (st, xf, v0, m_out), local, sems = refs[:6], refs[6:10], refs[10:16], refs[16]
     tmp = refs[17]
-    copies = [pltpu.make_async_copy(g, l, sems.at[i]) for i, (g, l) in enumerate(zip(given, local))]
-    for copy in copies:
+    stiff, crit, u, v, lab, mask = local
+    copies = [pltpu.make_async_copy(given[i], local[i], sems.at[i]) for i in (0, 1, 2, 4, 3)]
+    parts = [
+        pltpu.make_async_copy(
+            given[5].at[k0 * R : k1 * R, :], mask.at[k0 * R : k1 * R, :], sems.at[5 + i]
+        )
+        for i, (k0, k1) in enumerate(CHUNKS)
+    ]
+    for copy in copies[:4] + parts + copies[4:]:
         copy.start()
-    stiff, crit, u, v, lab, mask = local
     wx, ny = lax.axis_index("wx"), lax.axis_index("ny")
-    for copy in copies[:5]:
+    for copy in copies[:4]:
         copy.wait()
     for q in range(3):
         for x in range(X):
             st[q * R + x * Z : q * R + (x + 1) * Z, :] = u[pl.ds(q * R + x, Z, stride=X), :]
-            v0[q * R + x * Z : q * R + (x + 1) * Z, :] = v[pl.ds(q * R + x, Z, stride=X), :]
     for x in range(X):
         tmp[x * Z : (x + 1) * Z, :] = lab[pl.ds(x, Z, stride=X), :]
     label = tmp[...]
@@ -105,27 +113,32 @@
     zi = row % Z
     gx = wx * X + row // Z
     gy = ny * Y + lanes(R)
-    copies[5].wait()
-    for k, (a, b, c) in enumerate(OFFS):
-        for x in range(X):
-            m_out[k * R + x * Z : k * R + (x + 1) * Z, :] = mask[
-                pl.ds(k * R + x, Z, stride=X), :
-            ].astype(F32)
-        ok = (zi + b >= 0) & (zi + b < Z) & (gx + a < nwx * X)
-        if c:
-            ok = ok & (gy + c >= 0) & (gy + c < nny * Y)
-        m_out[k * R : (k + 1) * R, :] = jnp.where(ok, m_out[k * R : (k + 1) * R, :], 0.0)
-        if a:
-            o = rows_of(k)
-            at = STATE0 + PREV_AT[k]
-            xf[at : at + o, :] = m_out[(k + 1) * R - o : (k + 1) * R, :]
+    for part, (k0, k1) in zip(parts, CHUNKS):
+        part.wait()
+        for k in range(k0, k1):
+            a, b, c = OFFS[k]
+            for x in range(X):
+                m_out[k * R + x * Z : k * R + (x + 1) * Z, :] = mask[
+                    pl.ds(k * R + x, Z, stride=X), :
+                ].astype(F32)
+            ok = (zi + b >= 0) & (zi + b < Z) & (gx + a < nwx * X)
+            if c:
+                ok = ok & (gy + c >= 0) & (gy + c < nny * Y)
+            m_out[k * R : (k + 1) * R, :] = jnp.where(ok, m_out[k * R : (k + 1) * R, :], 0.0)
+            if a:
+                o, at = rows_of(k), STATE0 + PREV_AT[k]
+                xf[at : at + o, :] = m_out[(k + 1) * R - o : (k + 1) * R, :]
     if _at < PREV_ROWS:
         xf[STATE0 + _at : STATE0 + PREV_ROWS, :] = jnp.zeros((PREV_ROWS - _at, Y), F32)
-
-
-def pack_units(unit, units, to_upper, to_lower):
+    copies[4].wait()
+    for q in range(3):
+        for x in range(X):
+            v0[q * R + x * Z : q * R + (x + 1) * Z, :] = v[pl.ds(q * R + x, Z, stride=X), :]
+
+
+def pack_units(unit, units, to_upper, to_lower, first=0, final=YROWS // 8):
     lane = lanes(8)
-    for t in range(YROWS // 8):
+    for t in range(first, final):
         up = jnp.zeros((8, Y), F32)
         low = jnp.zeros((8, Y), F32)
         for p in range(SLOTS):
@@ -153,24 +166,37 @@
     pack_units(unit, UNITS_OWN, to_upper, to_lower)
 
 
-def pack_kernel(rf, rb, m, to_upper, to_lower, im):
-    def unit(n):
-        if n < 10:
-            ref, q = (rf, rb)[n // 5], n % 5
-            return ref[q * R : (q + 1) * R, :]
-        k = n - 10
+SPLIT = (5 + NB) // SLOTS
+
+
+def pack_kernel(rf, m, to_upper, to_lower, im):
+    for k in range(NB):
         o, at = rows_of(k), k * R
         if o == 0:
             im[at : at + R, :] = m[at : at + R, :]
+            continue
+        if OFFS[k][0]:
+            im[at : at + o, :] = rf[STATE0 + PREV_AT[k] : STATE0 + PREV_AT[k] + o, :]
         else:
-            if OFFS[k][0]:
-                im[at : at + o, :] = rf[STATE0 + PREV_AT[k] : STATE0 + PREV_AT[k] + o, :]
-            else:
-                im[at : at + o, :] = jnp.zeros((o, Y), F32)
-            im[at + o : at + R, :] = m[at : at + R - o, :]
-        return im[at : at + R, :]
-
-    pack_units(unit, UNITS_NEXT, to_upper, to_lower)
+            im[at : at + o, :] = jnp.zeros((o, Y), F32)
+        im[at + o : at + R, :] = m[at : at + R - o, :]
+
+    def unit(n):
+        return rf[n * R : (n + 1) * R, :] if n < 5 else im[(n - 5) * R : (n - 4) * R, :]
+
+    pack_units(unit, 5 + NB, to_upper, to_lower, 0, SPLIT)
+
+
+def pack_rest_kernel(upper, lower, rb, im, to_upper, to_lower):
+    to_upper[0 : 8 * SPLIT, :] = upper[...]
+    to_lower[0 : 8 * SPLIT, :] = lower[...]
+
+    def unit(n):
+        if n < 5 + NB:
+            return im[(n - 5) * R : (n - 4) * R, :]
+        return rb[(n - 5 - NB) * R : (n - 4 - NB) * R, :]
+
+    pack_units(unit, UNITS_NEXT, to_upper, to_lower, SPLIT)
 
 
 def group_place(lo, hi):
@@ -230,22 +256,22 @@
     return jnp.concatenate(rows, axis=0), edge
 
 
-def shift_slabs(main, number, sh, first=0):
+def shift_slabs(main, number, sh, first=0, reach=3):
     rows = 3 * R
-    for c in range(-3, 4):
+    for c in range(-reach, reach + 1):
         at = (number * 7 + c + 3) * rows + first
         sh[at : at + main.shape[0], :] = roll(main, -c)
 
 
-def shift_edges(edges, number, qh):
+def shift_edges(edges, number, qh, low=0, high=(3 * R - 16) // 8, reach=3):
     q = 3 * R - 16
     lane = lanes(8)
     tiles = []
-    for n in range(q // 8):
+    for n in range(low, high):
         part = [roll(edges[(n + g) // 3], G * (g - (n + g) % 3)) for g in range(3)]
         tiles.append(jnp.where(lane < G, part[0], jnp.where(lane < 2 * G, part[1], part[2])))
-    for c in range(-3, 4):
-        at = (number * 7 + c + 3) * q
+    for c in range(-reach, reach + 1):
+        at = (number * 7 + c + 3) * q + 8 * low
         for n, tile in enumerate(tiles):
             qh[at + 8 * n : at + 8 * n + 8, :] = roll(tile, -c)
 
@@ -318,7 +344,7 @@
 
 
 PART = 16
-PART_EDGE = 64
+PART_EDGE = 32
 
 
 def slab_kernel(nwx, st, rf, rb, v0, m, im, kc, hc, u1, v1, sh, acc):
@@ -357,7 +383,7 @@
         return outer_columns(n, rl, ru, beside[8 * n : 8 * n + 8, :])
 
     for q in range(5):
-        tiles = [tile(q), own_tile(q), tile(5 + q)]
+        tiles = [tile(q), own_tile(q), tile(5 + NB + q)]
         if q >= 3:
             tiles = [filled(x) for x in tiles]
         ue[8 * q : 8 * q + 8, :] = tiles[1]
@@ -369,14 +395,14 @@
         for n in numbers:
             k, sign = DIRECTED[n]
             o, c = sign * rows_of(k), sign * OFFS[k][2]
-            mask = own_tile(8 + k) if sign > 0 else roll(tile(10 + k), -c)
+            mask = own_tile(8 + k) if sign > 0 else roll(tile(5 + k), -c)
             mj, lj = (qh[edge_at(q, o, c) : edge_at(q, o, c) + EDGE, :] for q in (3, 4))
             kk, hh = coefficients(mask, mod, mj, lim, lj, length_of(k))
             kc[n * EDGE : (n + 1) * EDGE, :] = kk
             hc[n * EDGE : (n + 1) * EDGE, :] = hh
         add_forces(numbers, edges_from(ue, EDGE), qh, edge_at, EDGE, kc, hc, acc)
 
-    in_parts(live, ALL, PART_EDGE, part)
+    in_parts(live, ALL, 64, part)
     for q in range(3):
         vel = own_tile(5 + q) + DT * acc[q * EDGE : (q + 1) * EDGE, :]
         dis = ue[q * EDGE : (q + 1) * EDGE, :] + DT * vel
@@ -408,10 +434,10 @@
             mid, other = s[at : at + BLOCK, :], near[at : at + BLOCK, :]
             if far_sign < 0:
                 shift_slabs(jnp.concatenate([zero, mid[:R], other[:R]], axis=0), q, sh, R - 8)
-                shift_edges([zero, mid[R:], other[R:]], q, qh)
+                shift_edges([zero, mid[R:], other[R:]], q, qh, 2, 7)
             else:
                 shift_slabs(jnp.concatenate([other[:R], mid[:R], zero], axis=0), q, sh)
-                shift_edges([other[R:], mid[R:], zero], q, qh)
+                shift_edges([other[R:], mid[R:], zero], q, qh, 0, 5)
 
     for far_sign, side in ((-1, even), (1, jnp.logical_not(even))):
         pl.when(side)(functools.partial(build, far_sign))
@@ -440,25 +466,30 @@
     acc[...] = part[...]
     acc_e[...] = part_e[...]
 
-    def side_part(far_sign):
+    def build(far_sign):
         for q in range(3):
             at = q * BLOCK
             mid, close, other = (x[at : at + BLOCK, :] for x in (s, near, far))
             if far_sign < 0:
-                shift_slabs(jnp.concatenate([other[:R], mid[:8]], axis=0), q, sh)
-                shift_edges([other[R:], mid[R:], close[R:]], q, qh)
+                shift_slabs(jnp.concatenate([other[:R], mid[:8]], axis=0), q, sh, 0, 2)
+                shift_edges([other[R:], mid[R:], close[R:]], q, qh, 0, 4, 2)
             else:
-                shift_slabs(jnp.concatenate([mid[R - 8 : R], other[:R]], axis=0), q, sh, 2 * R - 8)
-                shift_edges([close[R:], mid[R:], other[R:]], q, qh)
+                shift_slabs(jnp.concatenate([mid[R - 8 : R], other[:R]], axis=0), q, sh, 2 * R - 8, 2)
+                shift_edges([close[R:], mid[R:], other[R:]], q, qh, 3, 7, 2)
+
+    def slab_part(lo, hi, numbers):
+        add_forces(numbers, rows_from(s, BLOCK), sh, slab_at, R, kc, hc, acc, lo, hi)
+
+    def edge_part(numbers):
+        add_forces(numbers, edges_from(s, BLOCK, R), qh, edge_at, EDGE, ke, he, acc_e)
+
+    for far_sign, side in ((-1, even), (1, jnp.logical_not(even))):
+        pl.when(side)(functools.partial(build, far_sign))
         leaving = toward(far_sign)
         for a in (1, 2, 3):
             lo, hi = (0, Z * a) if far_sign < 0 else (R - Z * a, R)
-            add_forces(leaving[a], rows_from(s, BLOCK), sh, slab_at, R, kc, hc, acc, lo, hi)
-        numbers = leaving[1] + leaving[2] + leaving[3]
-        add_forces(numbers, edges_from(s, BLOCK, R), qh, edge_at, EDGE, ke, he, acc_e)
-
-    for far_sign, side in ((-1, even), (1, jnp.logical_not(even))):
-        pl.when(side)(functools.partial(side_part, far_sign))
+            in_parts(side, leaving[a], PART_EDGE, functools.partial(slab_part, lo, hi))
+        in_parts(side, leaving[1] + leaving[2] + leaving[3], PART_EDGE, edge_part)
     for q in range(3):
         at = q * BLOCK
         vel = v[at : at + R, :] + DT * acc[q * R : (q + 1) * R, :]
@@ -503,7 +534,7 @@
         (STATE0, STATE0 + PREV_ROWS, 3 * R, NB * R),
         [pl.BlockSpec(memory_space=pltpu.HBM)] * 6,
         [pltpu.SMEM((MATS,), F32), pltpu.SMEM((MATS,), F32), tall(3 * R), tall(3 * R),
-         tall(R, i32), tall(NB * R, i32), pltpu.SemaphoreType.DMA((6,)), tall(R, i32)],
+         tall(R, i32), tall(NB * R, i32), pltpu.SemaphoreType.DMA((5 + len(CHUNKS),)), tall(R, i32)],
         16, tuple(pltpu.with_memory_space_constraint(x, pltpu.HBM) for x in (stiffness, critical, u, v, lab, mask)),
     )
     up = [(i, i + 1) for i in range(nny - 1)]
@@ -514,8 +545,10 @@
     rl1 = lax.ppermute(up1, "ny", up)
     ru1 = lax.ppermute(low1, "ny", down)
     up2, low2, im = call(
-        pack_kernel, (YROWS, YROWS, NB * R), vmem(3), [], 16, (rf, rb, m), 5_000_000
-    )
+        pack_kernel, (8 * SPLIT, 8 * SPLIT, NB * R), vmem(2), [], 16, (rf, m),
+        5_000_000,
+    )
+    up2, low2 = call(pack_rest_kernel, (YROWS, YROWS), vmem(4), [], 16, (up2, low2, rb, im))
     rl2 = lax.ppermute(up2, "ny", up)
     ru2 = lax.ppermute(low2, "ny", down)
     kc, hc, u1, v1 = call(

time: 69.4 us -> 69.1 us (level)
    pallas_call x10 -> x11, Pallas kernels: 12.4 us -> 11.9 us  [call(): pl.pallas_call(kernel, out_shape=tuple((shape(n) for n in outs)), in_spec...]
where the time goes in v4:
time: 69.1 us; the launch traced here: 68.6 us
  starting transfers between devices  44.6 us (65%)
  Pallas kernels  11.9 us (17%)
  waiting for transfers between devices  11.2 us (16%)
  between operations  0.83 us (1%)
    ppermute x2, starting transfers between devices, on_device(): rb = lax.ppermute(s, 'wx', far)  15.3 us
    ppermute x1, starting transfers between devices, on_device(): rb = lax.ppermute(st, 'wx', [(i + 1, i) for i in range(nwx - 1)])  12.4 us
    pallas_call x11, Pallas kernels, call(): pl.pallas_call(kernel, out_shape=tuple((shape(n) for n in outs)), in_spec...  11.9 us
    ppermute x2, waiting for transfers between devices, on_device(): rb = lax.ppermute(s, 'wx', far)  8.7 us
    ppermute x1, starting transfers between devices, on_device(): rl2 = lax.ppermute(up2, 'ny', up)  4.91 us
    ppermute x2, starting transfers between devices, on_device(): ra = lax.ppermute(s, 'wx', near)  3.84 us
    ppermute x1, starting transfers between devices, on_device(): rl1 = lax.ppermute(up1, 'ny', up)  3.61 us
    ppermute x1, waiting for transfers between devices, on_device(): ru2 = lax.ppermute(low2, 'ny', down)  2.52 us
  transfers between devices with their start and end apart: 10, of which 3 were waited for; matrix products, arithmetic and copies ran while one was open for 0% of the time, Pallas kernels for 11%

profile of v4, /device:TPU:32, one launch (start us, length us, event | category | flops | bytes accessed | tf_op | source)
XLA Modules:
  0.0 68.6 jit_solution(16867182532728939837)
XLA Ops:
  0.6 1.4 %shard_map.77 = (f32[120,128]{1,0:T(8,128)S(1)}, f32[544,128]{1,0:T(8,128)S(1)}, f32[72,128]{1,0:T(8,128)S(1)}, f32[1464,128]{1,0:T(8,128)S(1)}) custom-call(f32[8]{0:T(128)} %refs_0_.1, f32[8]{0:T(128)} %refs_1_.1, f32[72,128]{1,0:T(8,128)} %bitcast.19, f32[72,128]{1,0:T(8,128)} %bitcast.20, s32[24,128]{1,0:T(8,128)} %bitcast.21, s32[1464,128]{1,0:T(8,128)} %bitcast.18), custom_call_target="tpu_custom_call" | custom-call | tf_op jit(solution)/shard_map/pallas_call | solution.py:511
  2.0 1.9 %collective-permute-start = (f32[544,128]{1,0:T(8,128)S(1)}, f32[544,128]{1,0:T(8,128)S(1)}, u32[]{:S(2)}, u32[]{:S(2)}) collective-permute-start(f32[544,128]{1,0:T(8,128)S(1)} %get-tuple-element.31), channel_id=1, source_target_pairs={{0,4},{4,8},{8,12},{12,16},{16,20},{20,24},{24,28},{28,32},{32,36}... | collective-permute-start | bytes 835592 | tf_op jit(solution)/shard_map/ppermute | solution.py:542
  4.0 12.4 %collective-permute-start.1 = (f32[120,128]{1,0:T(8,128)S(1)}, f32[120,128]{1,0:T(8,128)S(1)}, u32[]{:S(2)}, u32[]{:S(2)}) collective-permute-start(f32[120,128]{1,0:T(8,128)S(1)} %get-tuple-element.35.st), channel_id=1, source_target_pairs={{4,0},{8,4},{12,8},{16,12},{20,16},{24,20},{28,24},{32,28},{36,32}... | collective-permute-start | bytes 184328 | tf_op jit(solution)/shard_map/ppermute | solution.py:543
  16.4 0.5 shard_map.80
  16.9 3.6 %collective-permute-start.4 = (f32[144,128]{1,0:T(8,128)S(1)}, f32[144,128]{1,0:T(8,128)S(1)}, u32[]{:S(2)}, u32[]{:S(2)}) collective-permute-start(f32[144,128]{1,0:T(8,128)S(1)} %get-tuple-element.40.up1), channel_id=1, source_target_pairs={{0,1},{1,2},{2,3},{4,5},{5,6},{6,7},{8,9},{9,10},{10,11},{12,13},{... | collective-permute-start | bytes 221192 | tf_op jit(solution)/shard_map/ppermute | solution.py:545
  20.5 1.3 %collective-permute-start.5 = (f32[144,128]{1,0:T(8,128)S(1)}, f32[144,128]{1,0:T(8,128)S(1)}, u32[]{:S(2)}, u32[]{:S(2)}) collective-permute-start(f32[144,128]{1,0:T(8,128)S(1)} %get-tuple-element.41.low1), channel_id=1, source_target_pairs={{1,0},{2,1},{3,2},{5,4},{6,5},{7,6},{9,8},{10,9},{11,10},{13,12},{... | collective-permute-start | bytes 221192 | tf_op jit(solution)/shard_map/ppermute | solution.py:546
  21.8 0.0 collective-permute-done.rf
  21.8 0.5 shard_map.78
  22.3 0.0 collective-permute-done.1.rb
  22.3 0.1 shard_map.79
  22.4 4.9 %collective-permute-start.2 = (f32[144,128]{1,0:T(8,128)S(1)}, f32[144,128]{1,0:T(8,128)S(1)}, u32[]{:S(2)}, u32[]{:S(2)}) collective-permute-start(f32[144,128]{1,0:T(8,128)S(1)} %get-tuple-element.37.up2), channel_id=1, source_target_pairs={{0,1},{1,2},{2,3},{4,5},{5,6},{6,7},{8,9},{9,10},{10,11},{12,13},{... | collective-permute-start | bytes 221192 | tf_op jit(solution)/shard_map/ppermute | solution.py:552
  27.3 1.3 %collective-permute-start.3 = (f32[144,128]{1,0:T(8,128)S(1)}, f32[144,128]{1,0:T(8,128)S(1)}, u32[]{:S(2)}, u32[]{:S(2)}) collective-permute-start(f32[144,128]{1,0:T(8,128)S(1)} %get-tuple-element.38.low2), channel_id=1, source_target_pairs={{1,0},{2,1},{3,2},{5,4},{6,5},{7,6},{9,8},{10,9},{11,10},{13,12},{... | collective-permute-start | bytes 221192 | tf_op jit(solution)/shard_map/ppermute | solution.py:553
  28.6 0.0 collective-permute-done.4.rl
  28.6 0.0 collective-permute-done.5.ru
  28.6 0.5 shard_map.81
  29.1 2.3 %shard_map.82 = (f32[2928,128]{1,0:T(8,128)S(1)}, f32[2928,128]{1,0:T(8,128)S(1)}, f32[72,128]{1,0:T(8,128)S(1)}, f32[72,128]{1,0:T(8,128)S(1)}) custom-call(f32[120,128]{1,0:T(8,128)S(1)} %get-tuple-element.35.st, f32[544,128]{1,0:T(8,128)S(1)} %collective-permute-done.rf, f32[120,128]{1,0:T(8,128)S(1)} %collective-permute-done.1.rb, ...), custom_call_target="tpu_custom_call" | custom-call | flops 50000000 | tf_op jit(solution)/shard_map/pallas_call | solution.py:511
  31.4 0.0 collective-permute-done.2.rl
  31.4 2.5 %collective-permute-done.3.ru = f32[144,128]{1,0:T(8,128)S(1)} collective-permute-done((f32[144,128]{1,0:T(8,128)S(1)}, f32[144,128]{1,0:T(8,128)S(1)}, u32[]{:S(2)}, u32[]{:S(2)}) %collective-permute-start.3) | collective-permute-done | bytes 73760 | tf_op jit(solution)/shard_map/ppermute | solution.py:553
  33.9 1.4 %shard_map.83 = (f32[976,128]{1,0:T(8,128)S(1)}, f32[976,128]{1,0:T(8,128)S(1)}, f32[96,128]{1,0:T(8,128)S(1)}, f32[96,128]{1,0:T(8,128)S(1)}) custom-call(f32[144,128]{1,0:T(8,128)S(1)} %collective-permute-done.2.rl, f32[144,128]{1,0:T(8,128)S(1)} %collective-permute-done.3.ru, f32[552,128]{1,0:T(8,128)S(1)} %get-tuple-element.42.own, ...), custom_call_target="tpu_custom_call" | custom-call | tf_op jit(solution)/shard_map/pallas_call | solution.py:511
  35.3 1.9 %collective-permute-start.6 = (f32[96,128]{1,0:T(8,128)S(1)}, f32[96,128]{1,0:T(8,128)S(1)}, u32[]{:S(2)}, u32[]{:S(2)}) collective-permute-start(f32[96,128]{1,0:T(8,128)S(1)} %get-tuple-element.46.s), channel_id=1, source_target_pairs={{0,4},{4,0},{8,12},{12,8},{16,20},{20,16},{24,28},{28,24},{32,36},... | collective-permute-start | bytes 147464 | tf_op jit(solution)/shard_map/ppermute | solution.py:574
  37.2 7.6 %collective-permute-start.7 = (f32[96,128]{1,0:T(8,128)S(1)}, f32[96,128]{1,0:T(8,128)S(1)}, u32[]{:S(2)}, u32[]{:S(2)}) collective-permute-start(f32[96,128]{1,0:T(8,128)S(1)} %get-tuple-element.46.s), channel_id=1, source_target_pairs={{4,8},{12,16},{20,24},{28,32},{36,40},{44,48},{52,56},{60,64},{68,... | collective-permute-start | bytes 147464 | tf_op jit(solution)/shard_map/ppermute | solution.py:573
  44.9 0.0 collective-permute-done.6.near
  44.9 1.7 %shard_map.84 = (f32[72,128]{1,0:T(8,128)S(1)}, f32[24,128]{1,0:T(8,128)S(1)}) custom-call(f32[96,128]{1,0:T(8,128)S(1)} %get-tuple-element.46.s, f32[96,128]{1,0:T(8,128)S(1)} %collective-permute-done.6.near, f32[2928,128]{1,0:T(8,128)S(1)} %get-tuple-element.48.kc, f32[2928,128]{1,0:T(8,128)S(1)} %get-tuple-element.49.hc, ...), custom_call_target="tpu_custom_call" | custom-call | flops 50000000 | tf_op jit(solution)/shard_map/pallas_call | solution.py:511
  46.5 4.2 %collective-permute-done.7.far = f32[96,128]{1,0:T(8,128)S(1)} collective-permute-done((f32[96,128]{1,0:T(8,128)S(1)}, f32[96,128]{1,0:T(8,128)S(1)}, u32[]{:S(2)}, u32[]{:S(2)}) %collective-permute-start.7) | collective-permute-done | bytes 49184 | tf_op jit(solution)/shard_map/ppermute | solution.py:573
  50.8 0.6 shard_map.85
  51.4 1.9 %collective-permute-start.8 = (f32[96,128]{1,0:T(8,128)S(1)}, f32[96,128]{1,0:T(8,128)S(1)}, u32[]{:S(2)}, u32[]{:S(2)}) collective-permute-start(f32[96,128]{1,0:T(8,128)S(1)} %get-tuple-element.54.s), channel_id=1, source_target_pairs={{0,4},{4,0},{8,12},{12,8},{16,20},{20,16},{24,28},{28,24},{32,36},... | collective-permute-start | bytes 147464 | tf_op jit(solution)/shard_map/ppermute | solution.py:574
  53.3 7.7 %collective-permute-start.9 = (f32[96,128]{1,0:T(8,128)S(1)}, f32[96,128]{1,0:T(8,128)S(1)}, u32[]{:S(2)}, u32[]{:S(2)}) collective-permute-start(f32[96,128]{1,0:T(8,128)S(1)} %get-tuple-element.54.s), channel_id=1, source_target_pairs={{4,8},{12,16},{20,24},{28,32},{36,40},{44,48},{52,56},{60,64},{68,... | collective-permute-start | bytes 147464 | tf_op jit(solution)/shard_map/ppermute | solution.py:573
  61.1 0.0 collective-permute-done.8.near
  61.1 1.8 %shard_map.86 = (f32[72,128]{1,0:T(8,128)S(1)}, f32[24,128]{1,0:T(8,128)S(1)}) custom-call(f32[96,128]{1,0:T(8,128)S(1)} %get-tuple-element.54.s, f32[96,128]{1,0:T(8,128)S(1)} %collective-permute-done.8.near, f32[2928,128]{1,0:T(8,128)S(1)} %get-tuple-element.48.kc, f32[2928,128]{1,0:T(8,128)S(1)} %get-tuple-element.49.hc, ...), custom_call_target="tpu_custom_call" | custom-call | flops 50000000 | tf_op jit(solution)/shard_map/pallas_call | solution.py:511
  62.9 4.5 %collective-permute-done.9.far = f32[96,128]{1,0:T(8,128)S(1)} collective-permute-done((f32[96,128]{1,0:T(8,128)S(1)}, f32[96,128]{1,0:T(8,128)S(1)}, u32[]{:S(2)}, u32[]{:S(2)}) %collective-permute-start.9) | collective-permute-done | bytes 49184 | tf_op jit(solution)/shard_map/ppermute | solution.py:573
  67.4 1.3 %shard_map.87 = (f32[72,128]{1,0:T(8,128)}, f32[72,128]{1,0:T(8,128)}) custom-call(f32[96,128]{1,0:T(8,128)S(1)} %get-tuple-element.54.s, f32[96,128]{1,0:T(8,128)S(1)} %collective-permute-done.8.near, f32[96,128]{1,0:T(8,128)S(1)} %collective-permute-done.9.far, f32[96,128]{1,0:T(8,128)S(1)} %get-tuple-element.55.v, f32[72,128]{1,0:T(8,128)S(1)} %get-tuple-element.56.part, ...), custom_call_target="tpu_custom_call" | custom-call | tf_op jit(solution)/shard_map/pallas_call | solution.py:511
Async XLA Ops:
  2.0 19.8 %collective-permute-start = (f32[544,128]{1,0:T(8,128)S(1)}, f32[544,128]{1,0:T(8,128)S(1)}, u32[]{:S(2)}, u32[]{:S(2)}) collective-permute-start(f32[544,128]{1,0:T(8,128)S(1)} %get-tuple-element.31), channel_id=1, source_target_pairs={{0,4},{4,8},{8,12},{12,16},{16,20},{20,24},{24,28},{28,32},{32,36}... | collective-permute-start | bytes 835592 | tf_op jit(solution)/shard_map/ppermute | solution.py:542
  4.0 18.3 %collective-permute-start.1 = (f32[120,128]{1,0:T(8,128)S(1)}, f32[120,128]{1,0:T(8,128)S(1)}, u32[]{:S(2)}, u32[]{:S(2)}) collective-permute-start(f32[120,128]{1,0:T(8,128)S(1)} %get-tuple-element.35.st), channel_id=1, source_target_pairs={{4,0},{8,4},{12,8},{16,12},{20,16},{24,20},{28,24},{32,28},{36,32}... | collective-permute-start | bytes 184328 | tf_op jit(solution)/shard_map/ppermute | solution.py:543
  16.9 11.7 %collective-permute-start.4 = (f32[144,128]{1,0:T(8,128)S(1)}, f32[144,128]{1,0:T(8,128)S(1)}, u32[]{:S(2)}, u32[]{:S(2)}) collective-permute-start(f32[144,128]{1,0:T(8,128)S(1)} %get-tuple-element.40.up1), channel_id=1, source_target_pairs={{0,1},{1,2},{2,3},{4,5},{5,6},{6,7},{8,9},{9,10},{10,11},{12,13},{... | collective-permute-start | bytes 221192 | tf_op jit(solution)/shard_map/ppermute | solution.py:545
  20.5 8.1 %collective-permute-start.5 = (f32[144,128]{1,0:T(8,128)S(1)}, f32[144,128]{1,0:T(8,128)S(1)}, u32[]{:S(2)}, u32[]{:S(2)}) collective-permute-start(f32[144,128]{1,0:T(8,128)S(1)} %get-tuple-element.41.low1), channel_id=1, source_target_pairs={{1,0},{2,1},{3,2},{5,4},{6,5},{7,6},{9,8},{10,9},{11,10},{13,12},{... | collective-permute-start | bytes 221192 | tf_op jit(solution)/shard_map/ppermute | solution.py:546
  22.4 9.0 %collective-permute-start.2 = (f32[144,128]{1,0:T(8,128)S(1)}, f32[144,128]{1,0:T(8,128)S(1)}, u32[]{:S(2)}, u32[]{:S(2)}) collective-permute-start(f32[144,128]{1,0:T(8,128)S(1)} %get-tuple-element.37.up2), channel_id=1, source_target_pairs={{0,1},{1,2},{2,3},{4,5},{5,6},{6,7},{8,9},{9,10},{10,11},{12,13},{... | collective-permute-start | bytes 221192 | tf_op jit(solution)/shard_map/ppermute | solution.py:552
  27.3 6.6 %collective-permute-start.3 = (f32[144,128]{1,0:T(8,128)S(1)}, f32[144,128]{1,0:T(8,128)S(1)}, u32[]{:S(2)}, u32[]{:S(2)}) collective-permute-start(f32[144,128]{1,0:T(8,128)S(1)} %get-tuple-element.38.low2), channel_id=1, source_target_pairs={{1,0},{2,1},{3,2},{5,4},{6,5},{7,6},{9,8},{10,9},{11,10},{13,12},{... | collective-permute-start | bytes 221192 | tf_op jit(solution)/shard_map/ppermute | solution.py:553
  35.3 9.6 %collective-permute-start.6 = (f32[96,128]{1,0:T(8,128)S(1)}, f32[96,128]{1,0:T(8,128)S(1)}, u32[]{:S(2)}, u32[]{:S(2)}) collective-permute-start(f32[96,128]{1,0:T(8,128)S(1)} %get-tuple-element.46.s), channel_id=1, source_target_pairs={{0,4},{4,0},{8,12},{12,8},{16,20},{20,16},{24,28},{28,24},{32,36},... | collective-permute-start | bytes 147464 | tf_op jit(solution)/shard_map/ppermute | solution.py:574
  37.2 13.5 %collective-permute-start.7 = (f32[96,128]{1,0:T(8,128)S(1)}, f32[96,128]{1,0:T(8,128)S(1)}, u32[]{:S(2)}, u32[]{:S(2)}) collective-permute-start(f32[96,128]{1,0:T(8,128)S(1)} %get-tuple-element.46.s), channel_id=1, source_target_pairs={{4,8},{12,16},{20,24},{28,32},{36,40},{44,48},{52,56},{60,64},{68,... | collective-permute-start | bytes 147464 | tf_op jit(solution)/shard_map/ppermute | solution.py:573
  51.4 9.7 %collective-permute-start.8 = (f32[96,128]{1,0:T(8,128)S(1)}, f32[96,128]{1,0:T(8,128)S(1)}, u32[]{:S(2)}, u32[]{:S(2)}) collective-permute-start(f32[96,128]{1,0:T(8,128)S(1)} %get-tuple-element.54.s), channel_id=1, source_target_pairs={{0,4},{4,0},{8,12},{12,8},{16,20},{20,16},{24,28},{28,24},{32,36},... | collective-permute-start | bytes 147464 | tf_op jit(solution)/shard_map/ppermute | solution.py:574
  53.3 14.0 %collective-permute-start.9 = (f32[96,128]{1,0:T(8,128)S(1)}, f32[96,128]{1,0:T(8,128)S(1)}, u32[]{:S(2)}, u32[]{:S(2)}) collective-permute-start(f32[96,128]{1,0:T(8,128)S(1)} %get-tuple-element.54.s), channel_id=1, source_target_pairs={{4,8},{12,16},{20,24},{28,32},{36,40},{44,48},{52,56},{60,64},{68,... | collective-permute-start | bytes 147464 | tf_op jit(solution)/shard_map/ppermute | solution.py:573

commit v5 on v4

--- a/solution.py
+++ b/solution.py
@@ -297,6 +297,7 @@
     hi = rows if hi is None else hi
     total = [acc[q * rows + lo : q * rows + hi, :] for q in range(3)]
     mine = [here(q)[lo:hi, :] if (lo, hi) == (0, rows) else here(q, lo, hi) for q in range(3)]
+    moved = {}
     for n in numbers:
         k, sign = DIRECTED[n]
         a, b, c = OFFS[k]
@@ -306,7 +307,9 @@
         for q in range(3):
             at = at_of(q, sign * rows_of(k), d[2])
             there = shifted[at + lo : at + hi, :]
-            e.append(there + float(d[q]) - mine[q] if d[q] else there - mine[q])
+            if (q, d[q]) not in moved:
+                moved[q, d[q]] = mine[q] - float(d[q]) if d[q] else mine[q]
+            e.append(there - moved[q, d[q]])
         sq = e[0] * e[0] + e[1] * e[1] + e[2] * e[2]
         t = sq * lax.rsqrt(jnp.maximum(sq, 1e-36)) - length
         at = n * rows

time: 69.1 us -> 69.1 us (level)
  no operation moved by 1% of the time
where the time goes in v5:
time: 69.1 us; the launch traced here: 68.6 us
  starting transfers between devices  44.6 us (65%)
  Pallas kernels  11.9 us (17%)
  waiting for transfers between devices  11.2 us (16%)
  between operations  0.83 us (1%)
    ppermute x2, starting transfers between devices, on_device(): rb = lax.ppermute(s, 'wx', far)  15.3 us
    ppermute x1, starting transfers between devices, on_device(): rb = lax.ppermute(st, 'wx', [(i + 1, i) for i in range(nwx - 1)])  12.4 us
    pallas_call x11, Pallas kernels, call(): pl.pallas_call(kernel, out_shape=tuple((shape(n) for n in outs)), in_spec...  11.9 us
    ppermute x2, waiting for transfers between devices, on_device(): rb = lax.ppermute(s, 'wx', far)  8.69 us
    ppermute x1, starting transfers between devices, on_device(): rl2 = lax.ppermute(up2, 'ny', up)  4.91 us
    ppermute x2, starting transfers between devices, on_device(): ra = lax.ppermute(s, 'wx', near)  3.84 us
    ppermute x1, starting transfers between devices, on_device(): rl1 = lax.ppermute(up1, 'ny', up)  3.61 us
    ppermute x1, waiting for transfers between devices, on_device(): ru2 = lax.ppermute(low2, 'ny', down)  2.52 us
  transfers between devices with their start and end apart: 10, of which 3 were waited for; matrix products, arithmetic and copies ran while one was open for 0% of the time, Pallas kernels for 11%

profile of v5, /device:TPU:32, one launch (start us, length us, event | category | flops | bytes accessed | tf_op | source)
XLA Modules:
  0.0 68.6 jit_solution(15616004855950507335)
XLA Ops:
  0.6 1.4 %shard_map.77 = (f32[120,128]{1,0:T(8,128)S(1)}, f32[544,128]{1,0:T(8,128)S(1)}, f32[72,128]{1,0:T(8,128)S(1)}, f32[1464,128]{1,0:T(8,128)S(1)}) custom-call(f32[8]{0:T(128)} %refs_0_.1, f32[8]{0:T(128)} %refs_1_.1, f32[72,128]{1,0:T(8,128)} %bitcast.19, f32[72,128]{1,0:T(8,128)} %bitcast.20, s32[24,128]{1,0:T(8,128)} %bitcast.21, s32[1464,128]{1,0:T(8,128)} %bitcast.18), custom_call_target="tpu_custom_call" | custom-call | tf_op jit(solution)/shard_map/pallas_call | solution.py:514
  2.0 1.9 %collective-permute-start = (f32[544,128]{1,0:T(8,128)S(1)}, f32[544,128]{1,0:T(8,128)S(1)}, u32[]{:S(2)}, u32[]{:S(2)}) collective-permute-start(f32[544,128]{1,0:T(8,128)S(1)} %get-tuple-element.31), channel_id=1, source_target_pairs={{0,4},{4,8},{8,12},{12,16},{16,20},{20,24},{24,28},{28,32},{32,36}... | collective-permute-start | bytes 835592 | tf_op jit(solution)/shard_map/ppermute | solution.py:545
  4.0 12.4 %collective-permute-start.1 = (f32[120,128]{1,0:T(8,128)S(1)}, f32[120,128]{1,0:T(8,128)S(1)}, u32[]{:S(2)}, u32[]{:S(2)}) collective-permute-start(f32[120,128]{1,0:T(8,128)S(1)} %get-tuple-element.35.st), channel_id=1, source_target_pairs={{4,0},{8,4},{12,8},{16,12},{20,16},{24,20},{28,24},{32,28},{36,32}... | collective-permute-start | bytes 184328 | tf_op jit(solution)/shard_map/ppermute | solution.py:546
  16.4 0.5 shard_map.80
  16.9 3.6 %collective-permute-start.4 = (f32[144,128]{1,0:T(8,128)S(1)}, f32[144,128]{1,0:T(8,128)S(1)}, u32[]{:S(2)}, u32[]{:S(2)}) collective-permute-start(f32[144,128]{1,0:T(8,128)S(1)} %get-tuple-element.40.up1), channel_id=1, source_target_pairs={{0,1},{1,2},{2,3},{4,5},{5,6},{6,7},{8,9},{9,10},{10,11},{12,13},{... | collective-permute-start | bytes 221192 | tf_op jit(solution)/shard_map/ppermute | solution.py:548
  20.5 1.3 %collective-permute-start.5 = (f32[144,128]{1,0:T(8,128)S(1)}, f32[144,128]{1,0:T(8,128)S(1)}, u32[]{:S(2)}, u32[]{:S(2)}) collective-permute-start(f32[144,128]{1,0:T(8,128)S(1)} %get-tuple-element.41.low1), channel_id=1, source_target_pairs={{1,0},{2,1},{3,2},{5,4},{6,5},{7,6},{9,8},{10,9},{11,10},{13,12},{... | collective-permute-start | bytes 221192 | tf_op jit(solution)/shard_map/ppermute | solution.py:549
  21.8 0.0 collective-permute-done.rf
  21.8 0.5 shard_map.78
  22.3 0.0 collective-permute-done.1.rb
  22.3 0.1 shard_map.79
  22.4 4.9 %collective-permute-start.2 = (f32[144,128]{1,0:T(8,128)S(1)}, f32[144,128]{1,0:T(8,128)S(1)}, u32[]{:S(2)}, u32[]{:S(2)}) collective-permute-start(f32[144,128]{1,0:T(8,128)S(1)} %get-tuple-element.37.up2), channel_id=1, source_target_pairs={{0,1},{1,2},{2,3},{4,5},{5,6},{6,7},{8,9},{9,10},{10,11},{12,13},{... | collective-permute-start | bytes 221192 | tf_op jit(solution)/shard_map/ppermute | solution.py:555
  27.3 1.3 %collective-permute-start.3 = (f32[144,128]{1,0:T(8,128)S(1)}, f32[144,128]{1,0:T(8,128)S(1)}, u32[]{:S(2)}, u32[]{:S(2)}) collective-permute-start(f32[144,128]{1,0:T(8,128)S(1)} %get-tuple-element.38.low2), channel_id=1, source_target_pairs={{1,0},{2,1},{3,2},{5,4},{6,5},{7,6},{9,8},{10,9},{11,10},{13,12},{... | collective-permute-start | bytes 221192 | tf_op jit(solution)/shard_map/ppermute | solution.py:556
  28.6 0.0 collective-permute-done.4.rl
  28.6 0.0 collective-permute-done.5.ru
  28.6 0.5 shard_map.81
  29.1 2.3 %shard_map.82 = (f32[2928,128]{1,0:T(8,128)S(1)}, f32[2928,128]{1,0:T(8,128)S(1)}, f32[72,128]{1,0:T(8,128)S(1)}, f32[72,128]{1,0:T(8,128)S(1)}) custom-call(f32[120,128]{1,0:T(8,128)S(1)} %get-tuple-element.35.st, f32[544,128]{1,0:T(8,128)S(1)} %collective-permute-done.rf, f32[120,128]{1,0:T(8,128)S(1)} %collective-permute-done.1.rb, ...), custom_call_target="tpu_custom_call" | custom-call | flops 50000000 | tf_op jit(solution)/shard_map/pallas_call | solution.py:514
  31.4 0.0 collective-permute-done.2.rl
  31.4 2.5 %collective-permute-done.3.ru = f32[144,128]{1,0:T(8,128)S(1)} collective-permute-done((f32[144,128]{1,0:T(8,128)S(1)}, f32[144,128]{1,0:T(8,128)S(1)}, u32[]{:S(2)}, u32[]{:S(2)}) %collective-permute-start.3) | collective-permute-done | bytes 73760 | tf_op jit(solution)/shard_map/ppermute | solution.py:556
  33.9 1.4 %shard_map.83 = (f32[976,128]{1,0:T(8,128)S(1)}, f32[976,128]{1,0:T(8,128)S(1)}, f32[96,128]{1,0:T(8,128)S(1)}, f32[96,128]{1,0:T(8,128)S(1)}) custom-call(f32[144,128]{1,0:T(8,128)S(1)} %collective-permute-done.2.rl, f32[144,128]{1,0:T(8,128)S(1)} %collective-permute-done.3.ru, f32[552,128]{1,0:T(8,128)S(1)} %get-tuple-element.42.own, ...), custom_call_target="tpu_custom_call" | custom-call | tf_op jit(solution)/shard_map/pallas_call | solution.py:514
  35.3 1.9 %collective-permute-start.6 = (f32[96,128]{1,0:T(8,128)S(1)}, f32[96,128]{1,0:T(8,128)S(1)}, u32[]{:S(2)}, u32[]{:S(2)}) collective-permute-start(f32[96,128]{1,0:T(8,128)S(1)} %get-tuple-element.46.s), channel_id=1, source_target_pairs={{0,4},{4,0},{8,12},{12,8},{16,20},{20,16},{24,28},{28,24},{32,36},... | collective-permute-start | bytes 147464 | tf_op jit(solution)/shard_map/ppermute | solution.py:577
  37.2 7.6 %collective-permute-start.7 = (f32[96,128]{1,0:T(8,128)S(1)}, f32[96,128]{1,0:T(8,128)S(1)}, u32[]{:S(2)}, u32[]{:S(2)}) collective-permute-start(f32[96,128]{1,0:T(8,128)S(1)} %get-tuple-element.46.s), channel_id=1, source_target_pairs={{4,8},{12,16},{20,24},{28,32},{36,40},{44,48},{52,56},{60,64},{68,... | collective-permute-start | bytes 147464 | tf_op jit(solution)/shard_map/ppermute | solution.py:576
  44.9 0.0 collective-permute-done.6.near
  44.9 1.7 %shard_map.84 = (f32[72,128]{1,0:T(8,128)S(1)}, f32[24,128]{1,0:T(8,128)S(1)}) custom-call(f32[96,128]{1,0:T(8,128)S(1)} %get-tuple-element.46.s, f32[96,128]{1,0:T(8,128)S(1)} %collective-permute-done.6.near, f32[2928,128]{1,0:T(8,128)S(1)} %get-tuple-element.48.kc, f32[2928,128]{1,0:T(8,128)S(1)} %get-tuple-element.49.hc, ...), custom_call_target="tpu_custom_call" | custom-call | flops 50000000 | tf_op jit(solution)/shard_map/pallas_call | solution.py:514
  46.5 4.2 %collective-permute-done.7.far = f32[96,128]{1,0:T(8,128)S(1)} collective-permute-done((f32[96,128]{1,0:T(8,128)S(1)}, f32[96,128]{1,0:T(8,128)S(1)}, u32[]{:S(2)}, u32[]{:S(2)}) %collective-permute-start.7) | collective-permute-done | bytes 49184 | tf_op jit(solution)/shard_map/ppermute | solution.py:576
  50.8 0.6 shard_map.85
  51.4 1.9 %collective-permute-start.8 = (f32[96,128]{1,0:T(8,128)S(1)}, f32[96,128]{1,0:T(8,128)S(1)}, u32[]{:S(2)}, u32[]{:S(2)}) collective-permute-start(f32[96,128]{1,0:T(8,128)S(1)} %get-tuple-element.54.s), channel_id=1, source_target_pairs={{0,4},{4,0},{8,12},{12,8},{16,20},{20,16},{24,28},{28,24},{32,36},... | collective-permute-start | bytes 147464 | tf_op jit(solution)/shard_map/ppermute | solution.py:577
  53.3 7.7 %collective-permute-start.9 = (f32[96,128]{1,0:T(8,128)S(1)}, f32[96,128]{1,0:T(8,128)S(1)}, u32[]{:S(2)}, u32[]{:S(2)}) collective-permute-start(f32[96,128]{1,0:T(8,128)S(1)} %get-tuple-element.54.s), channel_id=1, source_target_pairs={{4,8},{12,16},{20,24},{28,32},{36,40},{44,48},{52,56},{60,64},{68,... | collective-permute-start | bytes 147464 | tf_op jit(solution)/shard_map/ppermute | solution.py:576
  61.0 0.0 collective-permute-done.8.near
  61.1 1.8 %shard_map.86 = (f32[72,128]{1,0:T(8,128)S(1)}, f32[24,128]{1,0:T(8,128)S(1)}) custom-call(f32[96,128]{1,0:T(8,128)S(1)} %get-tuple-element.54.s, f32[96,128]{1,0:T(8,128)S(1)} %collective-permute-done.8.near, f32[2928,128]{1,0:T(8,128)S(1)} %get-tuple-element.48.kc, f32[2928,128]{1,0:T(8,128)S(1)} %get-tuple-element.49.hc, ...), custom_call_target="tpu_custom_call" | custom-call | flops 50000000 | tf_op jit(solution)/shard_map/pallas_call | solution.py:514
  62.9 4.5 %collective-permute-done.9.far = f32[96,128]{1,0:T(8,128)S(1)} collective-permute-done((f32[96,128]{1,0:T(8,128)S(1)}, f32[96,128]{1,0:T(8,128)S(1)}, u32[]{:S(2)}, u32[]{:S(2)}) %collective-permute-start.9) | collective-permute-done | bytes 49184 | tf_op jit(solution)/shard_map/ppermute | solution.py:576
  67.4 1.3 %shard_map.87 = (f32[72,128]{1,0:T(8,128)}, f32[72,128]{1,0:T(8,128)}) custom-call(f32[96,128]{1,0:T(8,128)S(1)} %get-tuple-element.54.s, f32[96,128]{1,0:T(8,128)S(1)} %collective-permute-done.8.near, f32[96,128]{1,0:T(8,128)S(1)} %collective-permute-done.9.far, f32[96,128]{1,0:T(8,128)S(1)} %get-tuple-element.55.v, f32[72,128]{1,0:T(8,128)S(1)} %get-tuple-element.56.part, ...), custom_call_target="tpu_custom_call" | custom-call | tf_op jit(solution)/shard_map/pallas_call | solution.py:514
Async XLA Ops:
  2.0 19.8 %collective-permute-start = (f32[544,128]{1,0:T(8,128)S(1)}, f32[544,128]{1,0:T(8,128)S(1)}, u32[]{:S(2)}, u32[]{:S(2)}) collective-permute-start(f32[544,128]{1,0:T(8,128)S(1)} %get-tuple-element.31), channel_id=1, source_target_pairs={{0,4},{4,8},{8,12},{12,16},{16,20},{20,24},{24,28},{28,32},{32,36}... | collective-permute-start | bytes 835592 | tf_op jit(solution)/shard_map/ppermute | solution.py:545
  4.0 18.3 %collective-permute-start.1 = (f32[120,128]{1,0:T(8,128)S(1)}, f32[120,128]{1,0:T(8,128)S(1)}, u32[]{:S(2)}, u32[]{:S(2)}) collective-permute-start(f32[120,128]{1,0:T(8,128)S(1)} %get-tuple-element.35.st), channel_id=1, source_target_pairs={{4,0},{8,4},{12,8},{16,12},{20,16},{24,20},{28,24},{32,28},{36,32}... | collective-permute-start | bytes 184328 | tf_op jit(solution)/shard_map/ppermute | solution.py:546
  16.9 11.7 %collective-permute-start.4 = (f32[144,128]{1,0:T(8,128)S(1)}, f32[144,128]{1,0:T(8,128)S(1)}, u32[]{:S(2)}, u32[]{:S(2)}) collective-permute-start(f32[144,128]{1,0:T(8,128)S(1)} %get-tuple-element.40.up1), channel_id=1, source_target_pairs={{0,1},{1,2},{2,3},{4,5},{5,6},{6,7},{8,9},{9,10},{10,11},{12,13},{... | collective-permute-start | bytes 221192 | tf_op jit(solution)/shard_map/ppermute | solution.py:548
  20.5 8.1 %collective-permute-start.5 = (f32[144,128]{1,0:T(8,128)S(1)}, f32[144,128]{1,0:T(8,128)S(1)}, u32[]{:S(2)}, u32[]{:S(2)}) collective-permute-start(f32[144,128]{1,0:T(8,128)S(1)} %get-tuple-element.41.low1), channel_id=1, source_target_pairs={{1,0},{2,1},{3,2},{5,4},{6,5},{7,6},{9,8},{10,9},{11,10},{13,12},{... | collective-permute-start | bytes 221192 | tf_op jit(solution)/shard_map/ppermute | solution.py:549
  22.4 9.0 %collective-permute-start.2 = (f32[144,128]{1,0:T(8,128)S(1)}, f32[144,128]{1,0:T(8,128)S(1)}, u32[]{:S(2)}, u32[]{:S(2)}) collective-permute-start(f32[144,128]{1,0:T(8,128)S(1)} %get-tuple-element.37.up2), channel_id=1, source_target_pairs={{0,1},{1,2},{2,3},{4,5},{5,6},{6,7},{8,9},{9,10},{10,11},{12,13},{... | collective-permute-start | bytes 221192 | tf_op jit(solution)/shard_map/ppermute | solution.py:555
  27.3 6.6 %collective-permute-start.3 = (f32[144,128]{1,0:T(8,128)S(1)}, f32[144,128]{1,0:T(8,128)S(1)}, u32[]{:S(2)}, u32[]{:S(2)}) collective-permute-start(f32[144,128]{1,0:T(8,128)S(1)} %get-tuple-element.38.low2), channel_id=1, source_target_pairs={{1,0},{2,1},{3,2},{5,4},{6,5},{7,6},{9,8},{10,9},{11,10},{13,12},{... | collective-permute-start | bytes 221192 | tf_op jit(solution)/shard_map/ppermute | solution.py:556
  35.3 9.6 %collective-permute-start.6 = (f32[96,128]{1,0:T(8,128)S(1)}, f32[96,128]{1,0:T(8,128)S(1)}, u32[]{:S(2)}, u32[]{:S(2)}) collective-permute-start(f32[96,128]{1,0:T(8,128)S(1)} %get-tuple-element.46.s), channel_id=1, source_target_pairs={{0,4},{4,0},{8,12},{12,8},{16,20},{20,16},{24,28},{28,24},{32,36},... | collective-permute-start | bytes 147464 | tf_op jit(solution)/shard_map/ppermute | solution.py:577
  37.2 13.5 %collective-permute-start.7 = (f32[96,128]{1,0:T(8,128)S(1)}, f32[96,128]{1,0:T(8,128)S(1)}, u32[]{:S(2)}, u32[]{:S(2)}) collective-permute-start(f32[96,128]{1,0:T(8,128)S(1)} %get-tuple-element.46.s), channel_id=1, source_target_pairs={{4,8},{12,16},{20,24},{28,32},{36,40},{44,48},{52,56},{60,64},{68,... | collective-permute-start | bytes 147464 | tf_op jit(solution)/shard_map/ppermute | solution.py:576
  51.4 9.7 %collective-permute-start.8 = (f32[96,128]{1,0:T(8,128)S(1)}, f32[96,128]{1,0:T(8,128)S(1)}, u32[]{:S(2)}, u32[]{:S(2)}) collective-permute-start(f32[96,128]{1,0:T(8,128)S(1)} %get-tuple-element.54.s), channel_id=1, source_target_pairs={{0,4},{4,0},{8,12},{12,8},{16,20},{20,16},{24,28},{28,24},{32,36},... | collective-permute-start | bytes 147464 | tf_op jit(solution)/shard_map/ppermute | solution.py:577
  53.3 14.0 %collective-permute-start.9 = (f32[96,128]{1,0:T(8,128)S(1)}, f32[96,128]{1,0:T(8,128)S(1)}, u32[]{:S(2)}, u32[]{:S(2)}) collective-permute-start(f32[96,128]{1,0:T(8,128)S(1)} %get-tuple-element.54.s), channel_id=1, source_target_pairs={{4,8},{12,16},{20,24},{28,32},{36,40},{44,48},{52,56},{60,64},{68,... | collective-permute-start | bytes 147464 | tf_op jit(solution)/shard_map/ppermute | solution.py:576
